TPU v7x, 512 devices: a 8x2x16 block of a 8x8x16 slice. The times are simulated.
512 devices in a mesh: parts: 2 (over y), gz: 128 (over x, z), gy: 2 (over core).
Axes of the slice: x: 8, y: 2, z: 16, core: 2. Of those that a mesh axis runs over, the one named last changes fastest.
The devices are a block of a 8x8x16 slice.
Arguments:
- direction: float32 [3, 256, 128, 128], P(None, ('parts', 'gz'), 'gy'), parts along dimension 1, may hold values from -6 to 6
- region: int32 [256, 128, 128], P(('parts', 'gz'), 'gy'), parts along dimension 0, may hold values from 0 to 3
- saturation: float32 [3], replicated, may hold values from 0.5 to 2
- kernel_main: float32 [6, 256, 256, 128], P(None, 'gz', 'gy'), may hold values from -6 to 6
- kernel_nyq: float32 [6, 256, 256], P(None, 'gz', 'gy'), may hold values from -6 to 6
Outputs:
- field: float32 [3, 256, 128, 128], P(None, ('parts', 'gz'), 'gy'), parts along dimension 1
There are 2 independent parts, one for each index of `parts`. A program takes and returns all parts, laid end to end along the dimension named above; an argument that names none is the same for every part. Nothing has to cross between parts.
Inputs may be any that keep to these rules, and one draw needn't show every extreme that they name: `region`: 0 marks an empty cell; other ids name materials.
All inputs are finite; a program needn't handle non-finite values.
Results may differ from a plain program's by a relative error of at most 0.00007.
Values sent between devices are 32-bit elements; how exact they have to be, the bound alone decides.
No kernel may reach another device: no remote copies, remote signals or barrier semaphores. Data moves between devices by JAX's collectives and lax.ppermute only.
A program may use at most 64 MiB of HBM per device.

v0:
```python
import math

import jax
import jax.numpy as jnp
import numpy as np
from jax import lax
from jax.sharding import PartitionSpec as P

exchange_stiffness = 0.25
tensor_index = ((0, 3, 4), (3, 1, 5), (4, 5, 2))
highest = lax.Precision.HIGHEST
lane_width = 128
swap = [(0, 1), (1, 0)]


def wave(first, second, period):
    angle = 2.0 * np.pi / period * (np.outer(first, second) % period)
    return np.cos(angle), np.sin(angle)


def slot_frequencies(groups_z):
    bits = groups_z.bit_length() - 1
    reversed_bits = np.array([int(format(d, f"0{bits}b")[::-1], 2) for d in range(groups_z)])
    return np.concatenate([2 * reversed_bits, 2 * reversed_bits + 1])


def tables(columns, rows, groups_z):
    f32 = lambda a: np.ascontiguousarray(a, dtype=np.float32)
    x = np.arange(columns)
    y = np.arange(rows)
    ky = np.arange(2 * rows)
    z = np.arange(groups_z)
    out = {}
    cx, sx = wave(x, x, 2 * columns)
    out["tx"] = f32(np.concatenate([cx, -sx], axis=1))
    half = rows // 2
    per_gy, per_gy_back = [], []
    for g in range(2):
        own_ky = ky[g * rows : (g + 1) * rows]
        blocks = []
        for h in (g, 1 - g):
            c, s = wave(y[h * half : (h + 1) * half], own_ky, 2 * rows)
            blocks.append(np.block([[c, -s], [s, c]]))
        per_gy.append(np.concatenate(blocks, axis=0))
        blocks = []
        for h in (g, 1 - g):
            c, s = wave(own_ky, y[h * half : (h + 1) * half], 2 * rows)
            blocks.append(np.block([[c, s], [-s, c]]))
        per_gy_back.append(np.concatenate(blocks, axis=1))
    out["ty"] = f32(np.stack(per_gy))
    out["ty_back"] = f32(np.stack(per_gy_back))
    kz = slot_frequencies(groups_z)
    c, s = wave(kz, z, 2 * groups_z)
    out["tz"] = f32(np.concatenate([c, s], axis=1))
    out["tz_back"] = f32(np.concatenate([c.T, s.T], axis=1))
    w = np.where(x == 0, 1.0, 2.0)[:, None]
    scale = 1.0 / (2.0 * columns * 2.0 * rows * 2.0 * groups_z)
    out["tx_back"] = f32(np.concatenate([w * cx, -w * sx], axis=1) * scale)
    forward, back = [], []
    for g in range(2):
        c, s = wave(ky[g * rows : (g + 1) * rows], np.concatenate([y[g * half : (g + 1) * half], y[(1 - g) * half : (2 - g) * half]]), 2 * rows)
        forward.append(np.stack([c, -s]))
        c, s = wave(ky, y[g * half : (g + 1) * half], 2 * rows)
        c, s = c.reshape(2, rows, half), s.reshape(2, rows, half)
        back.append(np.stack([c[0], -s[0], c[1], -s[1]]) * scale)
    out["ny"] = f32(np.stack(forward))
    out["ny_back"] = f32(np.stack(back))
    return {k: jnp.asarray(v) for k, v in out.items()}


def dot(a, b):
    return jnp.dot(a, b, precision=highest)


def spread(values):
    rows = values.shape[0]
    one = jnp.pad(values, ((0, 0), (0, 1)))
    return jnp.pad(jnp.concatenate([one, one, one], axis=1), ((0, 0), (0, 20)))


def spread_kernel(kernel):
    rows = [kernel[tensor_index[i][j]] if i < 3 and j < 3 else jnp.zeros_like(kernel[0]) for i in range(4) for j in range(4)]
    return jnp.stack(rows, axis=1)


def forward_x(moment, tx):
    three, rows, columns = moment.shape
    table = tx.reshape(columns, 2, columns)
    out = jnp.einsum("krx,cyx->kcry", table, moment, precision=highest)
    return out.reshape(columns, three, 2 * rows)


def forward_yz(own, other, ty, tz):
    both = jnp.concatenate([own, other], axis=2)
    planes, three, width = both.shape
    ready = dot(both.reshape(planes * three, width), ty).reshape(planes, three, 2, -1)
    real = ready[:, :, 0].transpose(1, 0, 2)
    imag = ready[:, :, 1].transpose(1, 0, 2)
    to_real = jnp.concatenate([real, imag], axis=1)
    to_imag = jnp.concatenate([imag, -real], axis=1)
    return jnp.stack(
        [
            jnp.einsum("pq,cqk->cpk", tz, to_real, precision=highest),
            jnp.einsum("pq,cqk->cpk", tz, to_imag, precision=highest),
        ],
        axis=1,
    )


def multiply_back(spectra, kernel, extra, tz, tz_back, ty_back, y_index):
    kernel = kernel.reshape(6, -1, kernel.shape[2])
    pieces = []
    for i in range(3):
        summed = kernel[tensor_index[i][0]] * spectra[0]
        for j in (1, 2):
            summed = summed + kernel[tensor_index[i][j]] * spectra[j]
        pieces.append(summed)
    field = jnp.stack(pieces)
    to_real = jnp.concatenate([field[:, 0], -field[:, 1]], axis=1)
    to_imag = jnp.concatenate([field[:, 1], field[:, 0]], axis=1)
    real = jnp.einsum("zp,cpk->czk", tz_back, to_real, precision=highest)
    imag = jnp.einsum("zp,cpk->czk", tz_back, to_imag, precision=highest)
    lines = jnp.concatenate([real, imag], axis=2)
    both = jnp.einsum("czk,ky->zcy", lines, ty_back, precision=highest)
    real, imag = extra[:, 0:12], extra[:, 32:44]
    k_col = jnp.concatenate([extra[:, 16:28], extra[:, 80:92]], axis=0)
    z_real = dot(tz, jnp.concatenate([real, imag], axis=0)) * k_col
    z_imag = dot(tz, jnp.concatenate([imag, -real], axis=0)) * k_col
    q_real = dot(tz_back, jnp.concatenate([z_real, -z_imag], axis=0))
    q_imag = dot(tz_back, jnp.concatenate([z_imag, z_real], axis=0))
    row = jnp.concatenate([jnp.pad(q_real, ((0, 0), (0, 20))), jnp.pad(q_imag, ((0, 0), (0, 20)))], axis=1)
    zero = jnp.zeros_like(row)
    row = jnp.concatenate([jnp.where(y_index == 0, row, zero), jnp.where(y_index == 1, row, zero)], axis=1)
    half = both.shape[2] // 2
    return (
        jnp.concatenate([both[:, :, :half], row[:, None]], axis=1),
        jnp.concatenate([both[:, :, half:], row[:, None]], axis=1),
    )


def back_x(received, tx_back, ny_back, signs):
    columns = received.shape[0]
    half = received.shape[2] // 2
    main = received[:, :3].reshape(columns, 3, 2, half)
    table = tx_back.reshape(columns, 2, columns)
    demag = jnp.einsum("kcry,krx->cyx", main, table, precision=highest)
    extra = received[:, 3].reshape(columns, 4, 32)[:, :, :12].reshape(columns, 4, 3, 4)[..., :3].sum(axis=3)
    nyquist = jnp.einsum("gqi,qgy->iy", extra, ny_back, precision=highest)
    return demag + nyquist[:, :, None] * signs


def local(direction, region, saturation, kernel_main, kernel_nyq):
    columns = direction.shape[3]
    half = direction.shape[2]
    groups_z = lax.axis_size("gz")
    rows = half * lax.axis_size("gy")
    y_index = lax.axis_index("gy")
    t = tables(columns, rows, groups_z)
    direction = direction[:, 0]
    region = region[0]
    magnetic = (region > 0).astype(jnp.float32)
    strength = jnp.zeros(region.shape, jnp.float32)
    for r in range(saturation.shape[0]):
        strength = strength + jnp.where(region == r + 1, saturation[r], 0.0)
    moment = direction * strength[None]
    signs = (1.0 - 2.0 * (jnp.arange(columns) % 2)).astype(jnp.float32)
    stacked = jnp.concatenate([direction * magnetic[None], magnetic[None]], axis=0)
    parts = lax.axis_size("parts")
    part = lax.axis_index("parts")
    share = -(-12 // parts)
    nyq_own = jnp.sum(moment * signs, axis=2)
    edge = jnp.where(y_index == 0, stacked[:, -1], stacked[:, 0])
    small = jnp.concatenate([edge, jnp.pad(nyq_own, ((0, 1), (0, columns - half)))], axis=0)
    small = lax.ppermute(small, "gy", swap)
    edge, nyq_other = small[:4], small[4:7, :half]
    line = jnp.concatenate([nyq_own, nyq_other], axis=1)
    nyq = jnp.einsum("rgy,cy->rgc", t["ny"][y_index], line, precision=highest)
    k_row = [spread_kernel(kernel_nyq[:, s]) for s in range(2)]
    zero = jnp.zeros_like(k_row[0])
    real, imag = spread(nyq[0]), spread(nyq[1])
    row = jnp.concatenate(
        [real[:, :16], k_row[0], imag[:, :16], zero, zero, k_row[1], zero, zero], axis=1
    )
    mine = jnp.minimum(part * share, 12 - share)
    main = lax.dynamic_slice_in_dim(kernel_main.reshape(12, rows, columns), mine, share, 0)
    send = jnp.concatenate([forward_x(moment, t["tx"]), row[:, None], main.transpose(2, 0, 1)], axis=1)
    width = send.shape[1]
    recv = lax.all_to_all(send.reshape(columns, width // 2, 2, columns), "gz", 0, 0, tiled=True)
    recv = recv.reshape(columns, width, columns)
    recv_m, recv_n, recv_k = recv[:, :3], recv[:, 3], recv[:, 4:]
    other_m = lax.ppermute(recv_m, "gy", swap)
    shares = [recv_k]
    for k in range(1, parts):
        shares.append(lax.ppermute(recv_k, "parts", [(p, (p + k) % parts) for p in range(parts)]))
    ordered = []
    for c in range(12):
        owner = c // share
        at = c - min(owner * share, 12 - share)
        piece = shares[0][:, at]
        for k in range(1, parts):
            piece = jnp.where((part - owner) % parts == k, shares[k][:, at], piece)
        ordered.append(piece)
    kernel = jnp.stack(ordered)
    up = [(i, i + 1) for i in range(groups_z - 1)]
    down = [(b, a) for a, b in up]
    before = lax.ppermute(stacked, "gz", up)
    after = lax.ppermute(stacked, "gz", down)
    spectra = forward_yz(recv_m, other_m, t["ty"][y_index], t["tz"])
    own, other = multiply_back(spectra, kernel, recv_n, t["tz"], t["tz_back"], t["ty_back"][y_index], y_index)
    send_f = own + lax.ppermute(other, "gy", swap)
    recv_f = lax.all_to_all(send_f, "gz", 0, 0, tiled=True)
    demag = back_x(recv_f, t["tx_back"], t["ny_back"][y_index], signs)
    low = jnp.where(y_index == 0, 0.0, edge)[:, None]
    high = jnp.where(y_index == 0, edge, 0.0)[:, None]
    tall = jnp.concatenate([low, stacked, high], axis=1)
    wide = jnp.pad(stacked, ((0, 0), (0, 0), (1, 1)))
    near = before + after + tall[:, :-2] + tall[:, 2:] + wide[..., :-2] + wide[..., 2:]
    exchange = exchange_stiffness * magnetic[None] * (near[:3] - near[3:4] * direction)
    return (demag + exchange)[:, None]


def solution(mesh):
    placed = (
        P(None, ("parts", "gz"), "gy", None),
        P(("parts", "gz"), "gy", None),
        P(),
        P(None, "gz", "gy", None),
        P(None, "gz", "gy"),
    )
    return jax.shard_map(
        local,
        mesh=mesh,
        in_specs=placed,
        out_specs=P(None, ("parts", "gz"), "gy", None),
        check_vma=False,
    )
```

profile of v0, /device:TPU:66, one launch (start us, length us, event | category | flops | bytes accessed | tf_op | source)
XLA Modules:
  0.0 168.8 jit_solution(18126243656628088357)
XLA Ops:
  0.0 0.6 copy-done.14
  0.7 0.7 fusion.85
  1.3 2.8 %select_bitcast_fusion.12 = (f32[64,128]{1,0:T(8,128)S(1)}, pred[1,64,128]{2,1,0:T(8,128)(4,1)S(1)}, f32[64,128]{1,0:T(8,128)S(1)}) fusion(s32[1,64,128]{2,1,0:T(8,128)} %param.14, f32[]{:T(128)} %bitcast.4, f32[]{:T(128)} %bitcast.3, f32[]{:T(128)} %bitcast.2), kind=kLoop, calls=%fused_computation.122 | loop fusion | flops 81920 | bytes 106508 | tf_op jit(solution)/shard_map/mul | solution.py:218
  4.2 0.2 fusion.38
  4.4 2.1 %collective-permute-start = (f32[8,128]{1,0:T(8,128)S(1)}, f32[8,128]{1,0:T(8,128)S(1)}, u32[]{:S(2)}, u32[]{:S(2)}) collective-permute-start(f32[8,128]{1,0:T(8,128)S(1)} %select_maximum_fusion.1), channel_id=1, source_target_pairs={{0,1},{1,0},{2,3},{3,2},{4,5},{5,4},{6,7},{7,6},{8,9},{9,8},{10,11... | collective-permute-start | bytes 12296 | tf_op jit(solution)/shard_map/ppermute | solution.py:174
  6.5 1.4 copy.195
  8.0 0.7 copy-done.13
  8.7 0.3 fusion.43
  10.5 0.6 copy-done.12
  11.1 0.2 fusion.39
  11.7 0.6 concatenate.84
  12.3 0.5 copy.197
  12.8 89.7 %all_to_all.10 = f32[128,5,2,128]{3,2,1,0:T(2,128)S(1)} all-to-all(f32[128,5,2,128]{3,2,1,0:T(2,128)S(1)} %copy.197), channel_id=1, replica_groups=mesh['parts'=2,'gz'=128,'gy'=2] {'gz'}, dimensions={0} | all-to-all | bytes 1310720 | tf_op jit(solution)/shard_map/all_to_all | solution.py:188
  102.6 2.1 %collective-permute-start.2 = (f32[128,3,128]{2,0,1:T(8,128)S(1)}, f32[128,3,128]{2,0,1:T(8,128)S(1)}, u32[]{:S(2)}, u32[]{:S(2)}) collective-permute-start(f32[128,3,128]{2,0,1:T(8,128)S(1)} %slice.344), channel_id=1, source_target_pairs={{0,1},{1,0},{2,3},{3,2},{4,5},{5,4},{6,7},{7,6},{8,9},{9,8},{10,11... | collective-permute-start | bytes 589832 | tf_op jit(solution)/shard_map/ppermute | solution.py:191
  104.8 4.9 %collective-permute-start.1 = (f32[128,6,128]{2,0,1:T(8,128)S(1)}, f32[128,6,128]{2,0,1:T(8,128)S(1)}, u32[]{:S(2)}, u32[]{:S(2)}) collective-permute-start(f32[128,6,128]{2,0,1:T(8,128)S(1)} %slice.339), channel_id=1, source_target_pairs={{0,256},{256,0},{1,257},{257,1},{2,258},{258,2},{3,259},{259,3},{4... | collective-permute-start | bytes 1179656 | tf_op jit(solution)/shard_map/ppermute | solution.py:194
  109.7 0.5 fusion.12
  110.3 0.9 copy-done.1
  111.2 0.8 convolution_bitcast_fusion.1
  112.0 0.8 convolution_bitcast_fusion.2
  112.8 6.4 %collective-permute-done.1 = f32[128,6,128]{2,0,1:T(8,128)S(1)} collective-permute-done((f32[128,6,128]{2,0,1:T(8,128)S(1)}, f32[128,6,128]{2,0,1:T(8,128)S(1)}, u32[]{:S(2)}, u32[]{:S(2)}) %collective-permute-start.1) | collective-permute-done | bytes 393248 | tf_op jit(solution)/shard_map/ppermute | solution.py:194
  119.4 0.8 copy-done.6
  120.2 0.3 fusion.47
  120.5 0.2 fusion.51
  122.1 0.8 copy-done.5
  122.8 0.2 fusion.1
  123.1 0.3 fusion.3
  123.4 0.6 copy-done.4
  124.2 0.2 fusion.86
  124.4 0.5 copy-done.3
  125.1 0.2 fusion.5
  125.4 0.8 convolution_bitcast_fusion.3
  126.2 0.8 convolution_bitcast_fusion.4
  127.0 0.2 copy-done.10
  127.2 0.6 convolution_bitcast_fusion
  127.9 2.0 %collective-permute-start.3 = (f32[128,4,128]{0,2,1:T(8,128)S(1)}, f32[128,4,128]{0,2,1:T(8,128)S(1)}, u32[]{:S(2)}, u32[]{:S(2)}) collective-permute-start(f32[128,4,128]{0,2,1:T(8,128)S(1)} %pad_maximum_fusion.2), channel_id=1, source_target_pairs={{0,1},{1,0},{2,3},{3,2},{4,5},{5,4},{6,7},{7,6},{8,9},{9,8},{10,11... | collective-permute-start | bytes 786440 | tf_op jit(solution)/shard_map/ppermute | solution.py:210
  129.8 1.5 collective-permute-done.3
  131.4 0.8 copy.211
  132.2 11.0 %all-to-all-start.1 = ((f32[128,4,128]{2,1,0:T(4,128)}), f32[128,4,128]{2,1,0:T(4,128)S(1)}, u32[]{:S(2)}, u32[]{:S(2)}) async-start(f32[128,4,128]{2,1,0:T(4,128)} %copy.211), calls=%async_computation.1 | async-start | bytes 524288 | tf_op jit(solution)/shard_map/all_to_all | solution.py:211
  143.3 3.4 %collective-permute-start.4 = (f32[4,64,128]{2,0,1:T(4,128)S(1)}, f32[4,64,128]{2,0,1:T(4,128)S(1)}, u32[]{:S(2)}, u32[]{:S(2)}) collective-permute-start(f32[4,64,128]{2,0,1:T(4,128)S(1)} %pad_maximum_fusion.5), channel_id=1, source_target_pairs={{0,2},{2,4},{4,6},{6,8},{8,10},{10,12},{12,14},{14,16},{16,18},{18... | collective-permute-start | bytes 393224 | tf_op jit(solution)/shard_map/ppermute | solution.py:206
  146.7 4.6 %collective-permute-start.5 = (f32[4,64,128]{2,0,1:T(4,128)S(1)}, f32[4,64,128]{2,0,1:T(4,128)S(1)}, u32[]{:S(2)}, u32[]{:S(2)}) collective-permute-start(f32[4,64,128]{2,0,1:T(4,128)S(1)} %pad_maximum_fusion.5), channel_id=1, source_target_pairs={{2,0},{4,2},{6,4},{8,6},{10,8},{12,10},{14,12},{16,14},{18,16},{20... | collective-permute-start | bytes 393224 | tf_op jit(solution)/shard_map/ppermute | solution.py:207
  151.3 6.8 %collective-permute-done.4 = f32[4,64,128]{2,0,1:T(4,128)S(1)} collective-permute-done((f32[4,64,128]{2,0,1:T(4,128)S(1)}, f32[4,64,128]{2,0,1:T(4,128)S(1)}, u32[]{:S(2)}, u32[]{:S(2)}) %collective-permute-start.4) | collective-permute-done | bytes 131104 | tf_op jit(solution)/shard_map/ppermute | solution.py:206
  158.1 0.2 fusion.30
  158.3 8.0 %all-to-all-done.1 = f32[128,4,128]{2,1,0:T(4,128)S(1)} async-done(((f32[128,4,128]{2,1,0:T(4,128)}), f32[128,4,128]{2,1,0:T(4,128)S(1)}, u32[]{:S(2)}, u32[]{:S(2)}) %all-to-all-start.1) | async-done | bytes 262176 | tf_op jit(solution)/shard_map/all_to_all | solution.py:211
  166.7 0.7 copy-done.9
  167.4 0.3 convolution_bitcast_fusion.5
  167.7 0.2 convolution_bitcast_fusion.6
  168.0 0.2 fusion.33
  168.2 0.6 copy.218
  (96 shorter events, 4.4 us)
Async XLA Ops:
  0.0 0.7 copy-start.14
  1.3 2.8 %copy-start.2 = (f32[3,1,64,128]{3,2,1,0:T(8,128)S(1)}, f32[3,1,64,128]{3,2,1,0:T(8,128)}, u32[]{:S(2)}) copy-start(f32[3,1,64,128]{3,2,1,0:T(8,128)} %param.13) | copy-start | bytes 294916
  4.4 4.2 %copy-start.7 = (f32[128,2,128,1]{2,0,1,3:T(8,128)S(1)}, f32[128,2,128,1]{2,0,1,3:T(8,128)}, u32[]{:S(2)}) copy-start(f32[128,2,128,1]{2,0,1,3:T(8,128)} %constant.131) | copy-start | bytes 393220
  4.4 6.1 %collective-permute-start = (f32[8,128]{1,0:T(8,128)S(1)}, f32[8,128]{1,0:T(8,128)S(1)}, u32[]{:S(2)}, u32[]{:S(2)}) collective-permute-start(f32[8,128]{1,0:T(8,128)S(1)} %select_maximum_fusion.1), channel_id=1, source_target_pairs={{0,1},{1,0},{2,3},{3,2},{4,5},{5,4},{6,7},{7,6},{8,9},{9,8},{10,11... | collective-permute-start | bytes 12296 | tf_op jit(solution)/shard_map/ppermute | solution.py:174
  7.9 0.7 copy-start.13
  10.2 1.0 copy-start.12
  102.5 2.2 %copy-start.8 = (f32[2,256,256]{1,2,0:T(8,128)S(1)}, f32[2,256,256]{1,2,0:T(8,128)}, u32[]{:S(2)}) copy-start(f32[2,256,256]{1,2,0:T(8,128)} %constant.98.clone) | copy-start | bytes 1572868
  102.6 7.1 %collective-permute-start.2 = (f32[128,3,128]{2,0,1:T(8,128)S(1)}, f32[128,3,128]{2,0,1:T(8,128)S(1)}, u32[]{:S(2)}, u32[]{:S(2)}) collective-permute-start(f32[128,3,128]{2,0,1:T(8,128)S(1)} %slice.344), channel_id=1, source_target_pairs={{0,1},{1,0},{2,3},{3,2},{4,5},{5,4},{6,7},{7,6},{8,9},{9,8},{10,11... | collective-permute-start | bytes 589832 | tf_op jit(solution)/shard_map/ppermute | solution.py:191
  104.8 14.5 %collective-permute-start.1 = (f32[128,6,128]{2,0,1:T(8,128)S(1)}, f32[128,6,128]{2,0,1:T(8,128)S(1)}, u32[]{:S(2)}, u32[]{:S(2)}) collective-permute-start(f32[128,6,128]{2,0,1:T(8,128)S(1)} %slice.339), channel_id=1, source_target_pairs={{0,256},{256,0},{1,257},{257,1},{2,258},{258,2},{3,259},{259,3},{4... | collective-permute-start | bytes 1179656 | tf_op jit(solution)/shard_map/ppermute | solution.py:194
  110.3 1.0 copy-start.1
  119.3 0.9 copy-start.6
  121.9 0.9 copy-start.5
  123.1 0.9 copy-start.4
  124.0 0.9 copy-start.3
  124.2 1.1 copy-start
  126.2 1.0 copy-start.10
  127.9 3.5 %collective-permute-start.3 = (f32[128,4,128]{0,2,1:T(8,128)S(1)}, f32[128,4,128]{0,2,1:T(8,128)S(1)}, u32[]{:S(2)}, u32[]{:S(2)}) collective-permute-start(f32[128,4,128]{0,2,1:T(8,128)S(1)} %pad_maximum_fusion.2), channel_id=1, source_target_pairs={{0,1},{1,0},{2,3},{3,2},{4,5},{5,4},{6,7},{7,6},{8,9},{9,8},{10,11... | collective-permute-start | bytes 786440 | tf_op jit(solution)/shard_map/ppermute | solution.py:210
  132.2 34.1 %all-to-all-start.1 = ((f32[128,4,128]{2,1,0:T(4,128)}), f32[128,4,128]{2,1,0:T(4,128)S(1)}, u32[]{:S(2)}, u32[]{:S(2)}) async-start(f32[128,4,128]{2,1,0:T(4,128)} %copy.211), calls=%async_computation.1 | async-start | bytes 524288 | tf_op jit(solution)/shard_map/all_to_all | solution.py:211
  143.3 14.8 %collective-permute-start.4 = (f32[4,64,128]{2,0,1:T(4,128)S(1)}, f32[4,64,128]{2,0,1:T(4,128)S(1)}, u32[]{:S(2)}, u32[]{:S(2)}) collective-permute-start(f32[4,64,128]{2,0,1:T(4,128)S(1)} %pad_maximum_fusion.5), channel_id=1, source_target_pairs={{0,2},{2,4},{4,6},{6,8},{8,10},{10,12},{12,14},{14,16},{16,18},{18... | collective-permute-start | bytes 393224 | tf_op jit(solution)/shard_map/ppermute | solution.py:206
  146.7 11.4 %collective-permute-start.5 = (f32[4,64,128]{2,0,1:T(4,128)S(1)}, f32[4,64,128]{2,0,1:T(4,128)S(1)}, u32[]{:S(2)}, u32[]{:S(2)}) collective-permute-start(f32[4,64,128]{2,0,1:T(4,128)S(1)} %pad_maximum_fusion.5), channel_id=1, source_target_pairs={{2,0},{4,2},{6,4},{8,6},{10,8},{12,10},{14,12},{16,14},{18,16},{20... | collective-permute-start | bytes 393224 | tf_op jit(solution)/shard_map/ppermute | solution.py:207
  166.5 0.9 copy-start.9
  166.6 1.1 copy-start.11
where the time goes:
time: 170 us; the launch traced here: 169 us
  blocking collectives  89.7 us (53%)
  starting transfers between devices  30 us (18%)
  waiting for transfers between devices  22.7 us (13%)
  local copies, waits for them, and re-layouts  14.4 us (8%)
  matrix products  7.22 us (4%)
  other arithmetic  4.09 us (2%)
    all_to_all x1, blocking collectives, local(): lax.all_to_all(send.reshape(columns, width // 2, 2, columns), 'gz', 0, 0,...  89.7 us
    all_to_all x1, starting transfers between devices, local(): recv_f = lax.all_to_all(send_f, 'gz', 0, 0, tiled=True)  11 us
    unnamed x32, local copies, waits for them, and re-layouts  8.02 us
    all_to_all x1, waiting for transfers between devices, local(): recv_f = lax.all_to_all(send_f, 'gz', 0, 0, tiled=True)  7.95 us
    ppermute x1, waiting for transfers between devices, local(): before = lax.ppermute(stacked, 'gz', up)  6.76 us
    ppermute x1, waiting for transfers between devices, local(): lax.ppermute(recv_k, 'parts', [(p, (p + k) % parts) for p in range(parts)])  6.43 us
    ppermute x1, starting transfers between devices, local(): lax.ppermute(recv_k, 'parts', [(p, (p + k) % parts) for p in range(parts)])  4.92 us
    ppermute x1, starting transfers between devices, local(): after = lax.ppermute(stacked, 'gz', down)  4.61 us
  transfers between devices with their start and end apart: 7, of which 4 were waited for; matrix products, arithmetic and copies ran while one was open for 3% of the time, Pallas kernels for 0%

commit v1 on v0

v1 whole, which is shorter than its diff:
```python
import math

import jax
import jax.numpy as jnp
import numpy as np
from jax import lax
from jax.experimental import pallas as pl
from jax.experimental.pallas import tpu as pltpu
from jax.sharding import PartitionSpec as P

exchange_stiffness = 0.25
tensor_index = ((0, 3, 4), (3, 1, 5), (4, 5, 2))
highest = lax.Precision.HIGHEST
components = 12
swap = [(0, 1), (1, 0)]
bf16 = jnp.bfloat16
f32 = jnp.float32
limits = pltpu.CompilerParams(vmem_limit_bytes=20 * 2**20)


def wave(first, second, period):
    angle = 2.0 * np.pi / period * (np.outer(first, second) % period)
    return np.cos(angle), np.sin(angle)


def slot_frequencies(groups_z):
    bits = groups_z.bit_length() - 1
    reversed_bits = np.array([int(format(d, f"0{bits}b")[::-1], 2) for d in range(groups_z)])
    return np.concatenate([2 * reversed_bits, 2 * reversed_bits + 1])


def tables(columns, rows, groups_z):
    half = rows // 2
    x = np.arange(columns)
    y = np.arange(rows)
    ky = np.arange(2 * rows)
    z = np.arange(groups_z)
    out = {}
    cx, sx = wave(x, x, 2 * columns)
    out["tx"] = np.concatenate([cx, -sx], axis=1)
    forward, back = [], []
    for g in range(2):
        own_ky = ky[g * rows : (g + 1) * rows]
        there, here = [], []
        for h in (g, 1 - g):
            c, s = wave(y[h * half : (h + 1) * half], own_ky, 2 * rows)
            there.append(np.block([[c, -s], [s, c]]))
            here.append(np.block([[c.T, s.T], [-s.T, c.T]]))
        forward.append(np.concatenate(there, axis=0))
        back.append(np.concatenate(here, axis=1))
    out["ty"] = np.stack(forward)
    out["ty_back"] = np.stack(back)
    c, s = wave(slot_frequencies(groups_z), z, 2 * groups_z)
    out["tz"] = np.concatenate([c, s], axis=1)
    out["tz_back"] = np.concatenate([c.T, s.T], axis=1)
    w = np.where(x == 0, 1.0, 2.0)[:, None]
    scale = 1.0 / (2.0 * columns * 2.0 * rows * 2.0 * groups_z)
    out["tx_back"] = np.concatenate([w * cx, -w * sx], axis=1) * scale
    forward, back = [], []
    for g in range(2):
        c, s = wave(ky, y[g * half : (g + 1) * half], 2 * rows)
        c, s = c.reshape(2, rows, half), s.reshape(2, rows, half)
        forward.append(np.concatenate([c[0], -s[0], c[1], -s[1]], axis=1))
        back.append(np.stack([c[0], -s[0], c[1], -s[1]]) * scale)
    out["ny"] = np.stack(forward)
    out["ny_back"] = np.stack(back)
    return out


def halves(table):
    table = np.asarray(table, dtype=np.float32)
    high = table.astype(bf16)
    low = (table - high.astype(np.float32)).astype(bf16)
    return jnp.asarray(np.stack([high, low]))


def split(x):
    high = x.astype(bf16)
    return high, (x - high.astype(f32)).astype(bf16)


def three(left, right, dims=((1,), (0,))):
    (lh, ll), (rh, rl) = left, right
    prod = lambda a, b: lax.dot_general(a, b, (dims, ((), ())), preferred_element_type=f32)
    return prod(lh, rh) + (prod(lh, rl) + prod(ll, rh))


def cross(real, imag, lower):
    return jnp.concatenate([jnp.concatenate([real, imag], axis=1), lower], axis=0)


def prepare_kernel(share, mine_ref, sat_ref, dir_hbm, reg_hbm, main_hbm, nyq_hbm, tx_hbm, ny_hbm,
                   send_ref, stack_ref, dirs, reg, main, nyq, tx, ny, rows_t, sems):
    three_c, half, columns = dirs.shape
    width = 4 + share
    copies = [
        pltpu.make_async_copy(reg_hbm, reg, sems.at[0]),
        pltpu.make_async_copy(dir_hbm, dirs, sems.at[1]),
        pltpu.make_async_copy(main_hbm.at[pl.ds(mine_ref[0], share)], main, sems.at[2]),
        pltpu.make_async_copy(tx_hbm, tx, sems.at[3]),
        pltpu.make_async_copy(ny_hbm.at[mine_ref[1]], ny, sems.at[4]),
        pltpu.make_async_copy(nyq_hbm, nyq, sems.at[5]),
    ]
    for c in copies:
        c.start()
    rows_t[...] = jnp.zeros_like(rows_t)
    copies[0].wait()
    region = reg[...]
    magnetic = (region > 0).astype(f32)
    strength = jnp.zeros(region.shape, f32)
    for r in range(3):
        strength = strength + jnp.where(region == r + 1, sat_ref[r], 0.0)
    copies[1].wait()
    stack_ref[3] = magnetic
    lane = lax.broadcasted_iota(jnp.int32, (half, columns), 1)
    signs = (1 - 2 * (lane % 2)).astype(f32)
    moments = []
    sums = jnp.zeros((half, columns), f32)
    for c in range(3):
        one = dirs[c]
        stack_ref[c] = one * magnetic
        moment = one * strength
        moments.append(moment)
        total = jnp.sum(moment * signs, axis=1, keepdims=True)
        sums = jnp.where((lane % 4 == c) & (lane % 32 < 12), total, sums)
    copies[3].wait()
    zero = jnp.zeros((half, columns), bf16)
    table = (tx[0], tx[1])
    for c in range(3):
        high, low = split(moments[c])
        wide = [jnp.concatenate([jnp.concatenate([p, zero], 1), jnp.concatenate([zero, p], 1)], 0) for p in (high, low)]
        send_ref[pl.ds(c, columns, stride=width), :] = three(table, wide, ((1,), (1,)))
    copies[2].wait()
    for r in range(share):
        send_ref[pl.ds(4 + r, columns, stride=width), :] = main[r].T
    copies[4].wait()
    parts = [split(jnp.where(lane // 32 == q, sums, 0.0)) for q in range(4)]
    stacked = [jnp.concatenate([p[k] for p in parts], axis=0) for k in range(2)]
    row = three((ny[0], ny[1]), stacked)
    copies[5].wait()
    for s in range(2):
        for i in range(3):
            for j in range(3):
                rows_t[pl.ds(64 * s + 16 + 4 * i + j, 1), :] = nyq[tensor_index[i][j], pl.ds(s, 1), :]
    send_ref[pl.ds(3, columns, stride=width), :] = row + rows_t[...].T


def prepare(mine, saturation, direction, region, kernel_main, kernel_nyq, tx, ny, share):
    _, half, columns = direction.shape
    rows = kernel_main.shape[1]
    any_spec = pl.BlockSpec(memory_space=pltpu.HBM)
    smem = pl.BlockSpec(memory_space=pltpu.SMEM)
    vmem = pl.BlockSpec(memory_space=pltpu.VMEM)

    def body(*refs):
        prepare_kernel(share, *refs)

    return pl.pallas_call(
        body,
        name="prepare",
        compiler_params=limits,
        out_shape=(
            jax.ShapeDtypeStruct((columns * (4 + share), columns), f32),
            jax.ShapeDtypeStruct((4, half, columns), f32),
        ),
        in_specs=[smem, smem] + [any_spec] * 6,
        out_specs=(vmem, vmem),
        scratch_shapes=[
            pltpu.VMEM((3, half, columns), f32),
            pltpu.VMEM((half, columns), jnp.int32),
            pltpu.VMEM((share, rows, columns), f32),
            pltpu.VMEM(kernel_nyq.shape, f32),
            pltpu.VMEM(tx.shape, bf16),
            pltpu.VMEM(ny.shape[1:], bf16),
            pltpu.VMEM((columns, columns), f32),
            pltpu.SemaphoreType.DMA((6,)),
        ],
    )(mine, saturation, direction, region, kernel_main, kernel_nyq, tx, ny)


def forward_kernel(where_ref, own, other, ty, tz, out):
    planes, width = own.shape[1:]
    table = (tz[0], tz[1])
    y_table = (ty[0], ty[1])
    for c in range(4):
        if c < 3:
            ready = three(split(jnp.concatenate([own[c], other[c]], axis=1)), y_table)
            real, imag = ready[:, :width], ready[:, width:]
        else:
            lane = lax.broadcasted_iota(jnp.int32, (planes, width), 1)
            summed = own[3] + other[3]
            summed = jnp.where(where_ref[1] == 0, summed, pltpu.roll(summed, 64, 1))
            real = jnp.where(lane < 12, summed, 0.0)
            imag = jnp.where(lane < 12, pltpu.roll(summed, width - 32, 1), 0.0)
        (rh, rl), (ih, il) = split(real), split(imag)
        crossed = [cross(r, i, jnp.concatenate([i, -r], axis=1)) for r, i in ((rh, ih), (rl, il))]
        out[c] = three(table, crossed)


def forward(where, own, other, ty, tz):
    planes, width = own.shape[1:]
    smem = pl.BlockSpec(memory_space=pltpu.SMEM)
    vmem = pl.BlockSpec(memory_space=pltpu.VMEM)
    return pl.pallas_call(
        forward_kernel,
        name="forward",
        compiler_params=limits,
        out_shape=jax.ShapeDtypeStruct((4, 2 * planes, 2 * width), f32),
        in_specs=[smem] + [vmem] * 4,
        out_specs=vmem,
    )(where, own, other, ty, tz)


def inverse_kernel(parts, share, where_ref, *refs):
    spectra, row_ref, ty, tz, *shares, own, other = refs
    planes, width = row_ref.shape
    part = where_ref[2]
    table = (tz[0], tz[1])
    y_table = (ty[0], ty[1])

    def kernel_row(c):
        owner = c // share
        at = c - min(owner * share, components - share)
        piece = shares[0][at]
        for k in range(1, parts):
            gone = part - owner
            gone = jnp.where(gone < 0, gone + parts, gone)
            piece = jnp.where(gone == k, shares[k][at], piece)
        return piece

    def back(real, imag):
        (rh, rl), (ih, il) = split(real), split(imag)
        crossed = [cross(r, i, jnp.concatenate([-i, r], axis=1)) for r, i in ((rh, ih), (rl, il))]
        return three(table, crossed)

    kernel = [jnp.concatenate([kernel_row(2 * t), kernel_row(2 * t + 1)], axis=0) for t in range(6)]
    for i in range(3):
        real = imag = None
        for j in range(3):
            k = kernel[tensor_index[i][j]]
            a, b = k * spectra[j, :, :width], k * spectra[j, :, width:]
            real, imag = (a, b) if real is None else (real + a, imag + b)
        lines = three(split(back(real, imag)), y_table)
        own[pl.ds(i, planes, stride=4), :] = lines[:, :width]
        other[pl.ds(i, planes, stride=4), :] = lines[:, width:]
    lane = lax.broadcasted_iota(jnp.int32, (planes, width), 1)
    row = row_ref[...]
    k = jnp.concatenate([pltpu.roll(row, width - 16, 1), pltpu.roll(row, width - 80, 1)], axis=0)
    k = jnp.where(jnp.concatenate([lane, lane], axis=0) < 12, k, 0.0)
    line = back(spectra[3, :, :width] * k, spectra[3, :, width:] * k)
    line = line[:, :width] + pltpu.roll(line[:, width:], 32, 1)
    line = jnp.where(where_ref[1] == 0, line, pltpu.roll(line, 64, 1))
    own[pl.ds(3, planes, stride=4), :] = line
    other[pl.ds(3, planes, stride=4), :] = line


def inverse(where, spectra, row, ty, tz, shares, share):
    planes, width = row.shape
    smem = pl.BlockSpec(memory_space=pltpu.SMEM)
    vmem = pl.BlockSpec(memory_space=pltpu.VMEM)
    parts = len(shares)

    def body(*refs):
        inverse_kernel(parts, share, *refs)

    half = jax.ShapeDtypeStruct((4 * planes, width), f32)
    return pl.pallas_call(
        body,
        name="inverse",
        compiler_params=limits,
        out_shape=(half, half),
        in_specs=[smem] + [vmem] * (4 + parts),
        out_specs=(vmem, vmem),
    )(where, spectra, row, ty, tz, *shares)


def back_x(received, tx_back, ny_back, signs):
    columns = received.shape[0]
    half = received.shape[2] // 2
    main = received[:, :3].reshape(columns, 3, 2, half)
    table = tx_back.reshape(columns, 2, columns)
    demag = jnp.einsum("kcry,krx->cyx", main, table, precision=highest)
    extra = received[:, 3].reshape(columns, 4, 32)[:, :, :12].reshape(columns, 4, 3, 4)[..., :3].sum(axis=3)
    nyquist = jnp.einsum("gqi,qgy->iy", extra, ny_back, precision=highest)
    return demag + nyquist[:, :, None] * signs


def local(direction, region, saturation, kernel_main, kernel_nyq):
    columns = direction.shape[3]
    half = direction.shape[2]
    groups_z = lax.axis_size("gz")
    rows = half * lax.axis_size("gy")
    parts = lax.axis_size("parts")
    y_index = lax.axis_index("gy")
    part = lax.axis_index("parts")
    share = -(-components // parts)
    t = tables(columns, rows, groups_z)
    direction = direction[:, 0]
    where = jnp.stack([jnp.minimum(part * share, components - share), y_index, part])
    send, stacked = prepare(
        where, saturation, direction, region[0], kernel_main.reshape(components, rows, columns), kernel_nyq,
        halves(t["tx"]), halves(t["ny"]).swapaxes(0, 1), share,
    )
    width = 4 + share
    recv = lax.all_to_all(send.reshape(columns, width // 2, 2, columns), "gz", 0, 0, tiled=True)
    recv = recv.reshape(columns, width, columns).transpose(1, 0, 2)
    shares = [recv[4:]]
    for k in range(1, parts):
        shares.append(lax.ppermute(shares[0], "parts", [(p, (p + k) % parts) for p in range(parts)]))
    own_m = recv[:4]
    other_m = lax.ppermute(own_m, "gy", swap)
    up = [(i, i + 1) for i in range(groups_z - 1)]
    down = [(b, a) for a, b in up]
    stacked, other_m = lax.optimization_barrier((stacked, other_m))
    before = lax.ppermute(stacked, "gz", up)
    after = lax.ppermute(stacked, "gz", down)
    edge = jnp.where(y_index == 0, stacked[:, -1], stacked[:, 0])
    edge = lax.ppermute(edge, "gy", swap)
    ty = halves(t["ty"])[:, y_index]
    ty_back = halves(t["ty_back"])[:, y_index]
    spectra = forward(where, own_m, other_m, ty, halves(t["tz"]))
    own, other = inverse(where, spectra, own_m[3], ty_back, halves(t["tz_back"]), shares, share)
    own, other = (a.reshape(groups_z, 4, columns) for a in (own, other))
    other, before, after, edge = lax.optimization_barrier((other, before, after, edge))
    send_f = own + lax.ppermute(other, "gy", swap)
    recv_f = lax.all_to_all(send_f, "gz", 0, 0, tiled=True)
    magnetic = stacked[3:4]
    low = jnp.where(y_index == 0, 0.0, edge)[:, None]
    high = jnp.where(y_index == 0, edge, 0.0)[:, None]
    tall = jnp.concatenate([low, stacked, high], axis=1)
    wide = jnp.pad(stacked, ((0, 0), (0, 0), (1, 1)))
    near = before + after + tall[:, :-2] + tall[:, 2:] + wide[..., :-2] + wide[..., 2:]
    exchange = exchange_stiffness * magnetic * (near[:3] - near[3:4] * direction)
    signs = (1.0 - 2.0 * (jnp.arange(columns) % 2)).astype(f32)
    demag = back_x(recv_f, jnp.asarray(t["tx_back"], f32), jnp.asarray(t["ny_back"], f32)[y_index], signs)
    return (demag + exchange)[:, None]


def solution(mesh):
    placed = (
        P(None, ("parts", "gz"), "gy", None),
        P(("parts", "gz"), "gy", None),
        P(),
        P(None, "gz", "gy", None),
        P(None, "gz", "gy"),
    )
    return jax.shard_map(
        local,
        mesh=mesh,
        in_specs=placed,
        out_specs=P(None, ("parts", "gz"), "gy", None),
        check_vma=False,
    )
```

time: 170 us -> 159 us (0.935)
  local copies, waits for them, and re-layouts: 14.4 us -> 6.62 us
  Pallas kernels: 0 us -> 6.2 us
  matrix products: 7.22 us -> 1.15 us
  other arithmetic: 4.09 us -> 1.01 us
    all_to_all x1, waiting for transfers between devices: 7.95 us -> 23 us  [local(): recv_f = lax.all_to_all(send_f, 'gz', 0, 0, tiled=True)]
    ppermute x1, waiting for transfers between devices: 6.76 us -> 0.01 us  [local(): before = lax.ppermute(stacked, 'gz', up)]
    dot_general x16 -> x0, matrix products: 6.65 us -> none  [the longest x9 2.34 us: dot(): return jnp.dot(a, b, precision=highest)]
    ppermute x3, waiting for transfers between devices: 6.43 us -> 0.01 us  [the longest x1 0.01 us: local(): other_m = lax.ppermute(own_m, 'gy', swap)]
    pallas_call x0 -> x3, Pallas kernels: none -> 6.2 us  [the longest x1 2.3 us: prepare(): pl.pallas_call(body, name='prepare', compiler_params=limits, out_shape=(j...]
    mul x2 -> x1, other arithmetic: 2.81 us -> 0.01 us  [local(): exchange_stiffness * magnetic * (near[:3] - near[3:4] * direction)]
    unnamed x32 -> x29, local copies, waits for them, and re-layouts: 8.02 us -> 6.16 us
  transfers between devices with their start and end apart: 7 -> 7, of which waited for: 4 -> 2; matrix products, arithmetic and copies ran while one was open for 3% -> 0% of each run, Pallas kernels for 0% -> 2%
where the time goes in v1:
time: 159 us
  blocking collectives  89.7 us (56%)
  starting transfers between devices  29.4 us (18%)
  waiting for transfers between devices  24.1 us (15%)
  local copies, waits for them, and re-layouts  6.62 us (4%)
  Pallas kernels  6.2 us (4%)
    all_to_all x1, blocking collectives, local(): lax.all_to_all(send.reshape(columns, width // 2, 2, columns), 'gz', 0, 0,...  89.7 us
    all_to_all x1, waiting for transfers between devices, local(): recv_f = lax.all_to_all(send_f, 'gz', 0, 0, tiled=True)  23 us
    all_to_all x1, starting transfers between devices, local(): recv_f = lax.all_to_all(send_f, 'gz', 0, 0, tiled=True)  10 us
    unnamed x29, local copies, waits for them, and re-layouts  6.16 us
    ppermute x1, starting transfers between devices, local(): lax.ppermute(shares[0], 'parts', [(p, (p + k) % parts) for p in range(par...  4.84 us
    ppermute x1, starting transfers between devices, local(): before = lax.ppermute(stacked, 'gz', up)  4.59 us
    ppermute x1, starting transfers between devices, local(): after = lax.ppermute(stacked, 'gz', down)  3.42 us
  transfers between devices with their start and end apart: 7, of which 2 were waited for; matrix products, arithmetic and copies ran while one was open for 0% of the time, Pallas kernels for 2%

profile of v1, /device:TPU:66, one launch (start us, length us, event | category | flops | bytes accessed | tf_op | source)
XLA Modules:
  0.0 158.5 jit_solution(5888618559138388050)
XLA Ops:
  0.0 0.1 pad_add_fusion.refs_0_.where_ref
  0.1 0.6 copy-done.8
  0.7 0.0 copy-done.9
  0.7 1.1 copy-done
  1.9 0.9 copy-done.1
  2.8 0.9 copy-done.4
  3.7 0.9 copy-done.6
  4.6 0.8 copy-done.7
  5.4 2.3 %prepare.1 = (f32[1280,128]{1,0:T(8,128)S(1)}, f32[4,64,128]{2,1,0:T(8,128)S(1)}) custom-call(s32[3]{0:T(128)S(1)} %pad_add_fusion.refs_0_.where_ref, f32[3]{0:T(128)S(1)} %copy-done.9, f32[3,64,128]{2,1,0:T(8,128)S(1)} %bitcast.56, s32[64,128]{1,0:T(8,128)S(1)} %bitcast.58, f32[12,128,128]{2,1,0:T(8,128)S(1)} %bitcast.54, f32[6,2,128]{2,1,0:T(2,128)S(1)} %copy-done.8, ...), custom_call_target="tpu_custom_call" | custom-call | tf_op jit(solution)/shard_map/prepare/pallas_call | solution.py:158
  7.7 89.7 %all_to_all.10 = f32[128,5,2,128]{3,2,1,0:T(2,128)S(1)} all-to-all(f32[128,5,2,128]{3,2,1,0:T(2,128)S(1)} %bitcast.55), channel_id=1, replica_groups=mesh['parts'=2,'gz'=128,'gy'=2] {'gz'}, dimensions={0} | all-to-all | bytes 1310720 | tf_op jit(solution)/shard_map/all_to_all | solution.py:305
  97.5 0.0 copy-start.11
  97.5 0.0 copy-start.10
  97.5 2.1 %collective-permute-start = (f32[4,128,128]{2,1,0:T(8,128)S(1)}, f32[4,128,128]{2,1,0:T(8,128)S(1)}, u32[]{:S(2)}, u32[]{:S(2)}) collective-permute-start(f32[4,128,128]{2,1,0:T(8,128)S(1)} %slice.67.own), channel_id=1, source_target_pairs={{0,1},{1,0},{2,3},{3,2},{4,5},{5,4},{6,7},{7,6},{8,9},{9,8},{10,11... | collective-permute-start | bytes 786440 | tf_op jit(solution)/shard_map/ppermute | solution.py:311
  99.6 0.0 copy-done.11
  99.6 0.0 copy-done.10
  99.7 0.0 copy-start.3
  99.7 4.8 %collective-permute-start.1 = (f32[6,128,128]{2,1,0:T(8,128)S(1)}, f32[6,128,128]{2,1,0:T(8,128)S(1)}, u32[]{:S(2)}, u32[]{:S(2)}) collective-permute-start(f32[6,128,128]{2,1,0:T(8,128)S(1)} %slice.69.refs_5_), channel_id=1, source_target_pairs={{0,256},{256,0},{1,257},{257,1},{2,258},{258,2},{3,259},{259,3},{4... | collective-permute-start | bytes 1179656 | tf_op jit(solution)/shard_map/ppermute | solution.py:309
  104.6 0.0 collective-permute-done.other
  104.6 4.6 %collective-permute-start.2 = (f32[4,64,128]{2,1,0:T(8,128)S(1)}, f32[4,64,128]{2,1,0:T(8,128)S(1)}, u32[]{:S(2)}, u32[]{:S(2)}) collective-permute-start(f32[4,64,128]{2,1,0:T(8,128)S(1)} %get-tuple-element.20), channel_id=1, source_target_pairs={{0,2},{2,4},{4,6},{6,8},{8,10},{10,12},{12,14},{14,16},{16,18},{18... | collective-permute-start | bytes 393224 | tf_op jit(solution)/shard_map/ppermute | solution.py:315
  109.2 3.4 %collective-permute-start.3 = (f32[4,64,128]{2,1,0:T(8,128)S(1)}, f32[4,64,128]{2,1,0:T(8,128)S(1)}, u32[]{:S(2)}, u32[]{:S(2)}) collective-permute-start(f32[4,64,128]{2,1,0:T(8,128)S(1)} %get-tuple-element.20), channel_id=1, source_target_pairs={{2,0},{4,2},{6,4},{8,6},{10,8},{12,10},{14,12},{16,14},{18,16},{20... | collective-permute-start | bytes 393224 | tf_op jit(solution)/shard_map/ppermute | solution.py:316
  112.6 0.1 copy.29
  112.7 2.0 %collective-permute-start.4 = (f32[4,128]{1,0:T(4,128)S(1)}, f32[4,128]{1,0:T(4,128)S(1)}, u32[]{:S(2)}, u32[]{:S(2)}) collective-permute-start(f32[4,128]{1,0:T(4,128)S(1)} %fusion.11), channel_id=1, source_target_pairs={{0,1},{1,0},{2,3},{3,2},{4,5},{5,4},{6,7},{7,6},{8,9},{9,8},{10,11... | collective-permute-start | bytes 6152 | tf_op jit(solution)/shard_map/ppermute | solution.py:318
  114.7 0.0 copy-done.3
  114.7 0.0 copy-start.5
  114.7 1.6 %forward.1.refs_1_ = f32[4,256,256]{2,1,0:T(8,128)S(1)} custom-call(s32[3]{0:T(128)S(1)} %pad_add_fusion.refs_0_.where_ref, f32[4,128,128]{2,1,0:T(8,128)S(1)} %slice.67.own, f32[4,128,128]{2,1,0:T(8,128)S(1)} %collective-permute-done.other, bf16[2,256,256]{2,1,0:T(8,128)(2,1)S(1)} %dynamic-slice_bitcast_fusion.1.ty, bf16[2,256,256]{2,1,0:T(8,128)(2,1)S(1)} %copy-done.3), custom_call_target="tpu_custom_call" | custom-call | tf_op jit(solution)/shard_map/forward/pallas_call | solution.py:204
  116.4 0.0 collective-permute-done.1.refs_6_
  116.4 0.0 copy-done.5
  116.4 2.3 %inverse.1 = (f32[512,128]{1,0:T(8,128)S(1)}, f32[512,128]{1,0:T(8,128)S(1)}) custom-call(s32[3]{0:T(128)S(1)} %pad_add_fusion.refs_0_.where_ref, f32[4,256,256]{2,1,0:T(8,128)S(1)} %forward.1.refs_1_, f32[128,128]{1,0:T(8,128)S(1)} %slice_bitcast_fusion.refs_2_, bf16[2,256,256]{2,1,0:T(8,128)(2,1)S(1)} %dynamic-slice_bitcast_fusion.refs_3_, ...), custom_call_target="tpu_custom_call" | custom-call | tf_op jit(solution)/shard_map/inverse/pallas_call | solution.py:267
  118.7 0.0 collective-permute-done.4
  118.7 0.0 collective-permute-done.2
  118.7 0.0 collective-permute-done.3
  118.7 2.4 %collective-permute-start.5 = (f32[128,4,128]{2,1,0:T(4,128)S(1)}, f32[128,4,128]{2,1,0:T(4,128)S(1)}, u32[]{:S(2)}, u32[]{:S(2)}) collective-permute-start(f32[128,4,128]{2,1,0:T(4,128)S(1)} %bitcast.59), channel_id=1, source_target_pairs={{0,1},{1,0},{2,3},{3,2},{4,5},{5,4},{6,7},{7,6},{8,9},{9,8},{10,11... | collective-permute-start | bytes 786440 | tf_op jit(solution)/shard_map/ppermute | solution.py:325
  121.1 1.1 collective-permute-done.5
  122.3 0.8 add.42
  123.0 10.0 %all-to-all-start.1 = ((f32[128,4,128]{2,1,0:T(4,128)}), f32[128,4,128]{2,1,0:T(4,128)S(1)}, u32[]{:S(2)}, u32[]{:S(2)}) async-start(f32[128,4,128]{2,1,0:T(4,128)} %add.42), calls=%async_computation.1 | async-start | bytes 524288 | tf_op jit(solution)/shard_map/all_to_all | solution.py:326
  133.1 0.1 fusion.4
  133.3 23.0 %all-to-all-done.1 = f32[128,4,128]{2,1,0:T(4,128)S(1)} async-done(((f32[128,4,128]{2,1,0:T(4,128)}), f32[128,4,128]{2,1,0:T(4,128)S(1)}, u32[]{:S(2)}, u32[]{:S(2)}) %all-to-all-start.1) | async-done | bytes 262176 | tf_op jit(solution)/shard_map/all_to_all | solution.py:326
  156.2 0.1 copy.31
  156.4 0.0 copy-start.13
  156.4 0.1 slice.73
  156.5 0.1 copy.38
  156.6 0.0 copy-start.12
  156.6 0.0 copy-start.2
  156.6 0.7 copy-done.13
  157.3 0.2 convolution_bitcast_fusion.1
  157.5 0.0 copy-done.12
  157.5 0.0 copy-done.2
  157.6 1.0 fusion.2
  (21 shorter events, 0.2 us)
Async XLA Ops:
  0.0 0.7 copy-start.8
  0.1 0.7 copy-start.9
  0.7 1.1 copy-start
  1.9 0.9 copy-start.1
  2.8 0.9 copy-start.4
  3.7 0.9 copy-start.6
  4.6 0.8 copy-start.7
  97.5 2.1 %copy-start.11 = (bf16[2,2,256,256]{3,2,0,1:T(8,128)(2,1)S(1)}, bf16[2,2,256,256]{3,2,0,1:T(8,128)(2,1)}, u32[]{:S(2)}) copy-start(bf16[2,2,256,256]{3,2,0,1:T(8,128)(2,1)} %constant.54.clone) | copy-start | bytes 1572868
  97.5 2.2 %copy-start.10 = (bf16[2,2,256,256]{3,2,0,1:T(8,128)(2,1)S(1)}, bf16[2,2,256,256]{3,2,0,1:T(8,128)(2,1)}, u32[]{:S(2)}) copy-start(bf16[2,2,256,256]{3,2,0,1:T(8,128)(2,1)} %constant.55.clone) | copy-start | bytes 1572868
  97.5 7.1 %collective-permute-start = (f32[4,128,128]{2,1,0:T(8,128)S(1)}, f32[4,128,128]{2,1,0:T(8,128)S(1)}, u32[]{:S(2)}, u32[]{:S(2)}) collective-permute-start(f32[4,128,128]{2,1,0:T(8,128)S(1)} %slice.67.own), channel_id=1, source_target_pairs={{0,1},{1,0},{2,3},{3,2},{4,5},{5,4},{6,7},{7,6},{8,9},{9,8},{10,11... | collective-permute-start | bytes 786440 | tf_op jit(solution)/shard_map/ppermute | solution.py:311
  99.7 15.0 %copy-start.3 = (bf16[2,256,256]{2,1,0:T(8,128)(2,1)S(1)}, bf16[2,256,256]{2,1,0:T(8,128)(2,1)}, u32[]{:S(2)}) copy-start(bf16[2,256,256]{2,1,0:T(8,128)(2,1)} %constant.56.clone.tz) | copy-start | bytes 786436
  99.7 16.6 %collective-permute-start.1 = (f32[6,128,128]{2,1,0:T(8,128)S(1)}, f32[6,128,128]{2,1,0:T(8,128)S(1)}, u32[]{:S(2)}, u32[]{:S(2)}) collective-permute-start(f32[6,128,128]{2,1,0:T(8,128)S(1)} %slice.69.refs_5_), channel_id=1, source_target_pairs={{0,256},{256,0},{1,257},{257,1},{2,258},{258,2},{3,259},{259,3},{4... | collective-permute-start | bytes 1179656 | tf_op jit(solution)/shard_map/ppermute | solution.py:309
  104.6 14.1 %collective-permute-start.2 = (f32[4,64,128]{2,1,0:T(8,128)S(1)}, f32[4,64,128]{2,1,0:T(8,128)S(1)}, u32[]{:S(2)}, u32[]{:S(2)}) collective-permute-start(f32[4,64,128]{2,1,0:T(8,128)S(1)} %get-tuple-element.20), channel_id=1, source_target_pairs={{0,2},{2,4},{4,6},{6,8},{8,10},{10,12},{12,14},{14,16},{16,18},{18... | collective-permute-start | bytes 393224 | tf_op jit(solution)/shard_map/ppermute | solution.py:315
  109.2 9.5 %collective-permute-start.3 = (f32[4,64,128]{2,1,0:T(8,128)S(1)}, f32[4,64,128]{2,1,0:T(8,128)S(1)}, u32[]{:S(2)}, u32[]{:S(2)}) collective-permute-start(f32[4,64,128]{2,1,0:T(8,128)S(1)} %get-tuple-element.20), channel_id=1, source_target_pairs={{2,0},{4,2},{6,4},{8,6},{10,8},{12,10},{14,12},{16,14},{18,16},{20... | collective-permute-start | bytes 393224 | tf_op jit(solution)/shard_map/ppermute | solution.py:316
  112.7 5.9 %collective-permute-start.4 = (f32[4,128]{1,0:T(4,128)S(1)}, f32[4,128]{1,0:T(4,128)S(1)}, u32[]{:S(2)}, u32[]{:S(2)}) collective-permute-start(f32[4,128]{1,0:T(4,128)S(1)} %fusion.11), channel_id=1, source_target_pairs={{0,1},{1,0},{2,3},{3,2},{4,5},{5,4},{6,7},{7,6},{8,9},{9,8},{10,11... | collective-permute-start | bytes 6152 | tf_op jit(solution)/shard_map/ppermute | solution.py:318
  114.7 1.7 %copy-start.5 = (bf16[2,128,512]{2,1,0:T(8,128)(2,1)S(1)}, bf16[2,128,512]{2,1,0:T(8,128)(2,1)}, u32[]{:S(2)}) copy-start(bf16[2,128,512]{2,1,0:T(8,128)(2,1)} %constant.57.clone.refs_4_) | copy-start | bytes 786436
  118.7 3.6 %collective-permute-start.5 = (f32[128,4,128]{2,1,0:T(4,128)S(1)}, f32[128,4,128]{2,1,0:T(4,128)S(1)}, u32[]{:S(2)}, u32[]{:S(2)}) collective-permute-start(f32[128,4,128]{2,1,0:T(4,128)S(1)} %bitcast.59), channel_id=1, source_target_pairs={{0,1},{1,0},{2,3},{3,2},{4,5},{5,4},{6,7},{7,6},{8,9},{9,8},{10,11... | collective-permute-start | bytes 786440 | tf_op jit(solution)/shard_map/ppermute | solution.py:325
  123.0 33.2 %all-to-all-start.1 = ((f32[128,4,128]{2,1,0:T(4,128)}), f32[128,4,128]{2,1,0:T(4,128)S(1)}, u32[]{:S(2)}, u32[]{:S(2)}) async-start(f32[128,4,128]{2,1,0:T(4,128)} %add.42), calls=%async_computation.1 | async-start | bytes 524288 | tf_op jit(solution)/shard_map/all_to_all | solution.py:326
  156.4 1.0 copy-start.13
  156.6 0.9 copy-start.12
  156.6 0.9 copy-start.2

commit v2 on v1

--- a/solution.py
+++ b/solution.py
@@ -1,5 +1,3 @@
-import math
-
 import jax
 import jax.numpy as jnp
 import numpy as np
@@ -8,9 +6,9 @@
 from jax.experimental.pallas import tpu as pltpu
 from jax.sharding import PartitionSpec as P
 
+
 exchange_stiffness = 0.25
 tensor_index = ((0, 3, 4), (3, 1, 5), (4, 5, 2))
-highest = lax.Precision.HIGHEST
 components = 12
 swap = [(0, 1), (1, 0)]
 bf16 = jnp.bfloat16
@@ -61,7 +59,7 @@
         c, s = wave(ky, y[g * half : (g + 1) * half], 2 * rows)
         c, s = c.reshape(2, rows, half), s.reshape(2, rows, half)
         forward.append(np.concatenate([c[0], -s[0], c[1], -s[1]], axis=1))
-        back.append(np.stack([c[0], -s[0], c[1], -s[1]]) * scale)
+        back.append(np.concatenate([c[0].T, -s[0].T, c[1].T, -s[1].T], axis=0) * scale)
     out["ny"] = np.stack(forward)
     out["ny_back"] = np.stack(back)
     return out
@@ -91,7 +89,7 @@
 
 def prepare_kernel(share, mine_ref, sat_ref, dir_hbm, reg_hbm, main_hbm, nyq_hbm, tx_hbm, ny_hbm,
                    send_ref, stack_ref, dirs, reg, main, nyq, tx, ny, rows_t, sems):
-    three_c, half, columns = dirs.shape
+    _, half, columns = dirs.shape
     width = 4 + share
     copies = [
         pltpu.make_async_copy(reg_hbm, reg, sems.at[0]),
@@ -175,13 +173,13 @@
             pltpu.VMEM((columns, columns), f32),
             pltpu.SemaphoreType.DMA((6,)),
         ],
-    )(mine, saturation, direction, region, kernel_main, kernel_nyq, tx, ny)
+    )(mine, saturation, *(pltpu.with_memory_space_constraint(a, pltpu.HBM) for a in (direction, region, kernel_main, kernel_nyq, tx, ny)))
 
 
 def forward_kernel(where_ref, own, other, ty, tz, out):
     planes, width = own.shape[1:]
     table = (tz[0], tz[1])
-    y_table = (ty[0], ty[1])
+    y_table = (ty[0, where_ref[1]], ty[1, where_ref[1]])
     for c in range(4):
         if c < 3:
             ready = three(split(jnp.concatenate([own[c], other[c]], axis=1)), y_table)
@@ -212,11 +210,11 @@
 
 
 def inverse_kernel(parts, share, where_ref, *refs):
-    spectra, row_ref, ty, tz, *shares, own, other = refs
+    spectra, row_ref, stack, ty, tz, *shares, own, other = refs
     planes, width = row_ref.shape
     part = where_ref[2]
     table = (tz[0], tz[1])
-    y_table = (ty[0], ty[1])
+    y_table = (ty[0, where_ref[1]], ty[1, where_ref[1]])
 
     def kernel_row(c):
         owner = c // share
@@ -252,9 +250,14 @@
     line = jnp.where(where_ref[1] == 0, line, pltpu.roll(line, 64, 1))
     own[pl.ds(3, planes, stride=4), :] = line
     other[pl.ds(3, planes, stride=4), :] = line
-
-
-def inverse(where, spectra, row, ty, tz, shares, share):
+    last = stack.shape[1] - 1
+    for c in range(4):
+        edge = jnp.where(where_ref[1] == 0, stack[c, last:], stack[c, :1])
+        other[4 * planes + c : 4 * planes + c + 1, :] = edge
+        other[4 * planes + 4 + c : 4 * planes + 5 + c, :] = edge
+
+
+def inverse(where, spectra, row, stacked, ty, tz, shares, share):
     planes, width = row.shape
     smem = pl.BlockSpec(memory_space=pltpu.SMEM)
     vmem = pl.BlockSpec(memory_space=pltpu.VMEM)
@@ -263,26 +266,59 @@
     def body(*refs):
         inverse_kernel(parts, share, *refs)
 
-    half = jax.ShapeDtypeStruct((4 * planes, width), f32)
+    shape = lambda rows: jax.ShapeDtypeStruct((rows, width), f32)
     return pl.pallas_call(
         body,
         name="inverse",
         compiler_params=limits,
-        out_shape=(half, half),
-        in_specs=[smem] + [vmem] * (4 + parts),
+        out_shape=(shape(4 * planes), shape(4 * planes + 8)),
+        in_specs=[smem] + [vmem] * (5 + parts),
         out_specs=(vmem, vmem),
-    )(where, spectra, row, ty, tz, *shares)
-
-
-def back_x(received, tx_back, ny_back, signs):
-    columns = received.shape[0]
-    half = received.shape[2] // 2
-    main = received[:, :3].reshape(columns, 3, 2, half)
-    table = tx_back.reshape(columns, 2, columns)
-    demag = jnp.einsum("kcry,krx->cyx", main, table, precision=highest)
-    extra = received[:, 3].reshape(columns, 4, 32)[:, :, :12].reshape(columns, 4, 3, 4)[..., :3].sum(axis=3)
-    nyquist = jnp.einsum("gqi,qgy->iy", extra, ny_back, precision=highest)
-    return demag + nyquist[:, :, None] * signs
+    )(where, spectra, row, stacked, ty, tz, *shares)
+
+
+def finish_kernel(where_ref, recv, arrived, stack, before, after, tx, ny, out):
+    _, half, columns = stack.shape
+    lane = lax.broadcasted_iota(jnp.int32, (half, columns), 1)
+    line = lax.broadcasted_iota(jnp.int32, (half, columns), 0)
+    signs = (1 - 2 * (lane % 2)).astype(f32)
+    lower = where_ref[1] == 0
+
+    def near(c):
+        one = stack[c]
+        edge = arrived[pl.ds(4 * columns + c, 1), :]
+        low = jnp.where(line == 0, jnp.where(lower, 0.0, edge), pltpu.roll(one, 1, 0))
+        high = jnp.where(line == half - 1, jnp.where(lower, edge, 0.0), pltpu.roll(one, half - 1, 0))
+        left = jnp.where(lane == 0, 0.0, pltpu.roll(one, 1, 1))
+        right = jnp.where(lane == columns - 1, 0.0, pltpu.roll(one, columns - 1, 1))
+        return before[c] + after[c] + low + high + left + right
+
+    count = near(3)
+    magnetic = stack[3]
+    nyquist = three((ny[0, where_ref[1]], ny[1, where_ref[1]]), split(recv[pl.ds(3, columns, stride=4), :]))
+    sums = jnp.zeros((half, columns), f32)
+    for q in range(4):
+        sums = jnp.where(lane // 32 == q, nyquist[q * half : (q + 1) * half], sums)
+    table = (tx[0], tx[1])
+    for c in range(3):
+        prod = three(split(recv[pl.ds(c, columns, stride=4), :].T), table)
+        demag = prod[:half, :columns] + prod[half:, columns:]
+        total = jnp.sum(jnp.where(lane % 32 // 4 == c, sums, 0.0), axis=1, keepdims=True)
+        exchange = exchange_stiffness * (magnetic * near(c) - count * stack[c])
+        out[c] = demag + total * signs + exchange
+
+
+def finish(where, recv, arrived, stacked, before, after, tx, ny):
+    smem = pl.BlockSpec(memory_space=pltpu.SMEM)
+    vmem = pl.BlockSpec(memory_space=pltpu.VMEM)
+    return pl.pallas_call(
+        finish_kernel,
+        name="finish",
+        compiler_params=limits,
+        out_shape=jax.ShapeDtypeStruct((3,) + stacked.shape[1:], f32),
+        in_specs=[smem] + [vmem] * 7,
+        out_specs=vmem,
+    )(where, recv, arrived, stacked, before, after, tx, ny)
 
 
 def local(direction, region, saturation, kernel_main, kernel_nyq):
@@ -314,26 +350,15 @@
     stacked, other_m = lax.optimization_barrier((stacked, other_m))
     before = lax.ppermute(stacked, "gz", up)
     after = lax.ppermute(stacked, "gz", down)
-    edge = jnp.where(y_index == 0, stacked[:, -1], stacked[:, 0])
-    edge = lax.ppermute(edge, "gy", swap)
-    ty = halves(t["ty"])[:, y_index]
-    ty_back = halves(t["ty_back"])[:, y_index]
-    spectra = forward(where, own_m, other_m, ty, halves(t["tz"]))
-    own, other = inverse(where, spectra, own_m[3], ty_back, halves(t["tz_back"]), shares, share)
-    own, other = (a.reshape(groups_z, 4, columns) for a in (own, other))
-    other, before, after, edge = lax.optimization_barrier((other, before, after, edge))
-    send_f = own + lax.ppermute(other, "gy", swap)
-    recv_f = lax.all_to_all(send_f, "gz", 0, 0, tiled=True)
-    magnetic = stacked[3:4]
-    low = jnp.where(y_index == 0, 0.0, edge)[:, None]
-    high = jnp.where(y_index == 0, edge, 0.0)[:, None]
-    tall = jnp.concatenate([low, stacked, high], axis=1)
-    wide = jnp.pad(stacked, ((0, 0), (0, 0), (1, 1)))
-    near = before + after + tall[:, :-2] + tall[:, 2:] + wide[..., :-2] + wide[..., 2:]
-    exchange = exchange_stiffness * magnetic * (near[:3] - near[3:4] * direction)
-    signs = (1.0 - 2.0 * (jnp.arange(columns) % 2)).astype(f32)
-    demag = back_x(recv_f, jnp.asarray(t["tx_back"], f32), jnp.asarray(t["ny_back"], f32)[y_index], signs)
-    return (demag + exchange)[:, None]
+    spectra = forward(where, own_m, other_m, halves(t["ty"]), halves(t["tz"]))
+    own, other = inverse(where, spectra, own_m[3], stacked, halves(t["ty_back"]), halves(t["tz_back"]), shares, share)
+    other, before, after = lax.optimization_barrier((other, before, after))
+    arrived = lax.ppermute(other, "gy", swap)
+    send_f = own + arrived[: 4 * groups_z]
+    recv_f = lax.all_to_all(send_f.reshape(groups_z, 4, columns), "gz", 0, 0, tiled=True)
+    recv_f = recv_f.reshape(4 * columns, columns)
+    tx_back, ny_back = halves(t["tx_back"]), halves(t["ny_back"])
+    return finish(where, recv_f, arrived, stacked, before, after, tx_back, ny_back)[:, None]
 
 
 def solution(mesh):
@@ -344,6 +369,7 @@
         P(None, "gz", "gy", None),
         P(None, "gz", "gy"),
     )
+
     return jax.shard_map(
         local,
         mesh=mesh,

time: 159 us -> 153 us (0.962)
  blocking collectives: 89.7 us -> 125 us
  waiting for transfers between devices: 24.1 us -> 1.55 us
  starting transfers between devices: 29.4 us -> 16.9 us
  local copies, waits for them, and re-layouts: 6.62 us -> 0.8 us
  Pallas kernels: 6.2 us -> 8.04 us
    all_to_all x0 -> x1, blocking collectives: none -> 34.9 us  [local(): lax.all_to_all(send_f.reshape(groups_z, 4, columns), 'gz', 0, 0, tiled=True)]
    all_to_all x1 -> x0, waiting for transfers between devices: 23 us -> none  [local(): recv_f = lax.all_to_all(send_f, 'gz', 0, 0, tiled=True)]
    all_to_all x1 -> x0, starting transfers between devices: 10 us -> none  [local(): recv_f = lax.all_to_all(send_f, 'gz', 0, 0, tiled=True)]
    unnamed x29 -> x14, local copies, waits for them, and re-layouts: 6.16 us -> 0.7 us
    ppermute x2 -> x1, starting transfers between devices: 4.39 us -> 1.95 us  [local(): arrived = lax.ppermute(other, 'gy', swap)]
    pallas_call x1 -> x2, Pallas kernels: 2.27 us -> 3.86 us  [the longest x1 2.27 us: inverse(): pl.pallas_call(body, name='inverse', compiler_params=limits, out_shape=(s...]
  transfers between devices with their start and end apart: 7 -> 5, of which waited for: 2 -> 1; matrix products, arithmetic and copies ran while one was open for 0% -> 0% of each run, Pallas kernels for 2% -> 3%
where the time goes in v2:
time: 153 us; the launch traced here: 152 us
  blocking collectives  125 us (82%)
  starting transfers between devices  16.9 us (11%)
  Pallas kernels  8.04 us (5%)
  waiting for transfers between devices  1.55 us (1%)
    all_to_all x1, blocking collectives, local(): lax.all_to_all(send.reshape(columns, width // 2, 2, columns), 'gz', 0, 0,...  89.7 us
    all_to_all x1, blocking collectives, local(): lax.all_to_all(send_f.reshape(groups_z, 4, columns), 'gz', 0, 0, tiled=True)  34.9 us
    ppermute x1, starting transfers between devices, local(): lax.ppermute(shares[0], 'parts', [(p, (p + k) % parts) for p in range(par...  4.85 us
    ppermute x1, starting transfers between devices, local(): before = lax.ppermute(stacked, 'gz', up)  4.6 us
    ppermute x1, starting transfers between devices, local(): after = lax.ppermute(stacked, 'gz', down)  3.41 us
  transfers between devices with their start and end apart: 5, of which 1 were waited for; matrix products, arithmetic and copies ran while one was open for 0% of the time, Pallas kernels for 3%

profile of v2, /device:TPU:66, one launch (start us, length us, event | category | flops | bytes accessed | tf_op | source)
XLA Modules:
  0.0 152.2 jit_solution(5545223365799306411)
XLA Ops:
  0.0 0.1 pad_add_fusion.refs_0_.where_ref
  0.1 0.0 copy-start.6
  0.1 0.7 copy-done.6
  0.7 2.6 %prepare.1 = (f32[1280,128]{1,0:T(8,128)S(1)}, f32[4,64,128]{2,1,0:T(8,128)S(1)}) custom-call(s32[3]{0:T(128)S(1)} %pad_add_fusion.refs_0_.where_ref, f32[3]{0:T(128)S(1)} %copy-done.6, f32[3,64,128]{2,1,0:T(8,128)} %bitcast.24, s32[64,128]{1,0:T(8,128)} %bitcast.25, f32[12,128,128]{2,1,0:T(8,128)} %bitcast.23, f32[6,2,128]{2,1,0:T(2,128)} %refs_5_.2, ...), custom_call_target="tpu_custom_call" | custom-call | tf_op jit(solution)/shard_map/prepare/pallas_call | solution.py:156
  3.3 89.7 %all_to_all.10 = f32[128,5,2,128]{3,2,1,0:T(2,128)S(1)} all-to-all(f32[128,5,2,128]{3,2,1,0:T(2,128)S(1)} %bitcast.18), channel_id=1, replica_groups=mesh['parts'=2,'gz'=128,'gy'=2] {'gz'}, dimensions={0} | all-to-all | bytes 1310720 | tf_op jit(solution)/shard_map/all_to_all | solution.py:341
  93.1 0.0 copy-start
  93.1 2.1 %collective-permute-start = (f32[4,128,128]{2,1,0:T(8,128)S(1)}, f32[4,128,128]{2,1,0:T(8,128)S(1)}, u32[]{:S(2)}, u32[]{:S(2)}) collective-permute-start(f32[4,128,128]{2,1,0:T(8,128)S(1)} %slice.17.own), channel_id=1, source_target_pairs={{0,1},{1,0},{2,3},{3,2},{4,5},{5,4},{6,7},{7,6},{8,9},{9,8},{10,11... | collective-permute-start | bytes 786440 | tf_op jit(solution)/shard_map/ppermute | solution.py:347
  95.2 0.0 copy-start.4
  95.3 4.8 %collective-permute-start.1 = (f32[6,128,128]{2,1,0:T(8,128)S(1)}, f32[6,128,128]{2,1,0:T(8,128)S(1)}, u32[]{:S(2)}, u32[]{:S(2)}) collective-permute-start(f32[6,128,128]{2,1,0:T(8,128)S(1)} %slice.19.refs_6_), channel_id=1, source_target_pairs={{0,256},{256,0},{1,257},{257,1},{2,258},{258,2},{3,259},{259,3},{4... | collective-permute-start | bytes 1179656 | tf_op jit(solution)/shard_map/ppermute | solution.py:345
  100.1 0.0 collective-permute-done.other
  100.1 4.6 %collective-permute-start.2 = (f32[4,64,128]{2,1,0:T(8,128)S(1)}, f32[4,64,128]{2,1,0:T(8,128)S(1)}, u32[]{:S(2)}, u32[]{:S(2)}) collective-permute-start(f32[4,64,128]{2,1,0:T(8,128)S(1)} %get-tuple-element.17.refs_3_.stack), channel_id=1, source_target_pairs={{0,2},{2,4},{4,6},{6,8},{8,10},{10,12},{12,14},{14,16},{16,18},{18... | collective-permute-start | bytes 393224 | tf_op jit(solution)/shard_map/ppermute | solution.py:351
  104.7 3.4 %collective-permute-start.3 = (f32[4,64,128]{2,1,0:T(8,128)S(1)}, f32[4,64,128]{2,1,0:T(8,128)S(1)}, u32[]{:S(2)}, u32[]{:S(2)}) collective-permute-start(f32[4,64,128]{2,1,0:T(8,128)S(1)} %get-tuple-element.17.refs_3_.stack), channel_id=1, source_target_pairs={{2,0},{4,2},{6,4},{8,6},{10,8},{12,10},{14,12},{16,14},{18,16},{20... | collective-permute-start | bytes 393224 | tf_op jit(solution)/shard_map/ppermute | solution.py:352
  108.2 0.0 copy-done
  108.2 0.0 copy-done.4
  108.2 0.0 copy-start.1
  108.2 0.0 copy-start.3
  108.2 1.6 %forward.1.refs_1_ = f32[4,256,256]{2,1,0:T(8,128)S(1)} custom-call(s32[3]{0:T(128)S(1)} %pad_add_fusion.refs_0_.where_ref, f32[4,128,128]{2,1,0:T(8,128)S(1)} %slice.17.own, f32[4,128,128]{2,1,0:T(8,128)S(1)} %collective-permute-done.other, bf16[2,2,256,256]{3,2,1,0:T(8,128)(2,1)S(1)} %copy-done, bf16[2,256,256]{2,1,0:T(8,128)(2,1)S(1)} %copy-done.4), custom_call_target="tpu_custom_call" | custom-call | tf_op jit(solution)/shard_map/forward/pallas_call | solution.py:202
  109.8 0.0 collective-permute-done.1.refs_7_
  109.9 0.0 copy-done.1
  109.9 0.0 copy-done.3
  109.9 2.3 %inverse.1 = (f32[512,128]{1,0:T(8,128)S(1)}, f32[520,128]{1,0:T(8,128)S(1)}) custom-call(s32[3]{0:T(128)S(1)} %pad_add_fusion.refs_0_.where_ref, f32[4,256,256]{2,1,0:T(8,128)S(1)} %forward.1.refs_1_, f32[128,128]{1,0:T(8,128)S(1)} %slice_bitcast_fusion.refs_2_, f32[4,64,128]{2,1,0:T(8,128)S(1)} %get-tuple-element.17.refs_3_.stack, ...), custom_call_target="tpu_custom_call" | custom-call | tf_op jit(solution)/shard_map/inverse/pallas_call | solution.py:270
  112.2 0.0 collective-permute-done.2.before
  112.2 0.0 collective-permute-done.3.after
  112.2 2.0 %collective-permute-start.4 = (f32[520,128]{1,0:T(8,128)S(1)}, f32[520,128]{1,0:T(8,128)S(1)}, u32[]{:S(2)}, u32[]{:S(2)}) collective-permute-start(f32[520,128]{1,0:T(8,128)S(1)} %get-tuple-element.20), channel_id=1, source_target_pairs={{0,1},{1,0},{2,3},{3,2},{4,5},{5,4},{6,7},{7,6},{8,9},{9,8},{10,11... | collective-permute-start | bytes 798728 | tf_op jit(solution)/shard_map/ppermute | solution.py:356
  114.1 1.5 collective-permute-done.4.arrived
  115.7 0.0 copy-start.2
  115.7 0.0 copy-start.5
  115.7 34.9 %all_to_all.11 = f32[128,4,128]{2,1,0:T(4,128)S(1)} all-to-all(f32[128,4,128]{2,1,0:T(4,128)S(1)} %bitcast.22), channel_id=1, replica_groups=mesh['parts'=2,'gz'=128,'gy'=2] {'gz'}, dimensions={0} | all-to-all | bytes 524288 | tf_op jit(solution)/shard_map/all_to_all | solution.py:358
  150.6 0.0 copy-done.2
  150.6 0.0 copy-done.5
  150.6 1.6 %finish.1 = f32[3,64,128]{2,1,0:T(8,128)} custom-call(s32[3]{0:T(128)S(1)} %pad_add_fusion.refs_0_.where_ref, f32[512,128]{1,0:T(8,128)S(1)} %bitcast.17, f32[520,128]{1,0:T(8,128)S(1)} %collective-permute-done.4.arrived, f32[4,64,128]{2,1,0:T(8,128)S(1)} %get-tuple-element.17.refs_3_.stack, f32[4,64,128]{2,1,0:T(8,128)S(1)} %collective-permute-done.2.before, ...), custom_call_target="tpu_custom_call" | custom-call | tf_op jit(solution)/shard_map/finish/pallas_call | solution.py:314
  (5 shorter events, 0.1 us)
Async XLA Ops:
  0.1 0.7 copy-start.6
  93.1 15.1 %copy-start = (bf16[2,2,256,256]{3,2,1,0:T(8,128)(2,1)S(1)}, bf16[2,2,256,256]{3,2,1,0:T(8,128)(2,1)}, u32[]{:S(2)}) copy-start(bf16[2,2,256,256]{3,2,1,0:T(8,128)(2,1)} %constant.28.clone.ty) | copy-start | bytes 1572868
  93.1 7.0 %collective-permute-start = (f32[4,128,128]{2,1,0:T(8,128)S(1)}, f32[4,128,128]{2,1,0:T(8,128)S(1)}, u32[]{:S(2)}, u32[]{:S(2)}) collective-permute-start(f32[4,128,128]{2,1,0:T(8,128)S(1)} %slice.17.own), channel_id=1, source_target_pairs={{0,1},{1,0},{2,3},{3,2},{4,5},{5,4},{6,7},{7,6},{8,9},{9,8},{10,11... | collective-permute-start | bytes 786440 | tf_op jit(solution)/shard_map/ppermute | solution.py:347
  95.2 13.0 %copy-start.4 = (bf16[2,256,256]{2,1,0:T(8,128)(2,1)S(1)}, bf16[2,256,256]{2,1,0:T(8,128)(2,1)}, u32[]{:S(2)}) copy-start(bf16[2,256,256]{2,1,0:T(8,128)(2,1)} %constant.29.clone.tz) | copy-start | bytes 786436
  95.3 14.6 %collective-permute-start.1 = (f32[6,128,128]{2,1,0:T(8,128)S(1)}, f32[6,128,128]{2,1,0:T(8,128)S(1)}, u32[]{:S(2)}, u32[]{:S(2)}) collective-permute-start(f32[6,128,128]{2,1,0:T(8,128)S(1)} %slice.19.refs_6_), channel_id=1, source_target_pairs={{0,256},{256,0},{1,257},{257,1},{2,258},{258,2},{3,259},{259,3},{4... | collective-permute-start | bytes 1179656 | tf_op jit(solution)/shard_map/ppermute | solution.py:345
  100.1 12.0 %collective-permute-start.2 = (f32[4,64,128]{2,1,0:T(8,128)S(1)}, f32[4,64,128]{2,1,0:T(8,128)S(1)}, u32[]{:S(2)}, u32[]{:S(2)}) collective-permute-start(f32[4,64,128]{2,1,0:T(8,128)S(1)} %get-tuple-element.17.refs_3_.stack), channel_id=1, source_target_pairs={{0,2},{2,4},{4,6},{6,8},{8,10},{10,12},{12,14},{14,16},{16,18},{18... | collective-permute-start | bytes 393224 | tf_op jit(solution)/shard_map/ppermute | solution.py:351
  104.7 7.4 %collective-permute-start.3 = (f32[4,64,128]{2,1,0:T(8,128)S(1)}, f32[4,64,128]{2,1,0:T(8,128)S(1)}, u32[]{:S(2)}, u32[]{:S(2)}) collective-permute-start(f32[4,64,128]{2,1,0:T(8,128)S(1)} %get-tuple-element.17.refs_3_.stack), channel_id=1, source_target_pairs={{2,0},{4,2},{6,4},{8,6},{10,8},{12,10},{14,12},{16,14},{18,16},{20... | collective-permute-start | bytes 393224 | tf_op jit(solution)/shard_map/ppermute | solution.py:352
  108.2 1.7 %copy-start.1 = (bf16[2,2,256,256]{3,2,1,0:T(8,128)(2,1)S(1)}, bf16[2,2,256,256]{3,2,1,0:T(8,128)(2,1)}, u32[]{:S(2)}) copy-start(bf16[2,2,256,256]{3,2,1,0:T(8,128)(2,1)} %constant.30.clone.refs_4_) | copy-start | bytes 1572868
  108.2 1.7 %copy-start.3 = (bf16[2,128,512]{2,1,0:T(8,128)(2,1)S(1)}, bf16[2,128,512]{2,1,0:T(8,128)(2,1)}, u32[]{:S(2)}) copy-start(bf16[2,128,512]{2,1,0:T(8,128)(2,1)} %constant.31.clone.refs_5_) | copy-start | bytes 786436
  112.2 3.5 %collective-permute-start.4 = (f32[520,128]{1,0:T(8,128)S(1)}, f32[520,128]{1,0:T(8,128)S(1)}, u32[]{:S(2)}, u32[]{:S(2)}) collective-permute-start(f32[520,128]{1,0:T(8,128)S(1)} %get-tuple-element.20), channel_id=1, source_target_pairs={{0,1},{1,0},{2,3},{3,2},{4,5},{5,4},{6,7},{7,6},{8,9},{9,8},{10,11... | collective-permute-start | bytes 798728 | tf_op jit(solution)/shard_map/ppermute | solution.py:356
  115.7 35.0 %copy-start.2 = (bf16[2,2,256,128]{3,2,1,0:T(8,128)(2,1)S(1)}, bf16[2,2,256,128]{3,2,1,0:T(8,128)(2,1)}, u32[]{:S(2)}) copy-start(bf16[2,2,256,128]{3,2,1,0:T(8,128)(2,1)} %constant.33.clone.ny) | copy-start | bytes 786436
  115.7 34.9 %copy-start.5 = (bf16[2,128,256]{2,1,0:T(8,128)(2,1)S(1)}, bf16[2,128,256]{2,1,0:T(8,128)(2,1)}, u32[]{:S(2)}) copy-start(bf16[2,128,256]{2,1,0:T(8,128)(2,1)} %constant.32.clone.tx) | copy-start | bytes 393220

commit v3 on v2

--- a/solution.py
+++ b/solution.py
@@ -87,8 +87,8 @@
     return jnp.concatenate([jnp.concatenate([real, imag], axis=1), lower], axis=0)
 
 
-def prepare_kernel(share, mine_ref, sat_ref, dir_hbm, reg_hbm, main_hbm, nyq_hbm, tx_hbm, ny_hbm,
-                   send_ref, stack_ref, dirs, reg, main, nyq, tx, ny, rows_t, sems):
+def prepare_kernel(share, mine_ref, sat_hbm, dir_hbm, reg_hbm, main_hbm, nyq_hbm, tx_hbm, ny_hbm,
+                   send_ref, stack_ref, sat_ref, dirs, reg, main, nyq, tx, ny, rows_t, sems):
     _, half, columns = dirs.shape
     width = 4 + share
     copies = [
@@ -98,6 +98,7 @@
         pltpu.make_async_copy(tx_hbm, tx, sems.at[3]),
         pltpu.make_async_copy(ny_hbm.at[mine_ref[1]], ny, sems.at[4]),
         pltpu.make_async_copy(nyq_hbm, nyq, sems.at[5]),
+        pltpu.make_async_copy(sat_hbm, sat_ref, sems.at[6]),
     ]
     for c in copies:
         c.start()
@@ -106,6 +107,7 @@
     region = reg[...]
     magnetic = (region > 0).astype(f32)
     strength = jnp.zeros(region.shape, f32)
+    copies[6].wait()
     for r in range(3):
         strength = strength + jnp.where(region == r + 1, sat_ref[r], 0.0)
     copies[1].wait()
@@ -161,9 +163,10 @@
             jax.ShapeDtypeStruct((columns * (4 + share), columns), f32),
             jax.ShapeDtypeStruct((4, half, columns), f32),
         ),
-        in_specs=[smem, smem] + [any_spec] * 6,
+        in_specs=[smem] + [any_spec] * 7,
         out_specs=(vmem, vmem),
         scratch_shapes=[
+            pltpu.SMEM(saturation.shape, f32),
             pltpu.VMEM((3, half, columns), f32),
             pltpu.VMEM((half, columns), jnp.int32),
             pltpu.VMEM((share, rows, columns), f32),
@@ -171,9 +174,9 @@
             pltpu.VMEM(tx.shape, bf16),
             pltpu.VMEM(ny.shape[1:], bf16),
             pltpu.VMEM((columns, columns), f32),
-            pltpu.SemaphoreType.DMA((6,)),
+            pltpu.SemaphoreType.DMA((7,)),
         ],
-    )(mine, saturation, *(pltpu.with_memory_space_constraint(a, pltpu.HBM) for a in (direction, region, kernel_main, kernel_nyq, tx, ny)))
+    )(mine, *(pltpu.with_memory_space_constraint(a, pltpu.HBM) for a in (saturation, direction, region, kernel_main, kernel_nyq, tx, ny)))
 
 
 def forward_kernel(where_ref, own, other, ty, tz, out):
@@ -209,22 +212,17 @@
     )(where, own, other, ty, tz)
 
 
-def inverse_kernel(parts, share, where_ref, *refs):
+def inverse_kernel(pairs, share, where_ref, *refs):
     spectra, row_ref, stack, ty, tz, *shares, own, other = refs
     planes, width = row_ref.shape
-    part = where_ref[2]
     table = (tz[0], tz[1])
     y_table = (ty[0, where_ref[1]], ty[1, where_ref[1]])
 
     def kernel_row(c):
-        owner = c // share
-        at = c - min(owner * share, components - share)
-        piece = shares[0][at]
-        for k in range(1, parts):
-            gone = part - owner
-            gone = jnp.where(gone < 0, gone + parts, gone)
-            piece = jnp.where(gone == k, shares[k][at], piece)
-        return piece
+        owner, at = c // share, c % share
+        if pairs == 1:
+            return shares[0][at]
+        return jnp.where(where_ref[2] == owner, shares[0][at], shares[1][at])
 
     def back(real, imag):
         (rh, rl), (ih, il) = split(real), split(imag)
@@ -261,10 +259,10 @@
     planes, width = row.shape
     smem = pl.BlockSpec(memory_space=pltpu.SMEM)
     vmem = pl.BlockSpec(memory_space=pltpu.VMEM)
-    parts = len(shares)
+    pairs = len(shares)
 
     def body(*refs):
-        inverse_kernel(parts, share, *refs)
+        inverse_kernel(pairs, share, *refs)
 
     shape = lambda rows: jax.ShapeDtypeStruct((rows, width), f32)
     return pl.pallas_call(
@@ -272,7 +270,7 @@
         name="inverse",
         compiler_params=limits,
         out_shape=(shape(4 * planes), shape(4 * planes + 8)),
-        in_specs=[smem] + [vmem] * (5 + parts),
+        in_specs=[smem] + [vmem] * (5 + pairs),
         out_specs=(vmem, vmem),
     )(where, spectra, row, stacked, ty, tz, *shares)
 
@@ -329,10 +327,11 @@
     parts = lax.axis_size("parts")
     y_index = lax.axis_index("gy")
     part = lax.axis_index("parts")
-    share = -(-components // parts)
+    pairs = 2 if parts % 2 == 0 else 1
+    share = components // pairs
     t = tables(columns, rows, groups_z)
     direction = direction[:, 0]
-    where = jnp.stack([jnp.minimum(part * share, components - share), y_index, part])
+    where = jnp.stack([part % pairs * share, y_index, part % pairs])
     send, stacked = prepare(
         where, saturation, direction, region[0], kernel_main.reshape(components, rows, columns), kernel_nyq,
         halves(t["tx"]), halves(t["ny"]).swapaxes(0, 1), share,
@@ -341,18 +340,18 @@
     recv = lax.all_to_all(send.reshape(columns, width // 2, 2, columns), "gz", 0, 0, tiled=True)
     recv = recv.reshape(columns, width, columns).transpose(1, 0, 2)
     shares = [recv[4:]]
-    for k in range(1, parts):
-        shares.append(lax.ppermute(shares[0], "parts", [(p, (p + k) % parts) for p in range(parts)]))
+    if pairs == 2:
+        shares.append(lax.ppermute(shares[0], "parts", [(p, p ^ 1) for p in range(parts)]))
     own_m = recv[:4]
     other_m = lax.ppermute(own_m, "gy", swap)
     up = [(i, i + 1) for i in range(groups_z - 1)]
     down = [(b, a) for a, b in up]
-    stacked, other_m = lax.optimization_barrier((stacked, other_m))
     before = lax.ppermute(stacked, "gz", up)
     after = lax.ppermute(stacked, "gz", down)
     spectra = forward(where, own_m, other_m, halves(t["ty"]), halves(t["tz"]))
-    own, other = inverse(where, spectra, own_m[3], stacked, halves(t["ty_back"]), halves(t["tz_back"]), shares, share)
-    other, before, after = lax.optimization_barrier((other, before, after))
+    own, other = inverse(
+        where, spectra, own_m[3], stacked, halves(t["ty_back"]), halves(t["tz_back"]), shares, share
+    )
     arrived = lax.ppermute(other, "gy", swap)
     send_f = own + arrived[: 4 * groups_z]
     recv_f = lax.all_to_all(send_f.reshape(groups_z, 4, columns), "gz", 0, 0, tiled=True)

time: 153 us -> 148 us (0.967)
  blocking collectives: 125 us -> 89.7 us
  waiting for transfers between devices: 1.55 us -> 18.8 us
  starting transfers between devices: 16.9 us -> 29.7 us
    all_to_all x1 -> x0, blocking collectives: 34.9 us -> none  [local(): lax.all_to_all(send_f.reshape(groups_z, 4, columns), 'gz', 0, 0, tiled=True)]
    all_to_all x0 -> x1, starting transfers between devices: none -> 12.9 us  [local(): lax.all_to_all(send_f.reshape(groups_z, 4, columns), 'gz', 0, 0, tiled=True)]
    all_to_all x0 -> x1, waiting for transfers between devices: none -> 8.21 us  [local(): lax.all_to_all(send_f.reshape(groups_z, 4, columns), 'gz', 0, 0, tiled=True)]
    ppermute x1, waiting for transfers between devices: 0.01 us -> 6.85 us  [local(): before = lax.ppermute(stacked, 'gz', up)]
  transfers between devices with their start and end apart: 5 -> 6, of which waited for: 1 -> 5; matrix products, arithmetic and copies ran while one was open for 0% -> 0% of each run, Pallas kernels for 3% -> 1%
where the time goes in v3:
time: 148 us; the launch traced here: 147 us
  blocking collectives  89.7 us (61%)
  starting transfers between devices  29.7 us (20%)
  waiting for transfers between devices  18.8 us (13%)
  Pallas kernels  8.07 us (5%)
    all_to_all x1, blocking collectives, local(): lax.all_to_all(send.reshape(columns, width // 2, 2, columns), 'gz', 0, 0,...  89.7 us
    all_to_all x1, starting transfers between devices, local(): lax.all_to_all(send_f.reshape(groups_z, 4, columns), 'gz', 0, 0, tiled=True)  12.9 us
    all_to_all x1, waiting for transfers between devices, local(): lax.all_to_all(send_f.reshape(groups_z, 4, columns), 'gz', 0, 0, tiled=True)  8.21 us
    ppermute x1, waiting for transfers between devices, local(): before = lax.ppermute(stacked, 'gz', up)  6.85 us
    ppermute x1, starting transfers between devices, local(): lax.ppermute(shares[0], 'parts', [(p, p ^ 1) for p in range(parts)])  4.84 us
    ppermute x1, starting transfers between devices, local(): after = lax.ppermute(stacked, 'gz', down)  4.61 us
    ppermute x1, starting transfers between devices, local(): before = lax.ppermute(stacked, 'gz', up)  3.4 us
  transfers between devices with their start and end apart: 6, of which 5 were waited for; matrix products, arithmetic and copies ran while one was open for 0% of the time, Pallas kernels for 1%

profile of v3, /device:TPU:66, one launch (start us, length us, event | category | flops | bytes accessed | tf_op | source)
XLA Modules:
  0.0 147.3 jit_solution(15592855334029911097)
XLA Ops:
  0.0 0.1 pad_add_fusion.refs_0_.where_ref
  0.1 2.6 %prepare.1 = (f32[1280,128]{1,0:T(8,128)S(1)}, f32[4,64,128]{2,1,0:T(8,128)S(1)}) custom-call(s32[3]{0:T(128)S(1)} %pad_add_fusion.refs_0_.where_ref, f32[3]{0:T(128)} %refs_1_.1, f32[3,64,128]{2,1,0:T(8,128)} %bitcast.23, s32[64,128]{1,0:T(8,128)} %bitcast.24, f32[12,128,128]{2,1,0:T(8,128)} %bitcast.22, f32[6,2,128]{2,1,0:T(2,128)} %refs_5_.2, ...), custom_call_target="tpu_custom_call" | custom-call | tf_op jit(solution)/shard_map/prepare/pallas_call | solution.py:158
  2.7 89.7 %all_to_all.10 = f32[128,5,2,128]{3,2,1,0:T(2,128)S(1)} all-to-all(f32[128,5,2,128]{3,2,1,0:T(2,128)S(1)} %bitcast.18), channel_id=1, replica_groups=mesh['parts'=2,'gz'=128,'gy'=2] {'gz'}, dimensions={0} | all-to-all | bytes 1310720 | tf_op jit(solution)/shard_map/all_to_all | solution.py:340
  92.4 0.0 copy-start.4
  92.5 0.0 copy-start
  92.5 4.8 %collective-permute-start.1 = (f32[6,128,128]{2,1,0:T(8,128)S(1)}, f32[6,128,128]{2,1,0:T(8,128)S(1)}, u32[]{:S(2)}, u32[]{:S(2)}) collective-permute-start(f32[6,128,128]{2,1,0:T(8,128)S(1)} %slice.19.refs_6_), channel_id=1, source_target_pairs={{0,256},{256,0},{1,257},{257,1},{2,258},{258,2},{3,259},{259,3},{4... | collective-permute-start | bytes 1179656 | tf_op jit(solution)/shard_map/ppermute | solution.py:344
  97.4 2.0 %collective-permute-start = (f32[4,128,128]{2,1,0:T(8,128)S(1)}, f32[4,128,128]{2,1,0:T(8,128)S(1)}, u32[]{:S(2)}, u32[]{:S(2)}) collective-permute-start(f32[4,128,128]{2,1,0:T(8,128)S(1)} %slice.17.own), channel_id=1, source_target_pairs={{0,1},{1,0},{2,3},{3,2},{4,5},{5,4},{6,7},{7,6},{8,9},{9,8},{10,11... | collective-permute-start | bytes 786440 | tf_op jit(solution)/shard_map/ppermute | solution.py:346
  99.3 0.0 copy-start.1
  99.3 0.0 copy-start.3
  99.4 1.5 collective-permute-done.other
  100.8 0.0 copy-done.4
  100.8 0.0 copy-done
  100.8 1.6 %forward.1.refs_1_ = f32[4,256,256]{2,1,0:T(8,128)S(1)} custom-call(s32[3]{0:T(128)S(1)} %pad_add_fusion.refs_0_.where_ref, f32[4,128,128]{2,1,0:T(8,128)S(1)} %slice.17.own, f32[4,128,128]{2,1,0:T(8,128)S(1)} %collective-permute-done.other, bf16[2,2,256,256]{3,2,1,0:T(8,128)(2,1)S(1)} %copy-done, bf16[2,256,256]{2,1,0:T(8,128)(2,1)S(1)} %copy-done.4), custom_call_target="tpu_custom_call" | custom-call | tf_op jit(solution)/shard_map/forward/pallas_call | solution.py:205
  102.4 0.8 collective-permute-done.1.refs_7_
  103.2 0.0 copy-done.1
  103.2 0.0 copy-done.3
  103.2 2.3 %inverse.1 = (f32[512,128]{1,0:T(8,128)S(1)}, f32[520,128]{1,0:T(8,128)S(1)}) custom-call(s32[3]{0:T(128)S(1)} %pad_add_fusion.refs_0_.where_ref, f32[4,256,256]{2,1,0:T(8,128)S(1)} %forward.1.refs_1_, f32[128,128]{1,0:T(8,128)S(1)} %slice_bitcast_fusion.refs_2_, f32[4,64,128]{2,1,0:T(8,128)S(1)} %get-tuple-element.10.refs_3_.stack, ...), custom_call_target="tpu_custom_call" | custom-call | tf_op jit(solution)/shard_map/inverse/pallas_call | solution.py:268
  105.5 2.0 %collective-permute-start.2 = (f32[520,128]{1,0:T(8,128)S(1)}, f32[520,128]{1,0:T(8,128)S(1)}, u32[]{:S(2)}, u32[]{:S(2)}) collective-permute-start(f32[520,128]{1,0:T(8,128)S(1)} %get-tuple-element.12), channel_id=1, source_target_pairs={{0,1},{1,0},{2,3},{3,2},{4,5},{5,4},{6,7},{7,6},{8,9},{9,8},{10,11... | collective-permute-start | bytes 798728 | tf_op jit(solution)/shard_map/ppermute | solution.py:355
  107.5 1.5 %collective-permute-done.2.arrived = f32[520,128]{1,0:T(8,128)S(1)} collective-permute-done((f32[520,128]{1,0:T(8,128)S(1)}, f32[520,128]{1,0:T(8,128)S(1)}, u32[]{:S(2)}, u32[]{:S(2)}) %collective-permute-start.2) | collective-permute-done | bytes 266272 | tf_op jit(solution)/shard_map/ppermute | solution.py:355
  109.0 0.7 slice_add_fusion
  109.7 0.0 copy-start.2
  109.7 0.0 copy-start.5
  109.7 12.9 %all-to-all-start.1 = ((f32[128,4,128]{2,1,0:T(4,128)}), f32[128,4,128]{2,1,0:T(4,128)S(1)}, u32[]{:S(2)}, u32[]{:S(2)}) async-start(f32[128,4,128]{2,1,0:T(4,128)} %bitcast.11), calls=%async_computation.1 | async-start | bytes 524288 | tf_op jit(solution)/shard_map/all_to_all | solution.py:357
  122.7 3.4 %collective-permute-start.3 = (f32[4,64,128]{2,1,0:T(8,128)S(1)}, f32[4,64,128]{2,1,0:T(8,128)S(1)}, u32[]{:S(2)}, u32[]{:S(2)}) collective-permute-start(f32[4,64,128]{2,1,0:T(8,128)S(1)} %get-tuple-element.10.refs_3_.stack), channel_id=1, source_target_pairs={{0,2},{2,4},{4,6},{6,8},{8,10},{10,12},{12,14},{14,16},{16,18},{18... | collective-permute-start | bytes 393224 | tf_op jit(solution)/shard_map/ppermute | solution.py:349
  126.1 4.6 %collective-permute-start.4 = (f32[4,64,128]{2,1,0:T(8,128)S(1)}, f32[4,64,128]{2,1,0:T(8,128)S(1)}, u32[]{:S(2)}, u32[]{:S(2)}) collective-permute-start(f32[4,64,128]{2,1,0:T(8,128)S(1)} %get-tuple-element.10.refs_3_.stack), channel_id=1, source_target_pairs={{2,0},{4,2},{6,4},{8,6},{10,8},{12,10},{14,12},{16,14},{18,16},{20... | collective-permute-start | bytes 393224 | tf_op jit(solution)/shard_map/ppermute | solution.py:350
  130.7 6.8 %collective-permute-done.3.before = f32[4,64,128]{2,1,0:T(8,128)S(1)} collective-permute-done((f32[4,64,128]{2,1,0:T(8,128)S(1)}, f32[4,64,128]{2,1,0:T(8,128)S(1)}, u32[]{:S(2)}, u32[]{:S(2)}) %collective-permute-start.3) | collective-permute-done | bytes 131104 | tf_op jit(solution)/shard_map/ppermute | solution.py:349
  137.5 0.0 collective-permute-done.4.after
  137.5 8.2 %all-to-all-done.1 = f32[128,4,128]{2,1,0:T(4,128)S(1)} async-done(((f32[128,4,128]{2,1,0:T(4,128)}), f32[128,4,128]{2,1,0:T(4,128)S(1)}, u32[]{:S(2)}, u32[]{:S(2)}) %all-to-all-start.1) | async-done | bytes 262176 | tf_op jit(solution)/shard_map/all_to_all | solution.py:357
  145.8 0.0 copy-done.2
  145.8 0.0 copy-done.5
  145.8 1.6 %finish.1 = f32[3,64,128]{2,1,0:T(8,128)} custom-call(s32[3]{0:T(128)S(1)} %pad_add_fusion.refs_0_.where_ref, f32[512,128]{1,0:T(8,128)S(1)} %bitcast.17, f32[520,128]{1,0:T(8,128)S(1)} %collective-permute-done.2.arrived, f32[4,64,128]{2,1,0:T(8,128)S(1)} %get-tuple-element.10.refs_3_.stack, f32[4,64,128]{2,1,0:T(8,128)S(1)} %collective-permute-done.3.before, ...), custom_call_target="tpu_custom_call" | custom-call | tf_op jit(solution)/shard_map/finish/pallas_call | solution.py:312
  (4 shorter events, 0.1 us)
Async XLA Ops:
  92.4 8.4 %copy-start.4 = (bf16[2,256,256]{2,1,0:T(8,128)(2,1)S(1)}, bf16[2,256,256]{2,1,0:T(8,128)(2,1)}, u32[]{:S(2)}) copy-start(bf16[2,256,256]{2,1,0:T(8,128)(2,1)} %constant.44.clone.tz) | copy-start | bytes 786436
  92.5 8.3 %copy-start = (bf16[2,2,256,256]{3,2,1,0:T(8,128)(2,1)S(1)}, bf16[2,2,256,256]{3,2,1,0:T(8,128)(2,1)}, u32[]{:S(2)}) copy-start(bf16[2,2,256,256]{3,2,1,0:T(8,128)(2,1)} %constant.43.clone.ty) | copy-start | bytes 1572868
  92.5 10.7 %collective-permute-start.1 = (f32[6,128,128]{2,1,0:T(8,128)S(1)}, f32[6,128,128]{2,1,0:T(8,128)S(1)}, u32[]{:S(2)}, u32[]{:S(2)}) collective-permute-start(f32[6,128,128]{2,1,0:T(8,128)S(1)} %slice.19.refs_6_), channel_id=1, source_target_pairs={{0,256},{256,0},{1,257},{257,1},{2,258},{258,2},{3,259},{259,3},{4... | collective-permute-start | bytes 1179656 | tf_op jit(solution)/shard_map/ppermute | solution.py:344
  97.4 3.5 %collective-permute-start = (f32[4,128,128]{2,1,0:T(8,128)S(1)}, f32[4,128,128]{2,1,0:T(8,128)S(1)}, u32[]{:S(2)}, u32[]{:S(2)}) collective-permute-start(f32[4,128,128]{2,1,0:T(8,128)S(1)} %slice.17.own), channel_id=1, source_target_pairs={{0,1},{1,0},{2,3},{3,2},{4,5},{5,4},{6,7},{7,6},{8,9},{9,8},{10,11... | collective-permute-start | bytes 786440 | tf_op jit(solution)/shard_map/ppermute | solution.py:346
  99.3 3.9 %copy-start.1 = (bf16[2,2,256,256]{3,2,1,0:T(8,128)(2,1)S(1)}, bf16[2,2,256,256]{3,2,1,0:T(8,128)(2,1)}, u32[]{:S(2)}) copy-start(bf16[2,2,256,256]{3,2,1,0:T(8,128)(2,1)} %constant.45.clone.refs_4_) | copy-start | bytes 1572868
  99.3 3.9 %copy-start.3 = (bf16[2,128,512]{2,1,0:T(8,128)(2,1)S(1)}, bf16[2,128,512]{2,1,0:T(8,128)(2,1)}, u32[]{:S(2)}) copy-start(bf16[2,128,512]{2,1,0:T(8,128)(2,1)} %constant.46.clone.refs_5_) | copy-start | bytes 786436
  105.5 3.5 %collective-permute-start.2 = (f32[520,128]{1,0:T(8,128)S(1)}, f32[520,128]{1,0:T(8,128)S(1)}, u32[]{:S(2)}, u32[]{:S(2)}) collective-permute-start(f32[520,128]{1,0:T(8,128)S(1)} %get-tuple-element.12), channel_id=1, source_target_pairs={{0,1},{1,0},{2,3},{3,2},{4,5},{5,4},{6,7},{7,6},{8,9},{9,8},{10,11... | collective-permute-start | bytes 798728 | tf_op jit(solution)/shard_map/ppermute | solution.py:355
  109.7 36.0 %copy-start.2 = (bf16[2,2,256,128]{3,2,1,0:T(8,128)(2,1)S(1)}, bf16[2,2,256,128]{3,2,1,0:T(8,128)(2,1)}, u32[]{:S(2)}) copy-start(bf16[2,2,256,128]{3,2,1,0:T(8,128)(2,1)} %constant.48.clone.ny) | copy-start | bytes 786436
  109.7 36.0 %copy-start.5 = (bf16[2,128,256]{2,1,0:T(8,128)(2,1)S(1)}, bf16[2,128,256]{2,1,0:T(8,128)(2,1)}, u32[]{:S(2)}) copy-start(bf16[2,128,256]{2,1,0:T(8,128)(2,1)} %constant.47.clone.tx) | copy-start | bytes 393220
  109.7 36.0 %all-to-all-start.1 = ((f32[128,4,128]{2,1,0:T(4,128)}), f32[128,4,128]{2,1,0:T(4,128)S(1)}, u32[]{:S(2)}, u32[]{:S(2)}) async-start(f32[128,4,128]{2,1,0:T(4,128)} %bitcast.11), calls=%async_computation.1 | async-start | bytes 524288 | tf_op jit(solution)/shard_map/all_to_all | solution.py:357
  122.7 14.9 %collective-permute-start.3 = (f32[4,64,128]{2,1,0:T(8,128)S(1)}, f32[4,64,128]{2,1,0:T(8,128)S(1)}, u32[]{:S(2)}, u32[]{:S(2)}) collective-permute-start(f32[4,64,128]{2,1,0:T(8,128)S(1)} %get-tuple-element.10.refs_3_.stack), channel_id=1, source_target_pairs={{0,2},{2,4},{4,6},{6,8},{8,10},{10,12},{12,14},{14,16},{16,18},{18... | collective-permute-start | bytes 393224 | tf_op jit(solution)/shard_map/ppermute | solution.py:349
  126.1 11.5 %collective-permute-start.4 = (f32[4,64,128]{2,1,0:T(8,128)S(1)}, f32[4,64,128]{2,1,0:T(8,128)S(1)}, u32[]{:S(2)}, u32[]{:S(2)}) collective-permute-start(f32[4,64,128]{2,1,0:T(8,128)S(1)} %get-tuple-element.10.refs_3_.stack), channel_id=1, source_target_pairs={{2,0},{4,2},{6,4},{8,6},{10,8},{12,10},{14,12},{16,14},{18,16},{20... | collective-permute-start | bytes 393224 | tf_op jit(solution)/shard_map/ppermute | solution.py:350

commit v4 on v3

--- a/solution.py
+++ b/solution.py
@@ -9,7 +9,6 @@
 
 exchange_stiffness = 0.25
 tensor_index = ((0, 3, 4), (3, 1, 5), (4, 5, 2))
-components = 12
 swap = [(0, 1), (1, 0)]
 bf16 = jnp.bfloat16
 f32 = jnp.float32
@@ -50,7 +49,7 @@
     out["ty_back"] = np.stack(back)
     c, s = wave(slot_frequencies(groups_z), z, 2 * groups_z)
     out["tz"] = np.concatenate([c, s], axis=1)
-    out["tz_back"] = np.concatenate([c.T, s.T], axis=1)
+    out["tz_back"] = np.stack([np.concatenate([t[k * groups_z : (k + 1) * groups_z].T for t in (c, s)], axis=1) for k in range(2)])
     w = np.where(x == 0, 1.0, 2.0)[:, None]
     scale = 1.0 / (2.0 * columns * 2.0 * rows * 2.0 * groups_z)
     out["tx_back"] = np.concatenate([w * cx, -w * sx], axis=1) * scale
@@ -87,14 +86,14 @@
     return jnp.concatenate([jnp.concatenate([real, imag], axis=1), lower], axis=0)
 
 
-def prepare_kernel(share, mine_ref, sat_hbm, dir_hbm, reg_hbm, main_hbm, nyq_hbm, tx_hbm, ny_hbm,
+def prepare_kernel(slots, mine_ref, sat_hbm, dir_hbm, reg_hbm, main_hbm, nyq_hbm, tx_hbm, ny_hbm,
                    send_ref, stack_ref, sat_ref, dirs, reg, main, nyq, tx, ny, rows_t, sems):
     _, half, columns = dirs.shape
-    width = 4 + share
+    width = 4 + 6 * slots
     copies = [
         pltpu.make_async_copy(reg_hbm, reg, sems.at[0]),
         pltpu.make_async_copy(dir_hbm, dirs, sems.at[1]),
-        pltpu.make_async_copy(main_hbm.at[pl.ds(mine_ref[0], share)], main, sems.at[2]),
+        pltpu.make_async_copy(main_hbm.at[:, pl.ds(mine_ref[0], slots)], main, sems.at[2]),
         pltpu.make_async_copy(tx_hbm, tx, sems.at[3]),
         pltpu.make_async_copy(ny_hbm.at[mine_ref[1]], ny, sems.at[4]),
         pltpu.make_async_copy(nyq_hbm, nyq, sems.at[5]),
@@ -131,8 +130,9 @@
         wide = [jnp.concatenate([jnp.concatenate([p, zero], 1), jnp.concatenate([zero, p], 1)], 0) for p in (high, low)]
         send_ref[pl.ds(c, columns, stride=width), :] = three(table, wide, ((1,), (1,)))
     copies[2].wait()
-    for r in range(share):
-        send_ref[pl.ds(4 + r, columns, stride=width), :] = main[r].T
+    for s in range(slots):
+        for r in range(6):
+            send_ref[pl.ds(4 + 6 * s + r, columns, stride=width), :] = main[r, s].T
     copies[4].wait()
     parts = [split(jnp.where(lane // 32 == q, sums, 0.0)) for q in range(4)]
     stacked = [jnp.concatenate([p[k] for p in parts], axis=0) for k in range(2)]
@@ -145,22 +145,22 @@
     send_ref[pl.ds(3, columns, stride=width), :] = row + rows_t[...].T
 
 
-def prepare(mine, saturation, direction, region, kernel_main, kernel_nyq, tx, ny, share):
+def prepare(mine, saturation, direction, region, kernel_main, kernel_nyq, tx, ny, slots):
     _, half, columns = direction.shape
-    rows = kernel_main.shape[1]
+    rows = kernel_main.shape[2]
     any_spec = pl.BlockSpec(memory_space=pltpu.HBM)
     smem = pl.BlockSpec(memory_space=pltpu.SMEM)
     vmem = pl.BlockSpec(memory_space=pltpu.VMEM)
 
     def body(*refs):
-        prepare_kernel(share, *refs)
+        prepare_kernel(slots, *refs)
 
     return pl.pallas_call(
         body,
         name="prepare",
         compiler_params=limits,
         out_shape=(
-            jax.ShapeDtypeStruct((columns * (4 + share), columns), f32),
+            jax.ShapeDtypeStruct((columns * (4 + 6 * slots), columns), f32),
             jax.ShapeDtypeStruct((4, half, columns), f32),
         ),
         in_specs=[smem] + [any_spec] * 7,
@@ -169,7 +169,7 @@
             pltpu.SMEM(saturation.shape, f32),
             pltpu.VMEM((3, half, columns), f32),
             pltpu.VMEM((half, columns), jnp.int32),
-            pltpu.VMEM((share, rows, columns), f32),
+            pltpu.VMEM((6, slots, rows, columns), f32),
             pltpu.VMEM(kernel_nyq.shape, f32),
             pltpu.VMEM(tx.shape, bf16),
             pltpu.VMEM(ny.shape[1:], bf16),
@@ -195,7 +195,9 @@
             imag = jnp.where(lane < 12, pltpu.roll(summed, width - 32, 1), 0.0)
         (rh, rl), (ih, il) = split(real), split(imag)
         crossed = [cross(r, i, jnp.concatenate([i, -r], axis=1)) for r, i in ((rh, ih), (rl, il))]
-        out[c] = three(table, crossed)
+        done = three(table, crossed)
+        out[c, 0] = done[:planes]
+        out[c, 1] = done[planes:]
 
 
 def forward(where, own, other, ty, tz):
@@ -206,48 +208,73 @@
         forward_kernel,
         name="forward",
         compiler_params=limits,
-        out_shape=jax.ShapeDtypeStruct((4, 2 * planes, 2 * width), f32),
+        out_shape=jax.ShapeDtypeStruct((4, 2, planes, 2 * width), f32),
         in_specs=[smem] + [vmem] * 4,
         out_specs=vmem,
     )(where, own, other, ty, tz)
 
 
-def inverse_kernel(pairs, share, where_ref, *refs):
-    spectra, row_ref, stack, ty, tz, *shares, own, other = refs
+def back(real, imag, table):
+    (rh, rl), (ih, il) = split(real), split(imag)
+    crossed = [cross(r, i, jnp.concatenate([-i, r], axis=1)) for r, i in ((rh, ih), (rl, il))]
+    return three(table, crossed)
+
+
+def field_of(kernel, spectra, slot, i):
+    width = kernel.shape[2]
+    real = imag = None
+    for j in range(3):
+        k = kernel[tensor_index[i][j]]
+        a, b = k * spectra[j, slot, :, :width], k * spectra[j, slot, :, width:]
+        real, imag = (a, b) if real is None else (real + a, imag + b)
+    return real, imag
+
+
+def first_half_kernel(where_ref, spectra, kernel, row_ref, tz, out, line_out):
     planes, width = row_ref.shape
-    table = (tz[0], tz[1])
+    slot = where_ref[0]
+    table = (tz[0, slot], tz[1, slot])
+    for i in range(3):
+        out[i] = back(*field_of(kernel, spectra, slot, i), table)
+    lane = lax.broadcasted_iota(jnp.int32, (planes, width), 1)
+    row = row_ref[...]
+    line = jnp.zeros((planes, 2 * width), f32)
+    for s in range(2):
+        k = jnp.where(lane < 12, pltpu.roll(row, width - 16 - 64 * s, 1), 0.0)
+        line = line + back(spectra[3, s, :, :width] * k, spectra[3, s, :, width:] * k, (tz[0, s], tz[1, s]))
+    line = line[:, :width] + pltpu.roll(line[:, width:], 32, 1)
+    line_out[...] = jnp.where(where_ref[1] == 0, line, pltpu.roll(line, 64, 1))
+
+
+def first_half(where, spectra, kernel, row, tz):
+    planes, width = row.shape
+    smem = pl.BlockSpec(memory_space=pltpu.SMEM)
+    vmem = pl.BlockSpec(memory_space=pltpu.VMEM)
+    return pl.pallas_call(
+        first_half_kernel,
+        name="first_half",
+        compiler_params=limits,
+        out_shape=(
+            jax.ShapeDtypeStruct((3, planes, 2 * width), f32),
+            jax.ShapeDtypeStruct((planes, width), f32),
+        ),
+        in_specs=[smem] + [vmem] * 4,
+        out_specs=(vmem, vmem),
+    )(where, spectra, kernel, row, tz)
+
+
+def second_half_kernel(where_ref, spectra, kernel, ready, line_ref, stack, tz, ty, own, other):
+    planes, width = line_ref.shape
+    slot = 1 - where_ref[0]
+    table = (tz[0, slot], tz[1, slot])
     y_table = (ty[0, where_ref[1]], ty[1, where_ref[1]])
-
-    def kernel_row(c):
-        owner, at = c // share, c % share
-        if pairs == 1:
-            return shares[0][at]
-        return jnp.where(where_ref[2] == owner, shares[0][at], shares[1][at])
-
-    def back(real, imag):
-        (rh, rl), (ih, il) = split(real), split(imag)
-        crossed = [cross(r, i, jnp.concatenate([-i, r], axis=1)) for r, i in ((rh, ih), (rl, il))]
-        return three(table, crossed)
-
-    kernel = [jnp.concatenate([kernel_row(2 * t), kernel_row(2 * t + 1)], axis=0) for t in range(6)]
     for i in range(3):
-        real = imag = None
-        for j in range(3):
-            k = kernel[tensor_index[i][j]]
-            a, b = k * spectra[j, :, :width], k * spectra[j, :, width:]
-            real, imag = (a, b) if real is None else (real + a, imag + b)
-        lines = three(split(back(real, imag)), y_table)
+        lines = ready[i] + back(*field_of(kernel, spectra, slot, i), table)
+        lines = three(split(lines), y_table)
         own[pl.ds(i, planes, stride=4), :] = lines[:, :width]
         other[pl.ds(i, planes, stride=4), :] = lines[:, width:]
-    lane = lax.broadcasted_iota(jnp.int32, (planes, width), 1)
-    row = row_ref[...]
-    k = jnp.concatenate([pltpu.roll(row, width - 16, 1), pltpu.roll(row, width - 80, 1)], axis=0)
-    k = jnp.where(jnp.concatenate([lane, lane], axis=0) < 12, k, 0.0)
-    line = back(spectra[3, :, :width] * k, spectra[3, :, width:] * k)
-    line = line[:, :width] + pltpu.roll(line[:, width:], 32, 1)
-    line = jnp.where(where_ref[1] == 0, line, pltpu.roll(line, 64, 1))
-    own[pl.ds(3, planes, stride=4), :] = line
-    other[pl.ds(3, planes, stride=4), :] = line
+    own[pl.ds(3, planes, stride=4), :] = line_ref[...]
+    other[pl.ds(3, planes, stride=4), :] = line_ref[...]
     last = stack.shape[1] - 1
     for c in range(4):
         edge = jnp.where(where_ref[1] == 0, stack[c, last:], stack[c, :1])
@@ -255,24 +282,21 @@
         other[4 * planes + 4 + c : 4 * planes + 5 + c, :] = edge
 
 
-def inverse(where, spectra, row, stacked, ty, tz, shares, share):
-    planes, width = row.shape
+def second_half(where, spectra, kernel, ready, line, stacked, tz, ty):
+    planes, width = line.shape
     smem = pl.BlockSpec(memory_space=pltpu.SMEM)
     vmem = pl.BlockSpec(memory_space=pltpu.VMEM)
-    pairs = len(shares)
-
-    def body(*refs):
-        inverse_kernel(pairs, share, *refs)
-
-    shape = lambda rows: jax.ShapeDtypeStruct((rows, width), f32)
     return pl.pallas_call(
-        body,
-        name="inverse",
+        second_half_kernel,
+        name="second_half",
         compiler_params=limits,
-        out_shape=(shape(4 * planes), shape(4 * planes + 8)),
-        in_specs=[smem] + [vmem] * (5 + pairs),
+        out_shape=(
+            jax.ShapeDtypeStruct((4 * planes, width), f32),
+            jax.ShapeDtypeStruct((4 * planes + 8, width), f32),
+        ),
+        in_specs=[smem] + [vmem] * 7,
         out_specs=(vmem, vmem),
-    )(where, spectra, row, stacked, ty, tz, *shares)
+    )(where, spectra, kernel, ready, line, stacked, tz, ty)
 
 
 def finish_kernel(where_ref, recv, arrived, stack, before, after, tx, ny, out):
@@ -328,34 +352,37 @@
     y_index = lax.axis_index("gy")
     part = lax.axis_index("parts")
     pairs = 2 if parts % 2 == 0 else 1
-    share = components // pairs
+    slots = 2 // pairs
     t = tables(columns, rows, groups_z)
     direction = direction[:, 0]
-    where = jnp.stack([part % pairs * share, y_index, part % pairs])
+    where = jnp.stack([part % pairs, y_index])
     send, stacked = prepare(
-        where, saturation, direction, region[0], kernel_main.reshape(components, rows, columns), kernel_nyq,
-        halves(t["tx"]), halves(t["ny"]).swapaxes(0, 1), share,
+        where, saturation, direction, region[0], kernel_main, kernel_nyq,
+        halves(t["tx"]), halves(t["ny"]).swapaxes(0, 1), slots,
     )
-    width = 4 + share
+    width = 4 + 6 * slots
     recv = lax.all_to_all(send.reshape(columns, width // 2, 2, columns), "gz", 0, 0, tiled=True)
     recv = recv.reshape(columns, width, columns).transpose(1, 0, 2)
-    shares = [recv[4:]]
+    kernel = recv[4:10]
     if pairs == 2:
-        shares.append(lax.ppermute(shares[0], "parts", [(p, p ^ 1) for p in range(parts)]))
+        kernel_other = lax.ppermute(kernel, "parts", [(p, p ^ 1) for p in range(parts)])
+    else:
+        kernel_other = recv[10:]
     own_m = recv[:4]
     other_m = lax.ppermute(own_m, "gy", swap)
-    up = [(i, i + 1) for i in range(groups_z - 1)]
-    down = [(b, a) for a, b in up]
-    before = lax.ppermute(stacked, "gz", up)
-    after = lax.ppermute(stacked, "gz", down)
+    tz_back = halves(t["tz_back"])
     spectra = forward(where, own_m, other_m, halves(t["ty"]), halves(t["tz"]))
-    own, other = inverse(
-        where, spectra, own_m[3], stacked, halves(t["ty_back"]), halves(t["tz_back"]), shares, share
-    )
+    ready, line = first_half(where, spectra, kernel, own_m[3], tz_back)
+    own, other = second_half(where, spectra, kernel_other, ready, line, stacked, tz_back, halves(t["ty_back"]))
     arrived = lax.ppermute(other, "gy", swap)
     send_f = own + arrived[: 4 * groups_z]
     recv_f = lax.all_to_all(send_f.reshape(groups_z, 4, columns), "gz", 0, 0, tiled=True)
     recv_f = recv_f.reshape(4 * columns, columns)
+    up = [(i, i + 1) for i in range(groups_z - 1)]
+    down = [(b, a) for a, b in up]
+    edge_planes, _ = lax.optimization_barrier((stacked, send_f))
+    before = lax.ppermute(edge_planes, "gz", up)
+    after = lax.ppermute(edge_planes, "gz", down)
     tx_back, ny_back = halves(t["tx_back"]), halves(t["ny_back"])
     return finish(where, recv_f, arrived, stacked, before, after, tx_back, ny_back)[:, None]
 

time: 148 us -> 147 us (level)
  starting transfers between devices: 29.7 us -> 27.8 us
  transfers between devices with their start and end apart: 6 -> 6, of which waited for: 5 -> 5; matrix products, arithmetic and copies ran while one was open for 0% -> 0% of each run, Pallas kernels for 1% -> 2%
where the time goes in v4:
time: 147 us; the launch traced here: 146 us
  blocking collectives  89.7 us (61%)
  starting transfers between devices  27.8 us (19%)
  waiting for transfers between devices  19.4 us (13%)
  Pallas kernels  8.18 us (6%)
    all_to_all x1, blocking collectives, local(): lax.all_to_all(send.reshape(columns, width // 2, 2, columns), 'gz', 0, 0,...  89.7 us
    all_to_all x1, starting transfers between devices, local(): lax.all_to_all(send_f.reshape(groups_z, 4, columns), 'gz', 0, 0, tiled=True)  12.4 us
    all_to_all x1, waiting for transfers between devices, local(): lax.all_to_all(send_f.reshape(groups_z, 4, columns), 'gz', 0, 0, tiled=True)  7.92 us
    ppermute x1, waiting for transfers between devices, local(): after = lax.ppermute(edge_planes, 'gz', down)  6.89 us
    ppermute x1, starting transfers between devices, local(): lax.ppermute(kernel, 'parts', [(p, p ^ 1) for p in range(parts)])  4.83 us
    ppermute x1, starting transfers between devices, local(): after = lax.ppermute(edge_planes, 'gz', down)  4.61 us
  transfers between devices with their start and end apart: 6, of which 5 were waited for; matrix products, arithmetic and copies ran while one was open for 0% of the time, Pallas kernels for 2%

profile of v4, /device:TPU:66, one launch (start us, length us, event | category | flops | bytes accessed | tf_op | source)
XLA Modules:
  0.0 146.2 jit_solution(18431676018327635414)
XLA Ops:
  0.0 0.1 pad_add_fusion.refs_0_.where_ref
  0.1 2.6 %prepare.1 = (f32[1280,128]{1,0:T(8,128)S(1)}, f32[4,64,128]{2,1,0:T(8,128)S(1)}) custom-call(s32[2]{0:T(128)S(1)} %pad_add_fusion.refs_0_.where_ref, f32[3]{0:T(128)} %refs_1_.1, f32[3,64,128]{2,1,0:T(8,128)} %bitcast.20, s32[64,128]{1,0:T(8,128)} %bitcast.21, f32[6,2,128,128]{3,2,1,0:T(8,128)} %refs_4_.1, f32[6,2,128]{2,1,0:T(2,128)} %refs_5_.1, ...), custom_call_target="tpu_custom_call" | custom-call | tf_op jit(solution)/shard_map/prepare/pallas_call | solution.py:158
  2.7 89.7 %all_to_all.10 = f32[128,5,2,128]{3,2,1,0:T(2,128)S(1)} all-to-all(f32[128,5,2,128]{3,2,1,0:T(2,128)S(1)} %bitcast.16), channel_id=1, replica_groups=mesh['parts'=2,'gz'=128,'gy'=2] {'gz'}, dimensions={0} | all-to-all | bytes 1310720 | tf_op jit(solution)/shard_map/all_to_all | solution.py:364
  92.4 0.0 copy-start.4
  92.5 0.0 copy-start.1
  92.5 4.8 %collective-permute-start.1 = (f32[6,128,128]{2,1,0:T(8,128)S(1)}, f32[6,128,128]{2,1,0:T(8,128)S(1)}, u32[]{:S(2)}, u32[]{:S(2)}) collective-permute-start(f32[6,128,128]{2,1,0:T(8,128)S(1)} %slice.18.kernel), channel_id=1, source_target_pairs={{0,256},{256,0},{1,257},{257,1},{2,258},{258,2},{3,259},{259,3},{4... | collective-permute-start | bytes 1179656 | tf_op jit(solution)/shard_map/ppermute | solution.py:368
  97.4 2.0 %collective-permute-start = (f32[4,128,128]{2,1,0:T(8,128)S(1)}, f32[4,128,128]{2,1,0:T(8,128)S(1)}, u32[]{:S(2)}, u32[]{:S(2)}) collective-permute-start(f32[4,128,128]{2,1,0:T(8,128)S(1)} %slice.17.own), channel_id=1, source_target_pairs={{0,1},{1,0},{2,3},{3,2},{4,5},{5,4},{6,7},{7,6},{8,9},{9,8},{10,11... | collective-permute-start | bytes 786440 | tf_op jit(solution)/shard_map/ppermute | solution.py:372
  99.3 0.0 copy-start
  99.3 1.5 %collective-permute-done.other = f32[4,128,128]{2,1,0:T(8,128)S(1)} collective-permute-done((f32[4,128,128]{2,1,0:T(8,128)S(1)}, f32[4,128,128]{2,1,0:T(8,128)S(1)}, u32[]{:S(2)}, u32[]{:S(2)}) %collective-permute-start) | collective-permute-done | bytes 262176 | tf_op jit(solution)/shard_map/ppermute | solution.py:372
  100.8 0.0 copy-done.4
  100.8 0.0 copy-done.1
  100.8 1.6 %forward.1.spectra = f32[4,2,128,256]{3,2,1,0:T(8,128)S(1)} custom-call(s32[2]{0:T(128)S(1)} %pad_add_fusion.refs_0_.where_ref, f32[4,128,128]{2,1,0:T(8,128)S(1)} %slice.17.own, f32[4,128,128]{2,1,0:T(8,128)S(1)} %collective-permute-done.other, bf16[2,2,256,256]{3,2,1,0:T(8,128)(2,1)S(1)} %copy-done.1, bf16[2,256,256]{2,1,0:T(8,128)(2,1)S(1)} %copy-done.4), custom_call_target="tpu_custom_call" | custom-call | tf_op jit(solution)/shard_map/forward/pallas_call | solution.py:207
  102.5 0.0 copy-done
  102.5 0.0 copy-start.2
  102.5 1.2 first_half.1
  103.7 0.0 collective-permute-done.1.kernel
  103.7 0.0 copy-done.2
  103.7 1.2 second_half.1
  104.9 2.1 %collective-permute-start.2 = (f32[520,128]{1,0:T(8,128)S(1)}, f32[520,128]{1,0:T(8,128)S(1)}, u32[]{:S(2)}, u32[]{:S(2)}) collective-permute-start(f32[520,128]{1,0:T(8,128)S(1)} %get-tuple-element.17), channel_id=1, source_target_pairs={{0,1},{1,0},{2,3},{3,2},{4,5},{5,4},{6,7},{7,6},{8,9},{9,8},{10,11... | collective-permute-start | bytes 798728 | tf_op jit(solution)/shard_map/ppermute | solution.py:377
  107.0 1.4 collective-permute-done.2.arrived
  108.4 0.7 slice_add_fusion
  109.1 0.0 copy-start.3
  109.1 0.0 copy-start.5
  109.1 12.4 %all-to-all-start.1 = ((f32[128,4,128]{2,1,0:T(4,128)}), f32[128,4,128]{2,1,0:T(4,128)S(1)}, u32[]{:S(2)}, u32[]{:S(2)}) async-start(f32[128,4,128]{2,1,0:T(4,128)} %bitcast.9), calls=%async_computation.1 | async-start | bytes 524288 | tf_op jit(solution)/shard_map/all_to_all | solution.py:379
  121.6 4.6 %collective-permute-start.4 = (f32[4,64,128]{2,1,0:T(8,128)S(1)}, f32[4,64,128]{2,1,0:T(8,128)S(1)}, u32[]{:S(2)}, u32[]{:S(2)}) collective-permute-start(f32[4,64,128]{2,1,0:T(8,128)S(1)} %get-tuple-element.18.stack), channel_id=1, source_target_pairs={{2,0},{4,2},{6,4},{8,6},{10,8},{12,10},{14,12},{16,14},{18,16},{20... | collective-permute-start | bytes 393224 | tf_op jit(solution)/shard_map/ppermute | solution.py:385
  126.2 2.0 %collective-permute-start.3 = (f32[4,64,128]{2,1,0:T(8,128)S(1)}, f32[4,64,128]{2,1,0:T(8,128)S(1)}, u32[]{:S(2)}, u32[]{:S(2)}) collective-permute-start(f32[4,64,128]{2,1,0:T(8,128)S(1)} %get-tuple-element.18.stack), channel_id=1, source_target_pairs={{0,2},{2,4},{4,6},{6,8},{8,10},{10,12},{12,14},{14,16},{16,18},{18... | collective-permute-start | bytes 393224 | tf_op jit(solution)/shard_map/ppermute | solution.py:384
  128.1 6.9 %collective-permute-done.4.after = f32[4,64,128]{2,1,0:T(8,128)S(1)} collective-permute-done((f32[4,64,128]{2,1,0:T(8,128)S(1)}, f32[4,64,128]{2,1,0:T(8,128)S(1)}, u32[]{:S(2)}, u32[]{:S(2)}) %collective-permute-start.4) | collective-permute-done | bytes 131104 | tf_op jit(solution)/shard_map/ppermute | solution.py:385
  135.0 1.7 %collective-permute-done.3.before = f32[4,64,128]{2,1,0:T(8,128)S(1)} collective-permute-done((f32[4,64,128]{2,1,0:T(8,128)S(1)}, f32[4,64,128]{2,1,0:T(8,128)S(1)}, u32[]{:S(2)}, u32[]{:S(2)}) %collective-permute-start.3) | collective-permute-done | bytes 131104 | tf_op jit(solution)/shard_map/ppermute | solution.py:384
  136.7 7.9 %all-to-all-done.1 = f32[128,4,128]{2,1,0:T(4,128)S(1)} async-done(((f32[128,4,128]{2,1,0:T(4,128)}), f32[128,4,128]{2,1,0:T(4,128)S(1)}, u32[]{:S(2)}, u32[]{:S(2)}) %all-to-all-start.1) | async-done | bytes 262176 | tf_op jit(solution)/shard_map/all_to_all | solution.py:379
  144.7 0.0 copy-done.3
  144.7 0.0 copy-done.5
  144.7 1.6 %finish.1 = f32[3,64,128]{2,1,0:T(8,128)} custom-call(s32[2]{0:T(128)S(1)} %pad_add_fusion.refs_0_.where_ref, f32[512,128]{1,0:T(8,128)S(1)} %bitcast.15, f32[520,128]{1,0:T(8,128)S(1)} %collective-permute-done.2.arrived, f32[4,64,128]{2,1,0:T(8,128)S(1)} %get-tuple-element.18.stack, f32[4,64,128]{2,1,0:T(8,128)S(1)} %collective-permute-done.3.before, ...), custom_call_target="tpu_custom_call" | custom-call | tf_op jit(solution)/shard_map/finish/pallas_call | solution.py:336
  (4 shorter events, 0.1 us)
Async XLA Ops:
  92.4 8.4 %copy-start.4 = (bf16[2,256,256]{2,1,0:T(8,128)(2,1)S(1)}, bf16[2,256,256]{2,1,0:T(8,128)(2,1)}, u32[]{:S(2)}) copy-start(bf16[2,256,256]{2,1,0:T(8,128)(2,1)} %constant.41.clone.tz) | copy-start | bytes 786436
  92.5 8.3 %copy-start.1 = (bf16[2,2,256,256]{3,2,1,0:T(8,128)(2,1)S(1)}, bf16[2,2,256,256]{3,2,1,0:T(8,128)(2,1)}, u32[]{:S(2)}) copy-start(bf16[2,2,256,256]{3,2,1,0:T(8,128)(2,1)} %constant.40.clone.ty) | copy-start | bytes 1572868
  92.5 11.2 %collective-permute-start.1 = (f32[6,128,128]{2,1,0:T(8,128)S(1)}, f32[6,128,128]{2,1,0:T(8,128)S(1)}, u32[]{:S(2)}, u32[]{:S(2)}) collective-permute-start(f32[6,128,128]{2,1,0:T(8,128)S(1)} %slice.18.kernel), channel_id=1, source_target_pairs={{0,256},{256,0},{1,257},{257,1},{2,258},{258,2},{3,259},{259,3},{4... | collective-permute-start | bytes 1179656 | tf_op jit(solution)/shard_map/ppermute | solution.py:368
  97.4 3.5 %collective-permute-start = (f32[4,128,128]{2,1,0:T(8,128)S(1)}, f32[4,128,128]{2,1,0:T(8,128)S(1)}, u32[]{:S(2)}, u32[]{:S(2)}) collective-permute-start(f32[4,128,128]{2,1,0:T(8,128)S(1)} %slice.17.own), channel_id=1, source_target_pairs={{0,1},{1,0},{2,3},{3,2},{4,5},{5,4},{6,7},{7,6},{8,9},{9,8},{10,11... | collective-permute-start | bytes 786440 | tf_op jit(solution)/shard_map/ppermute | solution.py:372
  99.3 3.1 %copy-start = (bf16[2,2,128,256]{3,2,1,0:T(8,128)(2,1)S(1)}, bf16[2,2,128,256]{3,2,1,0:T(8,128)(2,1)}, u32[]{:S(2)}) copy-start(bf16[2,2,128,256]{3,2,1,0:T(8,128)(2,1)} %constant.39.clone.tz) | copy-start | bytes 786436
  102.5 1.2 copy-start.2
  104.9 3.5 %collective-permute-start.2 = (f32[520,128]{1,0:T(8,128)S(1)}, f32[520,128]{1,0:T(8,128)S(1)}, u32[]{:S(2)}, u32[]{:S(2)}) collective-permute-start(f32[520,128]{1,0:T(8,128)S(1)} %get-tuple-element.17), channel_id=1, source_target_pairs={{0,1},{1,0},{2,3},{3,2},{4,5},{5,4},{6,7},{7,6},{8,9},{9,8},{10,11... | collective-permute-start | bytes 798728 | tf_op jit(solution)/shard_map/ppermute | solution.py:377
  109.1 35.5 %copy-start.3 = (bf16[2,2,256,128]{3,2,1,0:T(8,128)(2,1)S(1)}, bf16[2,2,256,128]{3,2,1,0:T(8,128)(2,1)}, u32[]{:S(2)}) copy-start(bf16[2,2,256,128]{3,2,1,0:T(8,128)(2,1)} %constant.44.clone.ny) | copy-start | bytes 786436
  109.1 35.5 %copy-start.5 = (bf16[2,128,256]{2,1,0:T(8,128)(2,1)S(1)}, bf16[2,128,256]{2,1,0:T(8,128)(2,1)}, u32[]{:S(2)}) copy-start(bf16[2,128,256]{2,1,0:T(8,128)(2,1)} %constant.43.clone.tx) | copy-start | bytes 393220
  109.1 35.5 %all-to-all-start.1 = ((f32[128,4,128]{2,1,0:T(4,128)}), f32[128,4,128]{2,1,0:T(4,128)S(1)}, u32[]{:S(2)}, u32[]{:S(2)}) async-start(f32[128,4,128]{2,1,0:T(4,128)} %bitcast.9), calls=%async_computation.1 | async-start | bytes 524288 | tf_op jit(solution)/shard_map/all_to_all | solution.py:379
  121.6 13.5 %collective-permute-start.4 = (f32[4,64,128]{2,1,0:T(8,128)S(1)}, f32[4,64,128]{2,1,0:T(8,128)S(1)}, u32[]{:S(2)}, u32[]{:S(2)}) collective-permute-start(f32[4,64,128]{2,1,0:T(8,128)S(1)} %get-tuple-element.18.stack), channel_id=1, source_target_pairs={{2,0},{4,2},{6,4},{8,6},{10,8},{12,10},{14,12},{16,14},{18,16},{20... | collective-permute-start | bytes 393224 | tf_op jit(solution)/shard_map/ppermute | solution.py:385
  126.2 10.6 %collective-permute-start.3 = (f32[4,64,128]{2,1,0:T(8,128)S(1)}, f32[4,64,128]{2,1,0:T(8,128)S(1)}, u32[]{:S(2)}, u32[]{:S(2)}) collective-permute-start(f32[4,64,128]{2,1,0:T(8,128)S(1)} %get-tuple-element.18.stack), channel_id=1, source_target_pairs={{0,2},{2,4},{4,6},{6,8},{8,10},{10,12},{12,14},{14,16},{16,18},{18... | collective-permute-start | bytes 393224 | tf_op jit(solution)/shard_map/ppermute | solution.py:384

commit v5 on v4

--- a/solution.py
+++ b/solution.py
@@ -1,3 +1,5 @@
+import functools
+
 import jax
 import jax.numpy as jnp
 import numpy as np
@@ -86,16 +88,21 @@
     return jnp.concatenate([jnp.concatenate([real, imag], axis=1), lower], axis=0)
 
 
-def prepare_kernel(slots, mine_ref, sat_hbm, dir_hbm, reg_hbm, main_hbm, nyq_hbm, tx_hbm, ny_hbm,
+def place(axis, count):
+    return lax.rem(lax.axis_index(axis), count)
+
+
+def prepare_kernel(slots, sat_hbm, dir_hbm, reg_hbm, main_hbm, nyq_hbm, tx_hbm, ny_hbm,
                    send_ref, stack_ref, sat_ref, dirs, reg, main, nyq, tx, ny, rows_t, sems):
     _, half, columns = dirs.shape
     width = 4 + 6 * slots
+    slot = place("parts", 2 // slots)
     copies = [
         pltpu.make_async_copy(reg_hbm, reg, sems.at[0]),
         pltpu.make_async_copy(dir_hbm, dirs, sems.at[1]),
-        pltpu.make_async_copy(main_hbm.at[:, pl.ds(mine_ref[0], slots)], main, sems.at[2]),
+        pltpu.make_async_copy(main_hbm.at[:, pl.ds(slot, slots)], main, sems.at[2]),
         pltpu.make_async_copy(tx_hbm, tx, sems.at[3]),
-        pltpu.make_async_copy(ny_hbm.at[mine_ref[1]], ny, sems.at[4]),
+        pltpu.make_async_copy(ny_hbm.at[place("gy", 2)], ny, sems.at[4]),
         pltpu.make_async_copy(nyq_hbm, nyq, sems.at[5]),
         pltpu.make_async_copy(sat_hbm, sat_ref, sems.at[6]),
     ]
@@ -145,25 +152,21 @@
     send_ref[pl.ds(3, columns, stride=width), :] = row + rows_t[...].T
 
 
-def prepare(mine, saturation, direction, region, kernel_main, kernel_nyq, tx, ny, slots):
+def prepare(saturation, direction, region, kernel_main, kernel_nyq, tx, ny, slots):
     _, half, columns = direction.shape
     rows = kernel_main.shape[2]
     any_spec = pl.BlockSpec(memory_space=pltpu.HBM)
-    smem = pl.BlockSpec(memory_space=pltpu.SMEM)
     vmem = pl.BlockSpec(memory_space=pltpu.VMEM)
 
-    def body(*refs):
-        prepare_kernel(slots, *refs)
-
     return pl.pallas_call(
-        body,
+        functools.partial(prepare_kernel, slots),
         name="prepare",
         compiler_params=limits,
         out_shape=(
             jax.ShapeDtypeStruct((columns * (4 + 6 * slots), columns), f32),
             jax.ShapeDtypeStruct((4, half, columns), f32),
         ),
-        in_specs=[smem] + [any_spec] * 7,
+        in_specs=[any_spec] * 7,
         out_specs=(vmem, vmem),
         scratch_shapes=[
             pltpu.SMEM(saturation.shape, f32),
@@ -176,13 +179,14 @@
             pltpu.VMEM((columns, columns), f32),
             pltpu.SemaphoreType.DMA((7,)),
         ],
-    )(mine, *(pltpu.with_memory_space_constraint(a, pltpu.HBM) for a in (saturation, direction, region, kernel_main, kernel_nyq, tx, ny)))
-
-
-def forward_kernel(where_ref, own, other, ty, tz, out):
+    )(*(pltpu.with_memory_space_constraint(a, pltpu.HBM) for a in (saturation, direction, region, kernel_main, kernel_nyq, tx, ny)))
+
+
+def forward_kernel(own, other, ty, tz, out):
     planes, width = own.shape[1:]
+    gy = place("gy", 2)
     table = (tz[0], tz[1])
-    y_table = (ty[0, where_ref[1]], ty[1, where_ref[1]])
+    y_table = (ty[0, gy], ty[1, gy])
     for c in range(4):
         if c < 3:
             ready = three(split(jnp.concatenate([own[c], other[c]], axis=1)), y_table)
@@ -190,7 +194,7 @@
         else:
             lane = lax.broadcasted_iota(jnp.int32, (planes, width), 1)
             summed = own[3] + other[3]
-            summed = jnp.where(where_ref[1] == 0, summed, pltpu.roll(summed, 64, 1))
+            summed = jnp.where(place("gy", 2) == 0, summed, pltpu.roll(summed, 64, 1))
             real = jnp.where(lane < 12, summed, 0.0)
             imag = jnp.where(lane < 12, pltpu.roll(summed, width - 32, 1), 0.0)
         (rh, rl), (ih, il) = split(real), split(imag)
@@ -200,18 +204,17 @@
         out[c, 1] = done[planes:]
 
 
-def forward(where, own, other, ty, tz):
+def forward(own, other, ty, tz):
     planes, width = own.shape[1:]
-    smem = pl.BlockSpec(memory_space=pltpu.SMEM)
     vmem = pl.BlockSpec(memory_space=pltpu.VMEM)
     return pl.pallas_call(
         forward_kernel,
         name="forward",
         compiler_params=limits,
         out_shape=jax.ShapeDtypeStruct((4, 2, planes, 2 * width), f32),
-        in_specs=[smem] + [vmem] * 4,
+        in_specs=[vmem] * 4,
         out_specs=vmem,
-    )(where, own, other, ty, tz)
+    )(own, other, ty, tz)
 
 
 def back(real, imag, table):
@@ -230,9 +233,9 @@
     return real, imag
 
 
-def first_half_kernel(where_ref, spectra, kernel, row_ref, tz, out, line_out):
+def first_half_kernel(pairs, spectra, kernel, row_ref, tz, out, line_out):
     planes, width = row_ref.shape
-    slot = where_ref[0]
+    slot = place("parts", pairs)
     table = (tz[0, slot], tz[1, slot])
     for i in range(3):
         out[i] = back(*field_of(kernel, spectra, slot, i), table)
@@ -243,31 +246,31 @@
         k = jnp.where(lane < 12, pltpu.roll(row, width - 16 - 64 * s, 1), 0.0)
         line = line + back(spectra[3, s, :, :width] * k, spectra[3, s, :, width:] * k, (tz[0, s], tz[1, s]))
     line = line[:, :width] + pltpu.roll(line[:, width:], 32, 1)
-    line_out[...] = jnp.where(where_ref[1] == 0, line, pltpu.roll(line, 64, 1))
-
-
-def first_half(where, spectra, kernel, row, tz):
+    line_out[...] = jnp.where(place("gy", 2) == 0, line, pltpu.roll(line, 64, 1))
+
+
+def first_half(pairs, spectra, kernel, row, tz):
     planes, width = row.shape
-    smem = pl.BlockSpec(memory_space=pltpu.SMEM)
     vmem = pl.BlockSpec(memory_space=pltpu.VMEM)
     return pl.pallas_call(
-        first_half_kernel,
+        functools.partial(first_half_kernel, pairs),
         name="first_half",
         compiler_params=limits,
         out_shape=(
             jax.ShapeDtypeStruct((3, planes, 2 * width), f32),
             jax.ShapeDtypeStruct((planes, width), f32),
         ),
-        in_specs=[smem] + [vmem] * 4,
+        in_specs=[vmem] * 4,
         out_specs=(vmem, vmem),
-    )(where, spectra, kernel, row, tz)
-
-
-def second_half_kernel(where_ref, spectra, kernel, ready, line_ref, stack, tz, ty, own, other):
+    )(spectra, kernel, row, tz)
+
+
+def second_half_kernel(pairs, spectra, kernel, ready, line_ref, stack, tz, ty, own, other):
     planes, width = line_ref.shape
-    slot = 1 - where_ref[0]
+    slot = 1 - place("parts", pairs)
+    gy = place("gy", 2)
     table = (tz[0, slot], tz[1, slot])
-    y_table = (ty[0, where_ref[1]], ty[1, where_ref[1]])
+    y_table = (ty[0, gy], ty[1, gy])
     for i in range(3):
         lines = ready[i] + back(*field_of(kernel, spectra, slot, i), table)
         lines = three(split(lines), y_table)
@@ -277,34 +280,34 @@
     other[pl.ds(3, planes, stride=4), :] = line_ref[...]
     last = stack.shape[1] - 1
     for c in range(4):
-        edge = jnp.where(where_ref[1] == 0, stack[c, last:], stack[c, :1])
+        edge = jnp.where(place("gy", 2) == 0, stack[c, last:], stack[c, :1])
         other[4 * planes + c : 4 * planes + c + 1, :] = edge
         other[4 * planes + 4 + c : 4 * planes + 5 + c, :] = edge
 
 
-def second_half(where, spectra, kernel, ready, line, stacked, tz, ty):
+def second_half(pairs, spectra, kernel, ready, line, stacked, tz, ty):
     planes, width = line.shape
-    smem = pl.BlockSpec(memory_space=pltpu.SMEM)
     vmem = pl.BlockSpec(memory_space=pltpu.VMEM)
     return pl.pallas_call(
-        second_half_kernel,
+        functools.partial(second_half_kernel, pairs),
         name="second_half",
         compiler_params=limits,
         out_shape=(
             jax.ShapeDtypeStruct((4 * planes, width), f32),
             jax.ShapeDtypeStruct((4 * planes + 8, width), f32),
         ),
-        in_specs=[smem] + [vmem] * 7,
+        in_specs=[vmem] * 7,
         out_specs=(vmem, vmem),
-    )(where, spectra, kernel, ready, line, stacked, tz, ty)
-
-
-def finish_kernel(where_ref, recv, arrived, stack, before, after, tx, ny, out):
+    )(spectra, kernel, ready, line, stacked, tz, ty)
+
+
+def finish_kernel(recv, arrived, stack, before, after, tx, ny, out):
     _, half, columns = stack.shape
     lane = lax.broadcasted_iota(jnp.int32, (half, columns), 1)
     line = lax.broadcasted_iota(jnp.int32, (half, columns), 0)
     signs = (1 - 2 * (lane % 2)).astype(f32)
-    lower = where_ref[1] == 0
+    gy = place("gy", 2)
+    lower = gy == 0
 
     def near(c):
         one = stack[c]
@@ -317,7 +320,7 @@
 
     count = near(3)
     magnetic = stack[3]
-    nyquist = three((ny[0, where_ref[1]], ny[1, where_ref[1]]), split(recv[pl.ds(3, columns, stride=4), :]))
+    nyquist = three((ny[0, gy], ny[1, gy]), split(recv[pl.ds(3, columns, stride=4), :]))
     sums = jnp.zeros((half, columns), f32)
     for q in range(4):
         sums = jnp.where(lane // 32 == q, nyquist[q * half : (q + 1) * half], sums)
@@ -330,17 +333,16 @@
         out[c] = demag + total * signs + exchange
 
 
-def finish(where, recv, arrived, stacked, before, after, tx, ny):
-    smem = pl.BlockSpec(memory_space=pltpu.SMEM)
+def finish(recv, arrived, stacked, before, after, tx, ny):
     vmem = pl.BlockSpec(memory_space=pltpu.VMEM)
     return pl.pallas_call(
         finish_kernel,
         name="finish",
         compiler_params=limits,
         out_shape=jax.ShapeDtypeStruct((3,) + stacked.shape[1:], f32),
-        in_specs=[smem] + [vmem] * 7,
+        in_specs=[vmem] * 7,
         out_specs=vmem,
-    )(where, recv, arrived, stacked, before, after, tx, ny)
+    )(recv, arrived, stacked, before, after, tx, ny)
 
 
 def local(direction, region, saturation, kernel_main, kernel_nyq):
@@ -349,18 +351,19 @@
     groups_z = lax.axis_size("gz")
     rows = half * lax.axis_size("gy")
     parts = lax.axis_size("parts")
-    y_index = lax.axis_index("gy")
-    part = lax.axis_index("parts")
     pairs = 2 if parts % 2 == 0 else 1
     slots = 2 // pairs
     t = tables(columns, rows, groups_z)
     direction = direction[:, 0]
-    where = jnp.stack([part % pairs, y_index])
     send, stacked = prepare(
-        where, saturation, direction, region[0], kernel_main, kernel_nyq,
+        saturation, direction, region[0], kernel_main, kernel_nyq,
         halves(t["tx"]), halves(t["ny"]).swapaxes(0, 1), slots,
     )
     width = 4 + 6 * slots
+    up = [(i, i + 1) for i in range(groups_z - 1)]
+    down = [(b, a) for a, b in up]
+    before = lax.ppermute(stacked, "gz", up)
+    after = lax.ppermute(stacked, "gz", down)
     recv = lax.all_to_all(send.reshape(columns, width // 2, 2, columns), "gz", 0, 0, tiled=True)
     recv = recv.reshape(columns, width, columns).transpose(1, 0, 2)
     kernel = recv[4:10]
@@ -371,20 +374,16 @@
     own_m = recv[:4]
     other_m = lax.ppermute(own_m, "gy", swap)
     tz_back = halves(t["tz_back"])
-    spectra = forward(where, own_m, other_m, halves(t["ty"]), halves(t["tz"]))
-    ready, line = first_half(where, spectra, kernel, own_m[3], tz_back)
-    own, other = second_half(where, spectra, kernel_other, ready, line, stacked, tz_back, halves(t["ty_back"]))
+    spectra = forward(own_m, other_m, halves(t["ty"]), halves(t["tz"]))
+    ready, line = first_half(pairs, spectra, kernel, own_m[3], tz_back)
+    own, other = second_half(pairs, spectra, kernel_other, ready, line, stacked, tz_back, halves(t["ty_back"]))
+    other, before, after = lax.optimization_barrier((other, before, after))
     arrived = lax.ppermute(other, "gy", swap)
     send_f = own + arrived[: 4 * groups_z]
     recv_f = lax.all_to_all(send_f.reshape(groups_z, 4, columns), "gz", 0, 0, tiled=True)
     recv_f = recv_f.reshape(4 * columns, columns)
-    up = [(i, i + 1) for i in range(groups_z - 1)]
-    down = [(b, a) for a, b in up]
-    edge_planes, _ = lax.optimization_barrier((stacked, send_f))
-    before = lax.ppermute(edge_planes, "gz", up)
-    after = lax.ppermute(edge_planes, "gz", down)
     tx_back, ny_back = halves(t["tx_back"]), halves(t["ny_back"])
-    return finish(where, recv_f, arrived, stacked, before, after, tx_back, ny_back)[:, None]
+    return finish(recv_f, arrived, stacked, before, after, tx_back, ny_back)[:, None]
 
 
 def solution(mesh):

time: 147 us -> 151 us (1.027)
  blocking collectives: 89.7 us -> 125 us
  waiting for transfers between devices: 19.4 us -> 2.75 us
  starting transfers between devices: 27.8 us -> 16.7 us
  Pallas kernels: 8.18 us -> 5.5 us
    all_to_all x0 -> x1, blocking collectives: none -> 35.1 us  [local(): lax.all_to_all(send_f.reshape(groups_z, 4, columns), 'gz', 0, 0, tiled=True)]
    all_to_all x1 -> x0, starting transfers between devices: 12.4 us -> none  [local(): lax.all_to_all(send_f.reshape(groups_z, 4, columns), 'gz', 0, 0, tiled=True)]
    all_to_all x1 -> x0, waiting for transfers between devices: 7.92 us -> none  [local(): lax.all_to_all(send_f.reshape(groups_z, 4, columns), 'gz', 0, 0, tiled=True)]
    ppermute x2, waiting for transfers between devices: 8.6 us -> 1.24 us  [the longest x1 1.24 us: local(): after = lax.ppermute(stacked, 'gz', down)]
    pallas_call x3, Pallas kernels: 4.97 us -> 3.36 us  [the longest x1 2.03 us: prepare(): pl.pallas_call(functools.partial(prepare_kernel, slots), name='prepare',...]
  transfers between devices with their start and end apart: 6 -> 5, of which waited for: 5 -> 2; matrix products, arithmetic and copies ran while one was open for 0% -> 0% of each run, Pallas kernels for 2% -> 2%
where the time goes in v5:
time: 151 us
  blocking collectives  125 us (83%)
  starting transfers between devices  16.7 us (11%)
  Pallas kernels  5.5 us (4%)
  waiting for transfers between devices  2.75 us (2%)
    all_to_all x1, blocking collectives, local(): lax.all_to_all(send.reshape(columns, width // 2, 2, columns), 'gz', 0, 0,...  89.7 us
    all_to_all x1, blocking collectives, local(): lax.all_to_all(send_f.reshape(groups_z, 4, columns), 'gz', 0, 0, tiled=True)  35.1 us
    ppermute x1, starting transfers between devices, local(): lax.ppermute(kernel, 'parts', [(p, p ^ 1) for p in range(parts)])  4.83 us
    ppermute x1, starting transfers between devices, local(): before = lax.ppermute(stacked, 'gz', up)  4.59 us
    ppermute x1, starting transfers between devices, local(): after = lax.ppermute(stacked, 'gz', down)  3.42 us
  transfers between devices with their start and end apart: 5, of which 2 were waited for; matrix products, arithmetic and copies ran while one was open for 0% of the time, Pallas kernels for 2%

profile of v5, /device:TPU:66, one launch (start us, length us, event | category | flops | bytes accessed | tf_op | source)
XLA Modules:
  0.0 150.5 jit_solution(10306230684508838506)
XLA Ops:
  0.0 2.0 %prepare.1 = (f32[1280,128]{1,0:T(8,128)S(1)}, f32[4,64,128]{2,1,0:T(8,128)S(1)}) custom-call(f32[3]{0:T(128)} %sat_hbm.1, f32[3,64,128]{2,1,0:T(8,128)} %bitcast.19, s32[64,128]{1,0:T(8,128)} %bitcast.20, f32[6,2,128,128]{3,2,1,0:T(8,128)} %main_hbm.1, f32[6,2,128]{2,1,0:T(2,128)} %nyq_hbm.1, bf16[2,128,256]{2,1,0:T(8,128)(2,1)} %constant.16.clone.tx_hbm, ...), custom_call_target="tpu_custom_call" | custom-call | tf_op jit(solution)/shard_map/prepare/pallas_call | solution.py:161
  2.0 89.7 %all_to_all.10 = f32[128,5,2,128]{3,2,1,0:T(2,128)S(1)} all-to-all(f32[128,5,2,128]{3,2,1,0:T(2,128)S(1)} %bitcast.14), channel_id=1, replica_groups=mesh['parts'=2,'gz'=128,'gy'=2] {'gz'}, dimensions={0} | all-to-all | bytes 1310720 | tf_op jit(solution)/shard_map/all_to_all | solution.py:367
  91.8 0.0 copy-start.3
  91.9 0.0 copy-start.2
  91.9 4.8 %collective-permute-start.1 = (f32[6,128,128]{2,1,0:T(8,128)S(1)}, f32[6,128,128]{2,1,0:T(8,128)S(1)}, u32[]{:S(2)}, u32[]{:S(2)}) collective-permute-start(f32[6,128,128]{2,1,0:T(8,128)S(1)} %slice.18.kernel), channel_id=1, source_target_pairs={{0,256},{256,0},{1,257},{257,1},{2,258},{258,2},{3,259},{259,3},{4... | collective-permute-start | bytes 1179656 | tf_op jit(solution)/shard_map/ppermute | solution.py:371
  96.7 2.0 %collective-permute-start = (f32[4,128,128]{2,1,0:T(8,128)S(1)}, f32[4,128,128]{2,1,0:T(8,128)S(1)}, u32[]{:S(2)}, u32[]{:S(2)}) collective-permute-start(f32[4,128,128]{2,1,0:T(8,128)S(1)} %slice.17.own), channel_id=1, source_target_pairs={{0,1},{1,0},{2,3},{3,2},{4,5},{5,4},{6,7},{7,6},{8,9},{9,8},{10,11... | collective-permute-start | bytes 786440 | tf_op jit(solution)/shard_map/ppermute | solution.py:375
  98.7 4.6 %collective-permute-start.2 = (f32[4,64,128]{2,1,0:T(8,128)S(1)}, f32[4,64,128]{2,1,0:T(8,128)S(1)}, u32[]{:S(2)}, u32[]{:S(2)}) collective-permute-start(f32[4,64,128]{2,1,0:T(8,128)S(1)} %get-tuple-element.17.stack), channel_id=1, source_target_pairs={{0,2},{2,4},{4,6},{6,8},{8,10},{10,12},{12,14},{14,16},{16,18},{18... | collective-permute-start | bytes 393224 | tf_op jit(solution)/shard_map/ppermute | solution.py:365
  103.3 3.4 %collective-permute-start.3 = (f32[4,64,128]{2,1,0:T(8,128)S(1)}, f32[4,64,128]{2,1,0:T(8,128)S(1)}, u32[]{:S(2)}, u32[]{:S(2)}) collective-permute-start(f32[4,64,128]{2,1,0:T(8,128)S(1)} %get-tuple-element.17.stack), channel_id=1, source_target_pairs={{2,0},{4,2},{6,4},{8,6},{10,8},{12,10},{14,12},{16,14},{18,16},{20... | collective-permute-start | bytes 393224 | tf_op jit(solution)/shard_map/ppermute | solution.py:366
  106.8 0.0 copy-start
  106.8 0.0 collective-permute-done.other
  106.8 0.0 copy-done.3
  106.8 0.0 copy-done.2
  106.8 1.1 forward.1.spectra
  107.9 0.0 copy-done
  107.9 0.0 copy-start.1
  107.9 0.7 first_half.1
  108.6 0.0 collective-permute-done.1.kernel
  108.6 0.3 copy-done.1
  108.9 0.7 second_half.1
  109.6 0.0 collective-permute-done.2.before
  109.6 1.2 collective-permute-done.3.after
  110.9 1.9 %collective-permute-start.4 = (f32[520,128]{1,0:T(8,128)S(1)}, f32[520,128]{1,0:T(8,128)S(1)}, u32[]{:S(2)}, u32[]{:S(2)}) collective-permute-start(f32[520,128]{1,0:T(8,128)S(1)} %get-tuple-element.20), channel_id=1, source_target_pairs={{0,1},{1,0},{2,3},{3,2},{4,5},{5,4},{6,7},{7,6},{8,9},{9,8},{10,11... | collective-permute-start | bytes 798728 | tf_op jit(solution)/shard_map/ppermute | solution.py:381
  112.8 1.5 %collective-permute-done.4.arrived = f32[520,128]{1,0:T(8,128)S(1)} collective-permute-done((f32[520,128]{1,0:T(8,128)S(1)}, f32[520,128]{1,0:T(8,128)S(1)}, u32[]{:S(2)}, u32[]{:S(2)}) %collective-permute-start.4) | collective-permute-done | bytes 266272 | tf_op jit(solution)/shard_map/ppermute | solution.py:381
  114.3 0.0 copy-start.4
  114.4 0.0 copy-start.5
  114.4 35.1 %all_to_all.11 = f32[128,4,128]{2,1,0:T(4,128)S(1)} all-to-all(f32[128,4,128]{2,1,0:T(4,128)S(1)} %bitcast.18), channel_id=1, replica_groups=mesh['parts'=2,'gz'=128,'gy'=2] {'gz'}, dimensions={0} | all-to-all | bytes 524288 | tf_op jit(solution)/shard_map/all_to_all | solution.py:383
  149.5 0.0 copy-done.4
  149.5 0.0 copy-done.5
  149.5 1.1 finish.1
  (5 shorter events, 0.1 us)
Async XLA Ops:
  91.8 14.9 %copy-start.3 = (bf16[2,256,256]{2,1,0:T(8,128)(2,1)S(1)}, bf16[2,256,256]{2,1,0:T(8,128)(2,1)}, u32[]{:S(2)}) copy-start(bf16[2,256,256]{2,1,0:T(8,128)(2,1)} %constant.20.clone.tz) | copy-start | bytes 786436
  91.9 14.9 %copy-start.2 = (bf16[2,2,256,256]{3,2,1,0:T(8,128)(2,1)S(1)}, bf16[2,2,256,256]{3,2,1,0:T(8,128)(2,1)}, u32[]{:S(2)}) copy-start(bf16[2,2,256,256]{3,2,1,0:T(8,128)(2,1)} %constant.19.clone.ty) | copy-start | bytes 1572868
  91.9 16.7 %collective-permute-start.1 = (f32[6,128,128]{2,1,0:T(8,128)S(1)}, f32[6,128,128]{2,1,0:T(8,128)S(1)}, u32[]{:S(2)}, u32[]{:S(2)}) collective-permute-start(f32[6,128,128]{2,1,0:T(8,128)S(1)} %slice.18.kernel), channel_id=1, source_target_pairs={{0,256},{256,0},{1,257},{257,1},{2,258},{258,2},{3,259},{259,3},{4... | collective-permute-start | bytes 1179656 | tf_op jit(solution)/shard_map/ppermute | solution.py:371
  96.7 10.0 %collective-permute-start = (f32[4,128,128]{2,1,0:T(8,128)S(1)}, f32[4,128,128]{2,1,0:T(8,128)S(1)}, u32[]{:S(2)}, u32[]{:S(2)}) collective-permute-start(f32[4,128,128]{2,1,0:T(8,128)S(1)} %slice.17.own), channel_id=1, source_target_pairs={{0,1},{1,0},{2,3},{3,2},{4,5},{5,4},{6,7},{7,6},{8,9},{9,8},{10,11... | collective-permute-start | bytes 786440 | tf_op jit(solution)/shard_map/ppermute | solution.py:375
  98.7 10.9 %collective-permute-start.2 = (f32[4,64,128]{2,1,0:T(8,128)S(1)}, f32[4,64,128]{2,1,0:T(8,128)S(1)}, u32[]{:S(2)}, u32[]{:S(2)}) collective-permute-start(f32[4,64,128]{2,1,0:T(8,128)S(1)} %get-tuple-element.17.stack), channel_id=1, source_target_pairs={{0,2},{2,4},{4,6},{6,8},{8,10},{10,12},{12,14},{14,16},{16,18},{18... | collective-permute-start | bytes 393224 | tf_op jit(solution)/shard_map/ppermute | solution.py:365
  103.3 7.5 %collective-permute-start.3 = (f32[4,64,128]{2,1,0:T(8,128)S(1)}, f32[4,64,128]{2,1,0:T(8,128)S(1)}, u32[]{:S(2)}, u32[]{:S(2)}) collective-permute-start(f32[4,64,128]{2,1,0:T(8,128)S(1)} %get-tuple-element.17.stack), channel_id=1, source_target_pairs={{2,0},{4,2},{6,4},{8,6},{10,8},{12,10},{14,12},{16,14},{18,16},{20... | collective-permute-start | bytes 393224 | tf_op jit(solution)/shard_map/ppermute | solution.py:366
  106.8 1.1 copy-start
  107.9 1.0 copy-start.1
  110.9 3.5 %collective-permute-start.4 = (f32[520,128]{1,0:T(8,128)S(1)}, f32[520,128]{1,0:T(8,128)S(1)}, u32[]{:S(2)}, u32[]{:S(2)}) collective-permute-start(f32[520,128]{1,0:T(8,128)S(1)} %get-tuple-element.20), channel_id=1, source_target_pairs={{0,1},{1,0},{2,3},{3,2},{4,5},{5,4},{6,7},{7,6},{8,9},{9,8},{10,11... | collective-permute-start | bytes 798728 | tf_op jit(solution)/shard_map/ppermute | solution.py:381
  114.3 35.1 %copy-start.4 = (bf16[2,2,256,128]{3,2,1,0:T(8,128)(2,1)S(1)}, bf16[2,2,256,128]{3,2,1,0:T(8,128)(2,1)}, u32[]{:S(2)}) copy-start(bf16[2,2,256,128]{3,2,1,0:T(8,128)(2,1)} %constant.23.clone.ny) | copy-start | bytes 786436
  114.4 35.1 %copy-start.5 = (bf16[2,128,256]{2,1,0:T(8,128)(2,1)S(1)}, bf16[2,128,256]{2,1,0:T(8,128)(2,1)}, u32[]{:S(2)}) copy-start(bf16[2,128,256]{2,1,0:T(8,128)(2,1)} %constant.22.clone.tx) | copy-start | bytes 393220

commit v6 on v5

--- a/solution.py
+++ b/solution.py
@@ -97,26 +97,25 @@
     _, half, columns = dirs.shape
     width = 4 + 6 * slots
     slot = place("parts", 2 // slots)
-    copies = [
-        pltpu.make_async_copy(reg_hbm, reg, sems.at[0]),
-        pltpu.make_async_copy(dir_hbm, dirs, sems.at[1]),
-        pltpu.make_async_copy(main_hbm.at[:, pl.ds(slot, slots)], main, sems.at[2]),
+    small = [
+        pltpu.make_async_copy(sat_hbm, sat_ref, sems.at[0]),
+        pltpu.make_async_copy(reg_hbm, reg, sems.at[1]),
+        pltpu.make_async_copy(dir_hbm, dirs, sems.at[2]),
         pltpu.make_async_copy(tx_hbm, tx, sems.at[3]),
-        pltpu.make_async_copy(ny_hbm.at[place("gy", 2)], ny, sems.at[4]),
-        pltpu.make_async_copy(nyq_hbm, nyq, sems.at[5]),
-        pltpu.make_async_copy(sat_hbm, sat_ref, sems.at[6]),
+        pltpu.make_async_copy(nyq_hbm, nyq, sems.at[4]),
+        pltpu.make_async_copy(ny_hbm.at[place("gy", 2)], ny, sems.at[5]),
     ]
-    for c in copies:
+    lines = [pltpu.make_async_copy(main_hbm.at[r, pl.ds(slot, slots)], main.at[r], sems.at[6 + r]) for r in range(6)]
+    for c in small[:3] + lines + small[3:]:
         c.start()
     rows_t[...] = jnp.zeros_like(rows_t)
-    copies[0].wait()
+    for c in small[:3]:
+        c.wait()
     region = reg[...]
     magnetic = (region > 0).astype(f32)
     strength = jnp.zeros(region.shape, f32)
-    copies[6].wait()
     for r in range(3):
         strength = strength + jnp.where(region == r + 1, sat_ref[r], 0.0)
-    copies[1].wait()
     stack_ref[3] = magnetic
     lane = lax.broadcasted_iota(jnp.int32, (half, columns), 1)
     signs = (1 - 2 * (lane % 2)).astype(f32)
@@ -129,26 +128,26 @@
         moments.append(moment)
         total = jnp.sum(moment * signs, axis=1, keepdims=True)
         sums = jnp.where((lane % 4 == c) & (lane % 32 < 12), total, sums)
-    copies[3].wait()
+    for r in range(6):
+        lines[r].wait()
+        for s in range(slots):
+            send_ref[pl.ds(4 + 6 * s + r, columns, stride=width), :] = main[r, s].T
+    small[3].wait()
     zero = jnp.zeros((half, columns), bf16)
     table = (tx[0], tx[1])
     for c in range(3):
         high, low = split(moments[c])
         wide = [jnp.concatenate([jnp.concatenate([p, zero], 1), jnp.concatenate([zero, p], 1)], 0) for p in (high, low)]
         send_ref[pl.ds(c, columns, stride=width), :] = three(table, wide, ((1,), (1,)))
-    copies[2].wait()
-    for s in range(slots):
-        for r in range(6):
-            send_ref[pl.ds(4 + 6 * s + r, columns, stride=width), :] = main[r, s].T
-    copies[4].wait()
-    parts = [split(jnp.where(lane // 32 == q, sums, 0.0)) for q in range(4)]
-    stacked = [jnp.concatenate([p[k] for p in parts], axis=0) for k in range(2)]
-    row = three((ny[0], ny[1]), stacked)
-    copies[5].wait()
+    small[4].wait()
     for s in range(2):
         for i in range(3):
             for j in range(3):
                 rows_t[pl.ds(64 * s + 16 + 4 * i + j, 1), :] = nyq[tensor_index[i][j], pl.ds(s, 1), :]
+    small[5].wait()
+    parts = [split(jnp.where(lane // 32 == q, sums, 0.0)) for q in range(4)]
+    stacked = [jnp.concatenate([p[k] for p in parts], axis=0) for k in range(2)]
+    row = three((ny[0], ny[1]), stacked)
     send_ref[pl.ds(3, columns, stride=width), :] = row + rows_t[...].T
 
 
@@ -177,7 +176,7 @@
             pltpu.VMEM(tx.shape, bf16),
             pltpu.VMEM(ny.shape[1:], bf16),
             pltpu.VMEM((columns, columns), f32),
-            pltpu.SemaphoreType.DMA((7,)),
+            pltpu.SemaphoreType.DMA((12,)),
         ],
     )(*(pltpu.with_memory_space_constraint(a, pltpu.HBM) for a in (saturation, direction, region, kernel_main, kernel_nyq, tx, ny)))
 
@@ -301,7 +300,33 @@
     )(spectra, kernel, ready, line, stacked, tz, ty)
 
 
-def finish_kernel(recv, arrived, stack, before, after, tx, ny, out):
+def total_kernel(own, arrived, out, ready, sems):
+    count = sems.shape[0]
+    size = own.shape[0] // count
+    copies = []
+    for k in range(count):
+        piece = pl.ds(k * size, size)
+        ready[piece, :] = own[piece, :] + arrived[piece, :]
+        copies.append(pltpu.make_async_copy(ready.at[piece], out.at[piece], sems.at[k]))
+        copies[-1].start()
+    for c in copies:
+        c.wait()
+
+
+def total(own, arrived):
+    vmem = pl.BlockSpec(memory_space=pltpu.VMEM)
+    return pl.pallas_call(
+        total_kernel,
+        name="total",
+        compiler_params=limits,
+        out_shape=jax.ShapeDtypeStruct(own.shape, f32),
+        in_specs=[vmem] * 2,
+        out_specs=pl.BlockSpec(memory_space=pltpu.HBM),
+        scratch_shapes=[pltpu.VMEM(own.shape, f32), pltpu.SemaphoreType.DMA((4,))],
+    )(own, arrived)
+
+
+def finish_kernel(recv, arrived, stack, before, after, tx, ny, out, ready, sems):
     _, half, columns = stack.shape
     lane = lax.broadcasted_iota(jnp.int32, (half, columns), 1)
     line = lax.broadcasted_iota(jnp.int32, (half, columns), 0)
@@ -325,12 +350,17 @@
     for q in range(4):
         sums = jnp.where(lane // 32 == q, nyquist[q * half : (q + 1) * half], sums)
     table = (tx[0], tx[1])
+    copies = []
     for c in range(3):
         prod = three(split(recv[pl.ds(c, columns, stride=4), :].T), table)
         demag = prod[:half, :columns] + prod[half:, columns:]
-        total = jnp.sum(jnp.where(lane % 32 // 4 == c, sums, 0.0), axis=1, keepdims=True)
+        line_sum = jnp.sum(jnp.where(lane % 32 // 4 == c, sums, 0.0), axis=1, keepdims=True)
         exchange = exchange_stiffness * (magnetic * near(c) - count * stack[c])
-        out[c] = demag + total * signs + exchange
+        ready[c] = demag + line_sum * signs + exchange
+        copies.append(pltpu.make_async_copy(ready.at[c], out.at[c], sems.at[c]))
+        copies[-1].start()
+    for c in copies:
+        c.wait()
 
 
 def finish(recv, arrived, stacked, before, after, tx, ny):
@@ -341,7 +371,8 @@
         compiler_params=limits,
         out_shape=jax.ShapeDtypeStruct((3,) + stacked.shape[1:], f32),
         in_specs=[vmem] * 7,
-        out_specs=vmem,
+        out_specs=pl.BlockSpec(memory_space=pltpu.HBM),
+        scratch_shapes=[pltpu.VMEM((3,) + stacked.shape[1:], f32), pltpu.SemaphoreType.DMA((3,))],
     )(recv, arrived, stacked, before, after, tx, ny)
 
 
@@ -360,10 +391,6 @@
         halves(t["tx"]), halves(t["ny"]).swapaxes(0, 1), slots,
     )
     width = 4 + 6 * slots
-    up = [(i, i + 1) for i in range(groups_z - 1)]
-    down = [(b, a) for a, b in up]
-    before = lax.ppermute(stacked, "gz", up)
-    after = lax.ppermute(stacked, "gz", down)
     recv = lax.all_to_all(send.reshape(columns, width // 2, 2, columns), "gz", 0, 0, tiled=True)
     recv = recv.reshape(columns, width, columns).transpose(1, 0, 2)
     kernel = recv[4:10]
@@ -377,11 +404,15 @@
     spectra = forward(own_m, other_m, halves(t["ty"]), halves(t["tz"]))
     ready, line = first_half(pairs, spectra, kernel, own_m[3], tz_back)
     own, other = second_half(pairs, spectra, kernel_other, ready, line, stacked, tz_back, halves(t["ty_back"]))
-    other, before, after = lax.optimization_barrier((other, before, after))
     arrived = lax.ppermute(other, "gy", swap)
-    send_f = own + arrived[: 4 * groups_z]
+    send_f = total(own, arrived)
     recv_f = lax.all_to_all(send_f.reshape(groups_z, 4, columns), "gz", 0, 0, tiled=True)
     recv_f = recv_f.reshape(4 * columns, columns)
+    up = [(i, i + 1) for i in range(groups_z - 1)]
+    down = [(b, a) for a, b in up]
+    edge_planes, _ = lax.optimization_barrier((stacked, send_f))
+    before = lax.ppermute(edge_planes, "gz", up)
+    after = lax.ppermute(edge_planes, "gz", down)
     tx_back, ny_back = halves(t["tx_back"]), halves(t["ny_back"])
     return finish(recv_f, arrived, stacked, before, after, tx_back, ny_back)[:, None]
 

time: 151 us -> 145 us (0.960)
  blocking collectives: 125 us -> 89.7 us
  waiting for transfers between devices: 2.75 us -> 20.1 us
  starting transfers between devices: 16.7 us -> 28.2 us
    all_to_all x1 -> x0, blocking collectives: 35.1 us -> none  [local(): lax.all_to_all(send_f.reshape(groups_z, 4, columns), 'gz', 0, 0, tiled=True)]
    all_to_all x0 -> x1, starting transfers between devices: none -> 12.9 us  [local(): lax.all_to_all(send_f.reshape(groups_z, 4, columns), 'gz', 0, 0, tiled=True)]
    all_to_all x0 -> x1, waiting for transfers between devices: none -> 7.92 us  [local(): lax.all_to_all(send_f.reshape(groups_z, 4, columns), 'gz', 0, 0, tiled=True)]
    ppermute x2, waiting for transfers between devices: 1.24 us -> 8.6 us  [the longest x1 6.89 us: local(): after = lax.ppermute(edge_planes, 'gz', down)]
  transfers between devices with their start and end apart: 5 -> 6, of which waited for: 2 -> 6; matrix products, arithmetic and copies ran while one was open for 0% -> 0% of each run, Pallas kernels for 2% -> 1%
where the time goes in v6:
time: 145 us
  blocking collectives  89.7 us (62%)
  starting transfers between devices  28.2 us (19%)
  waiting for transfers between devices  20.1 us (14%)
  Pallas kernels  6.55 us (5%)
    all_to_all x1, blocking collectives, local(): lax.all_to_all(send.reshape(columns, width // 2, 2, columns), 'gz', 0, 0,...  89.7 us
    all_to_all x1, starting transfers between devices, local(): lax.all_to_all(send_f.reshape(groups_z, 4, columns), 'gz', 0, 0, tiled=True)  12.9 us
    all_to_all x1, waiting for transfers between devices, local(): lax.all_to_all(send_f.reshape(groups_z, 4, columns), 'gz', 0, 0, tiled=True)  7.92 us
    ppermute x1, waiting for transfers between devices, local(): after = lax.ppermute(edge_planes, 'gz', down)  6.89 us
    ppermute x1, starting transfers between devices, local(): lax.ppermute(kernel, 'parts', [(p, p ^ 1) for p in range(parts)])  4.84 us
    ppermute x1, starting transfers between devices, local(): after = lax.ppermute(edge_planes, 'gz', down)  4.61 us
  transfers between devices with their start and end apart: 6, of which 6 were waited for; matrix products, arithmetic and copies ran while one was open for 0% of the time, Pallas kernels for 1%

profile of v6, /device:TPU:66, one launch (start us, length us, event | category | flops | bytes accessed | tf_op | source)
XLA Modules:
  0.0 144.9 jit_solution(10057257485545623632)
XLA Ops:
  0.0 2.3 %prepare.1 = (f32[1280,128]{1,0:T(8,128)S(1)}, f32[4,64,128]{2,1,0:T(8,128)S(1)}) custom-call(f32[3]{0:T(128)} %sat_hbm.1, f32[3,64,128]{2,1,0:T(8,128)} %bitcast.18, s32[64,128]{1,0:T(8,128)} %bitcast.19, f32[6,2,128,128]{3,2,1,0:T(8,128)} %main_hbm.1, f32[6,2,128]{2,1,0:T(2,128)} %nyq_hbm.1, bf16[2,128,256]{2,1,0:T(8,128)(2,1)} %constant.16.clone.tx_hbm, ...), custom_call_target="tpu_custom_call" | custom-call | tf_op jit(solution)/shard_map/prepare/pallas_call | solution.py:160
  2.4 89.7 %all_to_all.10 = f32[128,5,2,128]{3,2,1,0:T(2,128)S(1)} all-to-all(f32[128,5,2,128]{3,2,1,0:T(2,128)S(1)} %bitcast.14), channel_id=1, replica_groups=mesh['parts'=2,'gz'=128,'gy'=2] {'gz'}, dimensions={0} | all-to-all | bytes 1310720 | tf_op jit(solution)/shard_map/all_to_all | solution.py:394
  92.1 0.0 copy-start.3
  92.2 0.0 copy-start.2
  92.2 4.8 %collective-permute-start.1 = (f32[6,128,128]{2,1,0:T(8,128)S(1)}, f32[6,128,128]{2,1,0:T(8,128)S(1)}, u32[]{:S(2)}, u32[]{:S(2)}) collective-permute-start(f32[6,128,128]{2,1,0:T(8,128)S(1)} %slice.14.kernel), channel_id=1, source_target_pairs={{0,256},{256,0},{1,257},{257,1},{2,258},{258,2},{3,259},{259,3},{4... | collective-permute-start | bytes 1179656 | tf_op jit(solution)/shard_map/ppermute | solution.py:398
  97.1 2.0 %collective-permute-start = (f32[4,128,128]{2,1,0:T(8,128)S(1)}, f32[4,128,128]{2,1,0:T(8,128)S(1)}, u32[]{:S(2)}, u32[]{:S(2)}) collective-permute-start(f32[4,128,128]{2,1,0:T(8,128)S(1)} %slice.13.own), channel_id=1, source_target_pairs={{0,1},{1,0},{2,3},{3,2},{4,5},{5,4},{6,7},{7,6},{8,9},{9,8},{10,11... | collective-permute-start | bytes 786440 | tf_op jit(solution)/shard_map/ppermute | solution.py:402
  99.0 0.0 copy-start
  99.0 1.5 %collective-permute-done.other = f32[4,128,128]{2,1,0:T(8,128)S(1)} collective-permute-done((f32[4,128,128]{2,1,0:T(8,128)S(1)}, f32[4,128,128]{2,1,0:T(8,128)S(1)}, u32[]{:S(2)}, u32[]{:S(2)}) %collective-permute-start) | collective-permute-done | bytes 262176 | tf_op jit(solution)/shard_map/ppermute | solution.py:402
  100.5 0.0 copy-done.3
  100.5 0.0 copy-done.2
  100.5 1.1 forward.1.spectra
  101.6 0.0 copy-done
  101.6 0.0 copy-start.1
  101.6 0.7 first_half.1
  102.3 0.6 collective-permute-done.1.kernel
  102.9 0.0 copy-done.1
  102.9 0.7 second_half.1
  103.6 2.0 %collective-permute-start.2 = (f32[520,128]{1,0:T(8,128)S(1)}, f32[520,128]{1,0:T(8,128)S(1)}, u32[]{:S(2)}, u32[]{:S(2)}) collective-permute-start(f32[520,128]{1,0:T(8,128)S(1)} %get-tuple-element.17), channel_id=1, source_target_pairs={{0,1},{1,0},{2,3},{3,2},{4,5},{5,4},{6,7},{7,6},{8,9},{9,8},{10,11... | collective-permute-start | bytes 798728 | tf_op jit(solution)/shard_map/ppermute | solution.py:407
  105.6 1.5 %collective-permute-done.2.arrived = f32[520,128]{1,0:T(8,128)S(1)} collective-permute-done((f32[520,128]{1,0:T(8,128)S(1)}, f32[520,128]{1,0:T(8,128)S(1)}, u32[]{:S(2)}, u32[]{:S(2)}) %collective-permute-start.2) | collective-permute-done | bytes 266272 | tf_op jit(solution)/shard_map/ppermute | solution.py:407
  107.1 0.7 total.1
  107.8 0.0 copy-start.4
  107.8 0.0 copy-start.5
  107.8 12.9 %all-to-all-start.1 = ((f32[128,4,128]{2,1,0:T(4,128)}), f32[128,4,128]{2,1,0:T(4,128)S(1)}, u32[]{:S(2)}, u32[]{:S(2)}) async-start(f32[128,4,128]{2,1,0:T(4,128)} %bitcast.7), calls=%async_computation.1 | async-start | bytes 524288 | tf_op jit(solution)/shard_map/all_to_all | solution.py:409
  120.8 4.6 %collective-permute-start.4 = (f32[4,64,128]{2,1,0:T(8,128)S(1)}, f32[4,64,128]{2,1,0:T(8,128)S(1)}, u32[]{:S(2)}, u32[]{:S(2)}) collective-permute-start(f32[4,64,128]{2,1,0:T(8,128)S(1)} %get-tuple-element.18.stack), channel_id=1, source_target_pairs={{2,0},{4,2},{6,4},{8,6},{10,8},{12,10},{14,12},{16,14},{18,16},{20... | collective-permute-start | bytes 393224 | tf_op jit(solution)/shard_map/ppermute | solution.py:415
  125.4 2.0 %collective-permute-start.3 = (f32[4,64,128]{2,1,0:T(8,128)S(1)}, f32[4,64,128]{2,1,0:T(8,128)S(1)}, u32[]{:S(2)}, u32[]{:S(2)}) collective-permute-start(f32[4,64,128]{2,1,0:T(8,128)S(1)} %get-tuple-element.18.stack), channel_id=1, source_target_pairs={{0,2},{2,4},{4,6},{6,8},{8,10},{10,12},{12,14},{14,16},{16,18},{18... | collective-permute-start | bytes 393224 | tf_op jit(solution)/shard_map/ppermute | solution.py:414
  127.3 6.9 %collective-permute-done.4.after = f32[4,64,128]{2,1,0:T(8,128)S(1)} collective-permute-done((f32[4,64,128]{2,1,0:T(8,128)S(1)}, f32[4,64,128]{2,1,0:T(8,128)S(1)}, u32[]{:S(2)}, u32[]{:S(2)}) %collective-permute-start.4) | collective-permute-done | bytes 131104 | tf_op jit(solution)/shard_map/ppermute | solution.py:415
  134.2 1.7 %collective-permute-done.3.before = f32[4,64,128]{2,1,0:T(8,128)S(1)} collective-permute-done((f32[4,64,128]{2,1,0:T(8,128)S(1)}, f32[4,64,128]{2,1,0:T(8,128)S(1)}, u32[]{:S(2)}, u32[]{:S(2)}) %collective-permute-start.3) | collective-permute-done | bytes 131104 | tf_op jit(solution)/shard_map/ppermute | solution.py:414
  135.9 7.9 %all-to-all-done.1 = f32[128,4,128]{2,1,0:T(4,128)S(1)} async-done(((f32[128,4,128]{2,1,0:T(4,128)}), f32[128,4,128]{2,1,0:T(4,128)S(1)}, u32[]{:S(2)}, u32[]{:S(2)}) %all-to-all-start.1) | async-done | bytes 262176 | tf_op jit(solution)/shard_map/all_to_all | solution.py:409
  143.9 0.0 copy-done.4
  143.9 0.0 copy-done.5
  143.9 1.0 finish.1
  (4 shorter events, 0.1 us)
Async XLA Ops:
  92.1 8.4 %copy-start.3 = (bf16[2,256,256]{2,1,0:T(8,128)(2,1)S(1)}, bf16[2,256,256]{2,1,0:T(8,128)(2,1)}, u32[]{:S(2)}) copy-start(bf16[2,256,256]{2,1,0:T(8,128)(2,1)} %constant.20.clone.tz) | copy-start | bytes 786436
  92.2 8.3 %copy-start.2 = (bf16[2,2,256,256]{3,2,1,0:T(8,128)(2,1)S(1)}, bf16[2,2,256,256]{3,2,1,0:T(8,128)(2,1)}, u32[]{:S(2)}) copy-start(bf16[2,2,256,256]{3,2,1,0:T(8,128)(2,1)} %constant.19.clone.ty) | copy-start | bytes 1572868
  92.2 10.7 %collective-permute-start.1 = (f32[6,128,128]{2,1,0:T(8,128)S(1)}, f32[6,128,128]{2,1,0:T(8,128)S(1)}, u32[]{:S(2)}, u32[]{:S(2)}) collective-permute-start(f32[6,128,128]{2,1,0:T(8,128)S(1)} %slice.14.kernel), channel_id=1, source_target_pairs={{0,256},{256,0},{1,257},{257,1},{2,258},{258,2},{3,259},{259,3},{4... | collective-permute-start | bytes 1179656 | tf_op jit(solution)/shard_map/ppermute | solution.py:398
  97.1 3.5 %collective-permute-start = (f32[4,128,128]{2,1,0:T(8,128)S(1)}, f32[4,128,128]{2,1,0:T(8,128)S(1)}, u32[]{:S(2)}, u32[]{:S(2)}) collective-permute-start(f32[4,128,128]{2,1,0:T(8,128)S(1)} %slice.13.own), channel_id=1, source_target_pairs={{0,1},{1,0},{2,3},{3,2},{4,5},{5,4},{6,7},{7,6},{8,9},{9,8},{10,11... | collective-permute-start | bytes 786440 | tf_op jit(solution)/shard_map/ppermute | solution.py:402
  99.0 2.6 %copy-start = (bf16[2,2,128,256]{3,2,1,0:T(8,128)(2,1)S(1)}, bf16[2,2,128,256]{3,2,1,0:T(8,128)(2,1)}, u32[]{:S(2)}) copy-start(bf16[2,2,128,256]{3,2,1,0:T(8,128)(2,1)} %constant.18.clone.tz) | copy-start | bytes 786436
  101.6 1.3 copy-start.1
  103.6 3.5 %collective-permute-start.2 = (f32[520,128]{1,0:T(8,128)S(1)}, f32[520,128]{1,0:T(8,128)S(1)}, u32[]{:S(2)}, u32[]{:S(2)}) collective-permute-start(f32[520,128]{1,0:T(8,128)S(1)} %get-tuple-element.17), channel_id=1, source_target_pairs={{0,1},{1,0},{2,3},{3,2},{4,5},{5,4},{6,7},{7,6},{8,9},{9,8},{10,11... | collective-permute-start | bytes 798728 | tf_op jit(solution)/shard_map/ppermute | solution.py:407
  107.8 36.1 %copy-start.4 = (bf16[2,2,256,128]{3,2,1,0:T(8,128)(2,1)S(1)}, bf16[2,2,256,128]{3,2,1,0:T(8,128)(2,1)}, u32[]{:S(2)}) copy-start(bf16[2,2,256,128]{3,2,1,0:T(8,128)(2,1)} %constant.23.clone.ny) | copy-start | bytes 786436
  107.8 36.0 %copy-start.5 = (bf16[2,128,256]{2,1,0:T(8,128)(2,1)S(1)}, bf16[2,128,256]{2,1,0:T(8,128)(2,1)}, u32[]{:S(2)}) copy-start(bf16[2,128,256]{2,1,0:T(8,128)(2,1)} %constant.22.clone.tx) | copy-start | bytes 393220
  107.8 36.0 %all-to-all-start.1 = ((f32[128,4,128]{2,1,0:T(4,128)}), f32[128,4,128]{2,1,0:T(4,128)S(1)}, u32[]{:S(2)}, u32[]{:S(2)}) async-start(f32[128,4,128]{2,1,0:T(4,128)} %bitcast.7), calls=%async_computation.1 | async-start | bytes 524288 | tf_op jit(solution)/shard_map/all_to_all | solution.py:409
  120.8 13.5 %collective-permute-start.4 = (f32[4,64,128]{2,1,0:T(8,128)S(1)}, f32[4,64,128]{2,1,0:T(8,128)S(1)}, u32[]{:S(2)}, u32[]{:S(2)}) collective-permute-start(f32[4,64,128]{2,1,0:T(8,128)S(1)} %get-tuple-element.18.stack), channel_id=1, source_target_pairs={{2,0},{4,2},{6,4},{8,6},{10,8},{12,10},{14,12},{16,14},{18,16},{20... | collective-permute-start | bytes 393224 | tf_op jit(solution)/shard_map/ppermute | solution.py:415
  125.4 10.6 %collective-permute-start.3 = (f32[4,64,128]{2,1,0:T(8,128)S(1)}, f32[4,64,128]{2,1,0:T(8,128)S(1)}, u32[]{:S(2)}, u32[]{:S(2)}) collective-permute-start(f32[4,64,128]{2,1,0:T(8,128)S(1)} %get-tuple-element.18.stack), channel_id=1, source_target_pairs={{0,2},{2,4},{4,6},{6,8},{8,10},{10,12},{12,14},{14,16},{16,18},{18... | collective-permute-start | bytes 393224 | tf_op jit(solution)/shard_map/ppermute | solution.py:414

commit v7 on v5

--- a/solution.py
+++ b/solution.py
@@ -265,22 +265,20 @@
     )(spectra, kernel, row, tz)
 
 
-def second_half_kernel(pairs, spectra, kernel, ready, line_ref, stack, tz, ty, own, other):
+def second_half_kernel(pairs, spectra, kernel, ready, line_ref, stack, tz, ty, lines_out, other):
     planes, width = line_ref.shape
     slot = 1 - place("parts", pairs)
     gy = place("gy", 2)
     table = (tz[0, slot], tz[1, slot])
-    y_table = (ty[0, gy], ty[1, gy])
+    y_table = (ty[0, gy, :, width:], ty[1, gy, :, width:])
     for i in range(3):
         lines = ready[i] + back(*field_of(kernel, spectra, slot, i), table)
-        lines = three(split(lines), y_table)
-        own[pl.ds(i, planes, stride=4), :] = lines[:, :width]
-        other[pl.ds(i, planes, stride=4), :] = lines[:, width:]
-    own[pl.ds(3, planes, stride=4), :] = line_ref[...]
+        lines_out[i] = lines
+        other[pl.ds(i, planes, stride=4), :] = three(split(lines), y_table)
     other[pl.ds(3, planes, stride=4), :] = line_ref[...]
     last = stack.shape[1] - 1
     for c in range(4):
-        edge = jnp.where(place("gy", 2) == 0, stack[c, last:], stack[c, :1])
+        edge = jnp.where(gy == 0, stack[c, last:], stack[c, :1])
         other[4 * planes + c : 4 * planes + c + 1, :] = edge
         other[4 * planes + 4 + c : 4 * planes + 5 + c, :] = edge
 
@@ -293,7 +291,7 @@
         name="second_half",
         compiler_params=limits,
         out_shape=(
-            jax.ShapeDtypeStruct((4 * planes, width), f32),
+            jax.ShapeDtypeStruct((3, planes, 2 * width), f32),
             jax.ShapeDtypeStruct((4 * planes + 8, width), f32),
         ),
         in_specs=[vmem] * 7,
@@ -301,17 +299,38 @@
     )(spectra, kernel, ready, line, stacked, tz, ty)
 
 
-def finish_kernel(recv, arrived, stack, before, after, tx, ny, out):
+def own_half_kernel(lines, line_ref, ty, own):
+    planes, width = line_ref.shape
+    gy = place("gy", 2)
+    y_table = (ty[0, gy, :, :width], ty[1, gy, :, :width])
+    for i in range(3):
+        own[pl.ds(i, planes, stride=4), :] = three(split(lines[i]), y_table)
+    own[pl.ds(3, planes, stride=4), :] = line_ref[...]
+
+
+def own_half(lines, line, ty):
+    planes, width = line.shape
+    vmem = pl.BlockSpec(memory_space=pltpu.VMEM)
+    return pl.pallas_call(
+        own_half_kernel,
+        name="own_half",
+        compiler_params=limits,
+        out_shape=jax.ShapeDtypeStruct((4 * planes, width), f32),
+        in_specs=[vmem] * 3,
+        out_specs=vmem,
+    )(lines, line, ty)
+
+
+def exchange_kernel(arrived, stack, before, after, out):
     _, half, columns = stack.shape
     lane = lax.broadcasted_iota(jnp.int32, (half, columns), 1)
     line = lax.broadcasted_iota(jnp.int32, (half, columns), 0)
-    signs = (1 - 2 * (lane % 2)).astype(f32)
-    gy = place("gy", 2)
-    lower = gy == 0
+    lower = place("gy", 2) == 0
+    first_edge = arrived.shape[0] - 8
 
     def near(c):
         one = stack[c]
-        edge = arrived[pl.ds(4 * columns + c, 1), :]
+        edge = arrived[pl.ds(first_edge + c, 1), :]
         low = jnp.where(line == 0, jnp.where(lower, 0.0, edge), pltpu.roll(one, 1, 0))
         high = jnp.where(line == half - 1, jnp.where(lower, edge, 0.0), pltpu.roll(one, half - 1, 0))
         left = jnp.where(lane == 0, 0.0, pltpu.roll(one, 1, 1))
@@ -320,6 +339,27 @@
 
     count = near(3)
     magnetic = stack[3]
+    for c in range(3):
+        out[c] = exchange_stiffness * (magnetic * near(c) - count * stack[c])
+
+
+def exchange(arrived, stacked, before, after):
+    vmem = pl.BlockSpec(memory_space=pltpu.VMEM)
+    return pl.pallas_call(
+        exchange_kernel,
+        name="exchange",
+        compiler_params=limits,
+        out_shape=jax.ShapeDtypeStruct((3,) + stacked.shape[1:], f32),
+        in_specs=[vmem] * 4,
+        out_specs=vmem,
+    )(arrived, stacked, before, after)
+
+
+def finish_kernel(recv, added, tx, ny, out):
+    _, half, columns = added.shape
+    lane = lax.broadcasted_iota(jnp.int32, (half, columns), 1)
+    signs = (1 - 2 * (lane % 2)).astype(f32)
+    gy = place("gy", 2)
     nyquist = three((ny[0, gy], ny[1, gy]), split(recv[pl.ds(3, columns, stride=4), :]))
     sums = jnp.zeros((half, columns), f32)
     for q in range(4):
@@ -329,20 +369,19 @@
         prod = three(split(recv[pl.ds(c, columns, stride=4), :].T), table)
         demag = prod[:half, :columns] + prod[half:, columns:]
         total = jnp.sum(jnp.where(lane % 32 // 4 == c, sums, 0.0), axis=1, keepdims=True)
-        exchange = exchange_stiffness * (magnetic * near(c) - count * stack[c])
-        out[c] = demag + total * signs + exchange
-
-
-def finish(recv, arrived, stacked, before, after, tx, ny):
+        out[c] = demag + total * signs + added[c]
+
+
+def finish(recv, added, tx, ny):
     vmem = pl.BlockSpec(memory_space=pltpu.VMEM)
     return pl.pallas_call(
         finish_kernel,
         name="finish",
         compiler_params=limits,
-        out_shape=jax.ShapeDtypeStruct((3,) + stacked.shape[1:], f32),
-        in_specs=[vmem] * 7,
+        out_shape=jax.ShapeDtypeStruct(added.shape, f32),
+        in_specs=[vmem] * 4,
         out_specs=vmem,
-    )(recv, arrived, stacked, before, after, tx, ny)
+    )(recv, added, tx, ny)
 
 
 def local(direction, region, saturation, kernel_main, kernel_nyq):
@@ -360,10 +399,6 @@
         halves(t["tx"]), halves(t["ny"]).swapaxes(0, 1), slots,
     )
     width = 4 + 6 * slots
-    up = [(i, i + 1) for i in range(groups_z - 1)]
-    down = [(b, a) for a, b in up]
-    before = lax.ppermute(stacked, "gz", up)
-    after = lax.ppermute(stacked, "gz", down)
     recv = lax.all_to_all(send.reshape(columns, width // 2, 2, columns), "gz", 0, 0, tiled=True)
     recv = recv.reshape(columns, width, columns).transpose(1, 0, 2)
     kernel = recv[4:10]
@@ -376,14 +411,20 @@
     tz_back = halves(t["tz_back"])
     spectra = forward(own_m, other_m, halves(t["ty"]), halves(t["tz"]))
     ready, line = first_half(pairs, spectra, kernel, own_m[3], tz_back)
-    own, other = second_half(pairs, spectra, kernel_other, ready, line, stacked, tz_back, halves(t["ty_back"]))
-    other, before, after = lax.optimization_barrier((other, before, after))
+    ty_back = halves(t["ty_back"])
+    lines, other = second_half(pairs, spectra, kernel_other, ready, line, stacked, tz_back, ty_back)
     arrived = lax.ppermute(other, "gy", swap)
+    own = own_half(lines, line, ty_back)
     send_f = own + arrived[: 4 * groups_z]
     recv_f = lax.all_to_all(send_f.reshape(groups_z, 4, columns), "gz", 0, 0, tiled=True)
     recv_f = recv_f.reshape(4 * columns, columns)
+    up = [(i, i + 1) for i in range(groups_z - 1)]
+    down = [(b, a) for a, b in up]
+    edge_planes, _ = lax.optimization_barrier((stacked, send_f))
+    before = lax.ppermute(edge_planes, "gz", up)
+    after = lax.ppermute(edge_planes, "gz", down)
     tx_back, ny_back = halves(t["tx_back"]), halves(t["ny_back"])
-    return finish(recv_f, arrived, stacked, before, after, tx_back, ny_back)[:, None]
+    return finish(recv_f, exchange(arrived, stacked, before, after), tx_back, ny_back)[:, None]
 
 
 def solution(mesh):

time: 151 us -> 145 us (0.960)
  blocking collectives: 125 us -> 89.7 us
  waiting for transfers between devices: 2.75 us -> 19.5 us
  starting transfers between devices: 16.7 us -> 28.2 us
    all_to_all x1 -> x0, blocking collectives: 35.1 us -> none  [local(): lax.all_to_all(send_f.reshape(groups_z, 4, columns), 'gz', 0, 0, tiled=True)]
    all_to_all x0 -> x1, starting transfers between devices: none -> 12.8 us  [local(): lax.all_to_all(send_f.reshape(groups_z, 4, columns), 'gz', 0, 0, tiled=True)]
    all_to_all x0 -> x1, waiting for transfers between devices: none -> 7.71 us  [local(): lax.all_to_all(send_f.reshape(groups_z, 4, columns), 'gz', 0, 0, tiled=True)]
    ppermute x2, waiting for transfers between devices: 1.24 us -> 8.5 us  [the longest x1 6.74 us: local(): after = lax.ppermute(edge_planes, 'gz', down)]
  transfers between devices with their start and end apart: 5 -> 6, of which waited for: 2 -> 6; matrix products, arithmetic and copies ran while one was open for 0% -> 0% of each run, Pallas kernels for 2% -> 2%
where the time goes in v7:
time: 145 us
  blocking collectives  89.7 us (62%)
  starting transfers between devices  28.2 us (19%)
  waiting for transfers between devices  19.5 us (13%)
  Pallas kernels  6.13 us (4%)
    all_to_all x1, blocking collectives, local(): lax.all_to_all(send.reshape(columns, width // 2, 2, columns), 'gz', 0, 0,...  89.7 us
    all_to_all x1, starting transfers between devices, local(): lax.all_to_all(send_f.reshape(groups_z, 4, columns), 'gz', 0, 0, tiled=True)  12.8 us
    all_to_all x1, waiting for transfers between devices, local(): lax.all_to_all(send_f.reshape(groups_z, 4, columns), 'gz', 0, 0, tiled=True)  7.71 us
    ppermute x1, waiting for transfers between devices, local(): after = lax.ppermute(edge_planes, 'gz', down)  6.74 us
    ppermute x1, starting transfers between devices, local(): lax.ppermute(kernel, 'parts', [(p, p ^ 1) for p in range(parts)])  4.83 us
    ppermute x1, starting transfers between devices, local(): after = lax.ppermute(edge_planes, 'gz', down)  4.74 us
  transfers between devices with their start and end apart: 6, of which 6 were waited for; matrix products, arithmetic and copies ran while one was open for 0% of the time, Pallas kernels for 2%

profile of v7, /device:TPU:66, one launch (start us, length us, event | category | flops | bytes accessed | tf_op | source)
XLA Modules:
  0.0 144.6 jit_solution(13536482134993168148)
XLA Ops:
  0.0 2.0 %prepare.1 = (f32[1280,128]{1,0:T(8,128)S(1)}, f32[4,64,128]{2,1,0:T(8,128)S(1)}) custom-call(f32[3]{0:T(128)} %sat_hbm.1, f32[3,64,128]{2,1,0:T(8,128)} %bitcast.18, s32[64,128]{1,0:T(8,128)} %bitcast.19, f32[6,2,128,128]{3,2,1,0:T(8,128)} %main_hbm.1, f32[6,2,128]{2,1,0:T(2,128)} %nyq_hbm.1, bf16[2,128,256]{2,1,0:T(8,128)(2,1)} %constant.16.clone.tx_hbm, ...), custom_call_target="tpu_custom_call" | custom-call | tf_op jit(solution)/shard_map/prepare/pallas_call | solution.py:161
  2.0 89.7 %all_to_all.10 = f32[128,5,2,128]{3,2,1,0:T(2,128)S(1)} all-to-all(f32[128,5,2,128]{3,2,1,0:T(2,128)S(1)} %bitcast.14), channel_id=1, replica_groups=mesh['parts'=2,'gz'=128,'gy'=2] {'gz'}, dimensions={0} | all-to-all | bytes 1310720 | tf_op jit(solution)/shard_map/all_to_all | solution.py:402
  91.8 0.0 copy-start.3
  91.9 0.0 copy-start.2
  91.9 4.8 %collective-permute-start.1 = (f32[6,128,128]{2,1,0:T(8,128)S(1)}, f32[6,128,128]{2,1,0:T(8,128)S(1)}, u32[]{:S(2)}, u32[]{:S(2)}) collective-permute-start(f32[6,128,128]{2,1,0:T(8,128)S(1)} %slice.18.kernel), channel_id=1, source_target_pairs={{0,256},{256,0},{1,257},{257,1},{2,258},{258,2},{3,259},{259,3},{4... | collective-permute-start | bytes 1179656 | tf_op jit(solution)/shard_map/ppermute | solution.py:406
  96.7 2.0 %collective-permute-start = (f32[4,128,128]{2,1,0:T(8,128)S(1)}, f32[4,128,128]{2,1,0:T(8,128)S(1)}, u32[]{:S(2)}, u32[]{:S(2)}) collective-permute-start(f32[4,128,128]{2,1,0:T(8,128)S(1)} %slice.17.own), channel_id=1, source_target_pairs={{0,1},{1,0},{2,3},{3,2},{4,5},{5,4},{6,7},{7,6},{8,9},{9,8},{10,11... | collective-permute-start | bytes 786440 | tf_op jit(solution)/shard_map/ppermute | solution.py:410
  98.7 0.0 copy-start.1
  98.7 1.5 %collective-permute-done.other = f32[4,128,128]{2,1,0:T(8,128)S(1)} collective-permute-done((f32[4,128,128]{2,1,0:T(8,128)S(1)}, f32[4,128,128]{2,1,0:T(8,128)S(1)}, u32[]{:S(2)}, u32[]{:S(2)}) %collective-permute-start) | collective-permute-done | bytes 262176 | tf_op jit(solution)/shard_map/ppermute | solution.py:410
  100.2 0.0 copy-done.3
  100.2 0.0 copy-done.2
  100.2 1.1 forward.1.spectra
  101.3 0.0 copy-done.1
  101.3 0.0 copy-start
  101.3 0.7 first_half.1
  102.0 0.6 collective-permute-done.1.kernel
  102.6 0.0 copy-done
  102.6 0.8 second_half.1
  103.5 2.0 %collective-permute-start.2 = (f32[520,128]{1,0:T(8,128)S(1)}, f32[520,128]{1,0:T(8,128)S(1)}, u32[]{:S(2)}, u32[]{:S(2)}) collective-permute-start(f32[520,128]{1,0:T(8,128)S(1)} %get-tuple-element.17), channel_id=1, source_target_pairs={{0,1},{1,0},{2,3},{3,2},{4,5},{5,4},{6,7},{7,6},{8,9},{9,8},{10,11... | collective-permute-start | bytes 798728 | tf_op jit(solution)/shard_map/ppermute | solution.py:416
  105.4 0.3 own_half.1
  105.8 1.2 collective-permute-done.2.arrived
  106.9 0.7 slice_add_fusion
  107.7 12.8 %all-to-all-start.1 = ((f32[128,4,128]{2,1,0:T(4,128)}), f32[128,4,128]{2,1,0:T(4,128)S(1)}, u32[]{:S(2)}, u32[]{:S(2)}) async-start(f32[128,4,128]{2,1,0:T(4,128)} %bitcast.7), calls=%async_computation.1 | async-start | bytes 524288 | tf_op jit(solution)/shard_map/all_to_all | solution.py:419
  120.4 0.0 copy-start.4
  120.5 0.0 copy-start.5
  120.5 4.7 %collective-permute-start.4 = (f32[4,64,128]{2,1,0:T(8,128)S(1)}, f32[4,64,128]{2,1,0:T(8,128)S(1)}, u32[]{:S(2)}, u32[]{:S(2)}) collective-permute-start(f32[4,64,128]{2,1,0:T(8,128)S(1)} %get-tuple-element.18.stack), channel_id=1, source_target_pairs={{2,0},{4,2},{6,4},{8,6},{10,8},{12,10},{14,12},{16,14},{18,16},{20... | collective-permute-start | bytes 393224 | tf_op jit(solution)/shard_map/ppermute | solution.py:425
  125.2 2.0 %collective-permute-start.3 = (f32[4,64,128]{2,1,0:T(8,128)S(1)}, f32[4,64,128]{2,1,0:T(8,128)S(1)}, u32[]{:S(2)}, u32[]{:S(2)}) collective-permute-start(f32[4,64,128]{2,1,0:T(8,128)S(1)} %get-tuple-element.18.stack), channel_id=1, source_target_pairs={{0,2},{2,4},{4,6},{6,8},{8,10},{10,12},{12,14},{14,16},{16,18},{18... | collective-permute-start | bytes 393224 | tf_op jit(solution)/shard_map/ppermute | solution.py:424
  127.2 6.7 %collective-permute-done.4.after = f32[4,64,128]{2,1,0:T(8,128)S(1)} collective-permute-done((f32[4,64,128]{2,1,0:T(8,128)S(1)}, f32[4,64,128]{2,1,0:T(8,128)S(1)}, u32[]{:S(2)}, u32[]{:S(2)}) %collective-permute-start.4) | collective-permute-done | bytes 131104 | tf_op jit(solution)/shard_map/ppermute | solution.py:425
  133.9 1.8 %collective-permute-done.3.before = f32[4,64,128]{2,1,0:T(8,128)S(1)} collective-permute-done((f32[4,64,128]{2,1,0:T(8,128)S(1)}, f32[4,64,128]{2,1,0:T(8,128)S(1)}, u32[]{:S(2)}, u32[]{:S(2)}) %collective-permute-start.3) | collective-permute-done | bytes 131104 | tf_op jit(solution)/shard_map/ppermute | solution.py:424
  135.7 0.1 exchange.1.added
  135.8 7.7 %all-to-all-done.1 = f32[128,4,128]{2,1,0:T(4,128)S(1)} async-done(((f32[128,4,128]{2,1,0:T(4,128)}), f32[128,4,128]{2,1,0:T(4,128)S(1)}, u32[]{:S(2)}, u32[]{:S(2)}) %all-to-all-start.1) | async-done | bytes 262176 | tf_op jit(solution)/shard_map/all_to_all | solution.py:419
  143.5 0.0 copy-done.4
  143.5 0.0 copy-done.5
  143.5 1.0 finish.1
  (4 shorter events, 0.1 us)
Async XLA Ops:
  91.8 8.4 %copy-start.3 = (bf16[2,256,256]{2,1,0:T(8,128)(2,1)S(1)}, bf16[2,256,256]{2,1,0:T(8,128)(2,1)}, u32[]{:S(2)}) copy-start(bf16[2,256,256]{2,1,0:T(8,128)(2,1)} %constant.20.clone.tz) | copy-start | bytes 786436
  91.9 8.3 %copy-start.2 = (bf16[2,2,256,256]{3,2,1,0:T(8,128)(2,1)S(1)}, bf16[2,2,256,256]{3,2,1,0:T(8,128)(2,1)}, u32[]{:S(2)}) copy-start(bf16[2,2,256,256]{3,2,1,0:T(8,128)(2,1)} %constant.19.clone.ty) | copy-start | bytes 1572868
  91.9 10.7 %collective-permute-start.1 = (f32[6,128,128]{2,1,0:T(8,128)S(1)}, f32[6,128,128]{2,1,0:T(8,128)S(1)}, u32[]{:S(2)}, u32[]{:S(2)}) collective-permute-start(f32[6,128,128]{2,1,0:T(8,128)S(1)} %slice.18.kernel), channel_id=1, source_target_pairs={{0,256},{256,0},{1,257},{257,1},{2,258},{258,2},{3,259},{259,3},{4... | collective-permute-start | bytes 1179656 | tf_op jit(solution)/shard_map/ppermute | solution.py:406
  96.7 3.5 %collective-permute-start = (f32[4,128,128]{2,1,0:T(8,128)S(1)}, f32[4,128,128]{2,1,0:T(8,128)S(1)}, u32[]{:S(2)}, u32[]{:S(2)}) collective-permute-start(f32[4,128,128]{2,1,0:T(8,128)S(1)} %slice.17.own), channel_id=1, source_target_pairs={{0,1},{1,0},{2,3},{3,2},{4,5},{5,4},{6,7},{7,6},{8,9},{9,8},{10,11... | collective-permute-start | bytes 786440 | tf_op jit(solution)/shard_map/ppermute | solution.py:410
  98.7 2.6 %copy-start.1 = (bf16[2,2,128,256]{3,2,1,0:T(8,128)(2,1)S(1)}, bf16[2,2,128,256]{3,2,1,0:T(8,128)(2,1)}, u32[]{:S(2)}) copy-start(bf16[2,2,128,256]{3,2,1,0:T(8,128)(2,1)} %constant.18.clone.tz) | copy-start | bytes 786436
  101.3 1.3 copy-start
  103.5 3.5 %collective-permute-start.2 = (f32[520,128]{1,0:T(8,128)S(1)}, f32[520,128]{1,0:T(8,128)S(1)}, u32[]{:S(2)}, u32[]{:S(2)}) collective-permute-start(f32[520,128]{1,0:T(8,128)S(1)} %get-tuple-element.17), channel_id=1, source_target_pairs={{0,1},{1,0},{2,3},{3,2},{4,5},{5,4},{6,7},{7,6},{8,9},{9,8},{10,11... | collective-permute-start | bytes 798728 | tf_op jit(solution)/shard_map/ppermute | solution.py:416
  107.7 35.9 %all-to-all-start.1 = ((f32[128,4,128]{2,1,0:T(4,128)}), f32[128,4,128]{2,1,0:T(4,128)S(1)}, u32[]{:S(2)}, u32[]{:S(2)}) async-start(f32[128,4,128]{2,1,0:T(4,128)} %bitcast.7), calls=%async_computation.1 | async-start | bytes 524288 | tf_op jit(solution)/shard_map/all_to_all | solution.py:419
  120.4 23.1 %copy-start.4 = (bf16[2,2,256,128]{3,2,1,0:T(8,128)(2,1)S(1)}, bf16[2,2,256,128]{3,2,1,0:T(8,128)(2,1)}, u32[]{:S(2)}) copy-start(bf16[2,2,256,128]{3,2,1,0:T(8,128)(2,1)} %constant.23.clone.ny) | copy-start | bytes 786436
  120.5 23.1 %copy-start.5 = (bf16[2,128,256]{2,1,0:T(8,128)(2,1)S(1)}, bf16[2,128,256]{2,1,0:T(8,128)(2,1)}, u32[]{:S(2)}) copy-start(bf16[2,128,256]{2,1,0:T(8,128)(2,1)} %constant.22.clone.tx) | copy-start | bytes 393220
  120.5 13.4 %collective-permute-start.4 = (f32[4,64,128]{2,1,0:T(8,128)S(1)}, f32[4,64,128]{2,1,0:T(8,128)S(1)}, u32[]{:S(2)}, u32[]{:S(2)}) collective-permute-start(f32[4,64,128]{2,1,0:T(8,128)S(1)} %get-tuple-element.18.stack), channel_id=1, source_target_pairs={{2,0},{4,2},{6,4},{8,6},{10,8},{12,10},{14,12},{16,14},{18,16},{20... | collective-permute-start | bytes 393224 | tf_op jit(solution)/shard_map/ppermute | solution.py:425
  125.2 10.5 %collective-permute-start.3 = (f32[4,64,128]{2,1,0:T(8,128)S(1)}, f32[4,64,128]{2,1,0:T(8,128)S(1)}, u32[]{:S(2)}, u32[]{:S(2)}) collective-permute-start(f32[4,64,128]{2,1,0:T(8,128)S(1)} %get-tuple-element.18.stack), channel_id=1, source_target_pairs={{0,2},{2,4},{4,6},{6,8},{8,10},{10,12},{12,14},{14,16},{16,18},{18... | collective-permute-start | bytes 393224 | tf_op jit(solution)/shard_map/ppermute | solution.py:424

commit v8 on v5

--- a/solution.py
+++ b/solution.py
@@ -106,8 +106,8 @@
         pltpu.make_async_copy(nyq_hbm, nyq, sems.at[5]),
         pltpu.make_async_copy(sat_hbm, sat_ref, sems.at[6]),
     ]
-    for c in copies:
-        c.start()
+    for k in (6, 0, 1, 3, 2, 4, 5):
+        copies[k].start()
     rows_t[...] = jnp.zeros_like(rows_t)
     copies[0].wait()
     region = reg[...]
@@ -360,10 +360,6 @@
         halves(t["tx"]), halves(t["ny"]).swapaxes(0, 1), slots,
     )
     width = 4 + 6 * slots
-    up = [(i, i + 1) for i in range(groups_z - 1)]
-    down = [(b, a) for a, b in up]
-    before = lax.ppermute(stacked, "gz", up)
-    after = lax.ppermute(stacked, "gz", down)
     recv = lax.all_to_all(send.reshape(columns, width // 2, 2, columns), "gz", 0, 0, tiled=True)
     recv = recv.reshape(columns, width, columns).transpose(1, 0, 2)
     kernel = recv[4:10]
@@ -377,11 +373,15 @@
     spectra = forward(own_m, other_m, halves(t["ty"]), halves(t["tz"]))
     ready, line = first_half(pairs, spectra, kernel, own_m[3], tz_back)
     own, other = second_half(pairs, spectra, kernel_other, ready, line, stacked, tz_back, halves(t["ty_back"]))
-    other, before, after = lax.optimization_barrier((other, before, after))
     arrived = lax.ppermute(other, "gy", swap)
     send_f = own + arrived[: 4 * groups_z]
     recv_f = lax.all_to_all(send_f.reshape(groups_z, 4, columns), "gz", 0, 0, tiled=True)
     recv_f = recv_f.reshape(4 * columns, columns)
+    up = [(i, i + 1) for i in range(groups_z - 1)]
+    down = [(b, a) for a, b in up]
+    edge_planes, _ = lax.optimization_barrier((stacked, send_f))
+    before = lax.ppermute(edge_planes, "gz", up)
+    after = lax.ppermute(edge_planes, "gz", down)
     tx_back, ny_back = halves(t["tx_back"]), halves(t["ny_back"])
     return finish(recv_f, arrived, stacked, before, after, tx_back, ny_back)[:, None]
 

time: 151 us -> 145 us (0.960)
  blocking collectives: 125 us -> 89.7 us
  waiting for transfers between devices: 2.75 us -> 20.1 us
  starting transfers between devices: 16.7 us -> 28.2 us
    all_to_all x1 -> x0, blocking collectives: 35.1 us -> none  [local(): lax.all_to_all(send_f.reshape(groups_z, 4, columns), 'gz', 0, 0, tiled=True)]
    all_to_all x0 -> x1, starting transfers between devices: none -> 12.9 us  [local(): lax.all_to_all(send_f.reshape(groups_z, 4, columns), 'gz', 0, 0, tiled=True)]
    all_to_all x0 -> x1, waiting for transfers between devices: none -> 7.92 us  [local(): lax.all_to_all(send_f.reshape(groups_z, 4, columns), 'gz', 0, 0, tiled=True)]
    ppermute x2, waiting for transfers between devices: 1.24 us -> 8.6 us  [the longest x1 6.89 us: local(): after = lax.ppermute(edge_planes, 'gz', down)]
  transfers between devices with their start and end apart: 5 -> 6, of which waited for: 2 -> 6; matrix products, arithmetic and copies ran while one was open for 0% -> 0% of each run, Pallas kernels for 2% -> 1%
where the time goes in v8:
time: 145 us; the launch traced here: 144 us
  blocking collectives  89.7 us (62%)
  starting transfers between devices  28.2 us (19%)
  waiting for transfers between devices  20.1 us (14%)
  Pallas kernels  5.42 us (4%)
    all_to_all x1, blocking collectives, local(): lax.all_to_all(send.reshape(columns, width // 2, 2, columns), 'gz', 0, 0,...  89.7 us
    all_to_all x1, starting transfers between devices, local(): lax.all_to_all(send_f.reshape(groups_z, 4, columns), 'gz', 0, 0, tiled=True)  12.9 us
    all_to_all x1, waiting for transfers between devices, local(): lax.all_to_all(send_f.reshape(groups_z, 4, columns), 'gz', 0, 0, tiled=True)  7.92 us
    ppermute x1, waiting for transfers between devices, local(): after = lax.ppermute(edge_planes, 'gz', down)  6.89 us
    ppermute x1, starting transfers between devices, local(): lax.ppermute(kernel, 'parts', [(p, p ^ 1) for p in range(parts)])  4.84 us
    ppermute x1, starting transfers between devices, local(): after = lax.ppermute(edge_planes, 'gz', down)  4.61 us
  transfers between devices with their start and end apart: 6, of which 6 were waited for; matrix products, arithmetic and copies ran while one was open for 0% of the time, Pallas kernels for 1%

profile of v8, /device:TPU:66, one launch (start us, length us, event | category | flops | bytes accessed | tf_op | source)
XLA Modules:
  0.0 144.5 jit_solution(16583332599612159048)
XLA Ops:
  0.0 2.0 %prepare.1 = (f32[1280,128]{1,0:T(8,128)S(1)}, f32[4,64,128]{2,1,0:T(8,128)S(1)}) custom-call(f32[3]{0:T(128)} %sat_hbm.1, f32[3,64,128]{2,1,0:T(8,128)} %bitcast.18, s32[64,128]{1,0:T(8,128)} %bitcast.19, f32[6,2,128,128]{3,2,1,0:T(8,128)} %main_hbm.1, f32[6,2,128]{2,1,0:T(2,128)} %nyq_hbm.1, bf16[2,128,256]{2,1,0:T(8,128)(2,1)} %constant.16.clone.tx_hbm, ...), custom_call_target="tpu_custom_call" | custom-call | tf_op jit(solution)/shard_map/prepare/pallas_call | solution.py:161
  2.0 89.7 %all_to_all.10 = f32[128,5,2,128]{3,2,1,0:T(2,128)S(1)} all-to-all(f32[128,5,2,128]{3,2,1,0:T(2,128)S(1)} %bitcast.14), channel_id=1, replica_groups=mesh['parts'=2,'gz'=128,'gy'=2] {'gz'}, dimensions={0} | all-to-all | bytes 1310720 | tf_op jit(solution)/shard_map/all_to_all | solution.py:363
  91.7 0.0 copy-start.3
  91.8 0.0 copy-start.2
  91.8 4.8 %collective-permute-start.1 = (f32[6,128,128]{2,1,0:T(8,128)S(1)}, f32[6,128,128]{2,1,0:T(8,128)S(1)}, u32[]{:S(2)}, u32[]{:S(2)}) collective-permute-start(f32[6,128,128]{2,1,0:T(8,128)S(1)} %slice.18.kernel), channel_id=1, source_target_pairs={{0,256},{256,0},{1,257},{257,1},{2,258},{258,2},{3,259},{259,3},{4... | collective-permute-start | bytes 1179656 | tf_op jit(solution)/shard_map/ppermute | solution.py:367
  96.7 2.0 %collective-permute-start = (f32[4,128,128]{2,1,0:T(8,128)S(1)}, f32[4,128,128]{2,1,0:T(8,128)S(1)}, u32[]{:S(2)}, u32[]{:S(2)}) collective-permute-start(f32[4,128,128]{2,1,0:T(8,128)S(1)} %slice.17.own), channel_id=1, source_target_pairs={{0,1},{1,0},{2,3},{3,2},{4,5},{5,4},{6,7},{7,6},{8,9},{9,8},{10,11... | collective-permute-start | bytes 786440 | tf_op jit(solution)/shard_map/ppermute | solution.py:371
  98.7 0.0 copy-start
  98.7 1.5 %collective-permute-done.other = f32[4,128,128]{2,1,0:T(8,128)S(1)} collective-permute-done((f32[4,128,128]{2,1,0:T(8,128)S(1)}, f32[4,128,128]{2,1,0:T(8,128)S(1)}, u32[]{:S(2)}, u32[]{:S(2)}) %collective-permute-start) | collective-permute-done | bytes 262176 | tf_op jit(solution)/shard_map/ppermute | solution.py:371
  100.1 0.0 copy-done.3
  100.1 0.0 copy-done.2
  100.1 1.1 forward.1.spectra
  101.2 0.0 copy-done
  101.2 0.0 copy-start.1
  101.3 0.7 first_half.1
  101.9 0.6 collective-permute-done.1.kernel
  102.5 0.0 copy-done.1
  102.5 0.7 second_half.1
  103.2 2.0 %collective-permute-start.2 = (f32[520,128]{1,0:T(8,128)S(1)}, f32[520,128]{1,0:T(8,128)S(1)}, u32[]{:S(2)}, u32[]{:S(2)}) collective-permute-start(f32[520,128]{1,0:T(8,128)S(1)} %get-tuple-element.17), channel_id=1, source_target_pairs={{0,1},{1,0},{2,3},{3,2},{4,5},{5,4},{6,7},{7,6},{8,9},{9,8},{10,11... | collective-permute-start | bytes 798728 | tf_op jit(solution)/shard_map/ppermute | solution.py:376
  105.2 1.5 %collective-permute-done.2.arrived = f32[520,128]{1,0:T(8,128)S(1)} collective-permute-done((f32[520,128]{1,0:T(8,128)S(1)}, f32[520,128]{1,0:T(8,128)S(1)}, u32[]{:S(2)}, u32[]{:S(2)}) %collective-permute-start.2) | collective-permute-done | bytes 266272 | tf_op jit(solution)/shard_map/ppermute | solution.py:376
  106.7 0.7 slice_add_fusion
  107.4 0.0 copy-start.4
  107.4 0.0 copy-start.5
  107.4 12.9 %all-to-all-start.1 = ((f32[128,4,128]{2,1,0:T(4,128)}), f32[128,4,128]{2,1,0:T(4,128)S(1)}, u32[]{:S(2)}, u32[]{:S(2)}) async-start(f32[128,4,128]{2,1,0:T(4,128)} %bitcast.7), calls=%async_computation.1 | async-start | bytes 524288 | tf_op jit(solution)/shard_map/all_to_all | solution.py:378
  120.3 4.6 %collective-permute-start.4 = (f32[4,64,128]{2,1,0:T(8,128)S(1)}, f32[4,64,128]{2,1,0:T(8,128)S(1)}, u32[]{:S(2)}, u32[]{:S(2)}) collective-permute-start(f32[4,64,128]{2,1,0:T(8,128)S(1)} %get-tuple-element.18.stack), channel_id=1, source_target_pairs={{2,0},{4,2},{6,4},{8,6},{10,8},{12,10},{14,12},{16,14},{18,16},{20... | collective-permute-start | bytes 393224 | tf_op jit(solution)/shard_map/ppermute | solution.py:384
  124.9 2.0 %collective-permute-start.3 = (f32[4,64,128]{2,1,0:T(8,128)S(1)}, f32[4,64,128]{2,1,0:T(8,128)S(1)}, u32[]{:S(2)}, u32[]{:S(2)}) collective-permute-start(f32[4,64,128]{2,1,0:T(8,128)S(1)} %get-tuple-element.18.stack), channel_id=1, source_target_pairs={{0,2},{2,4},{4,6},{6,8},{8,10},{10,12},{12,14},{14,16},{16,18},{18... | collective-permute-start | bytes 393224 | tf_op jit(solution)/shard_map/ppermute | solution.py:383
  126.9 6.9 %collective-permute-done.4.after = f32[4,64,128]{2,1,0:T(8,128)S(1)} collective-permute-done((f32[4,64,128]{2,1,0:T(8,128)S(1)}, f32[4,64,128]{2,1,0:T(8,128)S(1)}, u32[]{:S(2)}, u32[]{:S(2)}) %collective-permute-start.4) | collective-permute-done | bytes 131104 | tf_op jit(solution)/shard_map/ppermute | solution.py:384
  133.8 1.7 %collective-permute-done.3.before = f32[4,64,128]{2,1,0:T(8,128)S(1)} collective-permute-done((f32[4,64,128]{2,1,0:T(8,128)S(1)}, f32[4,64,128]{2,1,0:T(8,128)S(1)}, u32[]{:S(2)}, u32[]{:S(2)}) %collective-permute-start.3) | collective-permute-done | bytes 131104 | tf_op jit(solution)/shard_map/ppermute | solution.py:383
  135.5 7.9 %all-to-all-done.1 = f32[128,4,128]{2,1,0:T(4,128)S(1)} async-done(((f32[128,4,128]{2,1,0:T(4,128)}), f32[128,4,128]{2,1,0:T(4,128)S(1)}, u32[]{:S(2)}, u32[]{:S(2)}) %all-to-all-start.1) | async-done | bytes 262176 | tf_op jit(solution)/shard_map/all_to_all | solution.py:378
  143.4 0.0 copy-done.4
  143.4 0.0 copy-done.5
  143.4 1.1 finish.1
  (4 shorter events, 0.1 us)
Async XLA Ops:
  91.7 8.4 %copy-start.3 = (bf16[2,256,256]{2,1,0:T(8,128)(2,1)S(1)}, bf16[2,256,256]{2,1,0:T(8,128)(2,1)}, u32[]{:S(2)}) copy-start(bf16[2,256,256]{2,1,0:T(8,128)(2,1)} %constant.20.clone.tz) | copy-start | bytes 786436
  91.8 8.4 %copy-start.2 = (bf16[2,2,256,256]{3,2,1,0:T(8,128)(2,1)S(1)}, bf16[2,2,256,256]{3,2,1,0:T(8,128)(2,1)}, u32[]{:S(2)}) copy-start(bf16[2,2,256,256]{3,2,1,0:T(8,128)(2,1)} %constant.19.clone.ty) | copy-start | bytes 1572868
  91.8 10.7 %collective-permute-start.1 = (f32[6,128,128]{2,1,0:T(8,128)S(1)}, f32[6,128,128]{2,1,0:T(8,128)S(1)}, u32[]{:S(2)}, u32[]{:S(2)}) collective-permute-start(f32[6,128,128]{2,1,0:T(8,128)S(1)} %slice.18.kernel), channel_id=1, source_target_pairs={{0,256},{256,0},{1,257},{257,1},{2,258},{258,2},{3,259},{259,3},{4... | collective-permute-start | bytes 1179656 | tf_op jit(solution)/shard_map/ppermute | solution.py:367
  96.7 3.5 %collective-permute-start = (f32[4,128,128]{2,1,0:T(8,128)S(1)}, f32[4,128,128]{2,1,0:T(8,128)S(1)}, u32[]{:S(2)}, u32[]{:S(2)}) collective-permute-start(f32[4,128,128]{2,1,0:T(8,128)S(1)} %slice.17.own), channel_id=1, source_target_pairs={{0,1},{1,0},{2,3},{3,2},{4,5},{5,4},{6,7},{7,6},{8,9},{9,8},{10,11... | collective-permute-start | bytes 786440 | tf_op jit(solution)/shard_map/ppermute | solution.py:371
  98.7 2.6 %copy-start = (bf16[2,2,128,256]{3,2,1,0:T(8,128)(2,1)S(1)}, bf16[2,2,128,256]{3,2,1,0:T(8,128)(2,1)}, u32[]{:S(2)}) copy-start(bf16[2,2,128,256]{3,2,1,0:T(8,128)(2,1)} %constant.18.clone.tz) | copy-start | bytes 786436
  101.2 1.3 copy-start.1
  103.2 3.5 %collective-permute-start.2 = (f32[520,128]{1,0:T(8,128)S(1)}, f32[520,128]{1,0:T(8,128)S(1)}, u32[]{:S(2)}, u32[]{:S(2)}) collective-permute-start(f32[520,128]{1,0:T(8,128)S(1)} %get-tuple-element.17), channel_id=1, source_target_pairs={{0,1},{1,0},{2,3},{3,2},{4,5},{5,4},{6,7},{7,6},{8,9},{9,8},{10,11... | collective-permute-start | bytes 798728 | tf_op jit(solution)/shard_map/ppermute | solution.py:376
  107.4 36.0 %copy-start.4 = (bf16[2,2,256,128]{3,2,1,0:T(8,128)(2,1)S(1)}, bf16[2,2,256,128]{3,2,1,0:T(8,128)(2,1)}, u32[]{:S(2)}) copy-start(bf16[2,2,256,128]{3,2,1,0:T(8,128)(2,1)} %constant.23.clone.ny) | copy-start | bytes 786436
  107.4 36.0 %copy-start.5 = (bf16[2,128,256]{2,1,0:T(8,128)(2,1)S(1)}, bf16[2,128,256]{2,1,0:T(8,128)(2,1)}, u32[]{:S(2)}) copy-start(bf16[2,128,256]{2,1,0:T(8,128)(2,1)} %constant.22.clone.tx) | copy-start | bytes 393220
  107.4 36.0 %all-to-all-start.1 = ((f32[128,4,128]{2,1,0:T(4,128)}), f32[128,4,128]{2,1,0:T(4,128)S(1)}, u32[]{:S(2)}, u32[]{:S(2)}) async-start(f32[128,4,128]{2,1,0:T(4,128)} %bitcast.7), calls=%async_computation.1 | async-start | bytes 524288 | tf_op jit(solution)/shard_map/all_to_all | solution.py:378
  120.3 13.5 %collective-permute-start.4 = (f32[4,64,128]{2,1,0:T(8,128)S(1)}, f32[4,64,128]{2,1,0:T(8,128)S(1)}, u32[]{:S(2)}, u32[]{:S(2)}) collective-permute-start(f32[4,64,128]{2,1,0:T(8,128)S(1)} %get-tuple-element.18.stack), channel_id=1, source_target_pairs={{2,0},{4,2},{6,4},{8,6},{10,8},{12,10},{14,12},{16,14},{18,16},{20... | collective-permute-start | bytes 393224 | tf_op jit(solution)/shard_map/ppermute | solution.py:384
  124.9 10.6 %collective-permute-start.3 = (f32[4,64,128]{2,1,0:T(8,128)S(1)}, f32[4,64,128]{2,1,0:T(8,128)S(1)}, u32[]{:S(2)}, u32[]{:S(2)}) collective-permute-start(f32[4,64,128]{2,1,0:T(8,128)S(1)} %get-tuple-element.18.stack), channel_id=1, source_target_pairs={{0,2},{2,4},{4,6},{6,8},{8,10},{10,12},{12,14},{14,16},{16,18},{18... | collective-permute-start | bytes 393224 | tf_op jit(solution)/shard_map/ppermute | solution.py:383
